TPU v7x, 8 devices: a whole 2x2x1 slice. The times are simulated.
8 devices in a mesh: dp: 1 (over z), tp: 2 (over y), cp: 4 (over x, core).
Axes of the slice: x: 2, y: 2, z: 1, core: 2. Of those that a mesh axis runs over, the one named last changes fastest.
Arguments:
- x: bfloat16 [2048, 8192], P(('dp', 'cp'))
- doc_id: int32 [2048], P(('dp', 'cp'))
- pos_in_doc: int32 [2048], P(('dp', 'cp'))
- norm_gain: float32 [8192], replicated
- w_q: bfloat16 [8192, 8192], P(None, 'tp')
- w_k: bfloat16 [8192, 1024], P(None, 'tp')
- w_v: bfloat16 [8192, 1024], P(None, 'tp')
- w_o: bfloat16 [8192, 8192], P('tp')
- inv_freq: float32 [64], replicated
Outputs:
- output 1: bfloat16 [2048, 8192], P(('dp', 'cp'))
- output 2: bfloat16 [2048, 8, 128], P(('dp', 'cp'), 'tp')
- output 3: bfloat16 [2048, 8, 128], P(('dp', 'cp'), 'tp')
All inputs are finite; a program needn't handle non-finite values.
Results may differ from a plain program's by a relative error of at most 0.00419103.
Values are sent between devices in bfloat16 or wider.
A program may use at most 1 GiB of HBM per device.

v0:
```python
import jax
import jax.numpy as jnp
from jax import lax
from jax.sharding import PartitionSpec as P

QUERY_ROWS = 128


def rms_norm(x_in, norm_gain):
    x_f32 = x_in.astype(jnp.float32)
    inv_rms = lax.rsqrt(jnp.mean(x_f32 * x_f32, axis=-1, keepdims=True) + 1e-5)
    return (x_f32 * inv_rms * norm_gain).astype(jnp.bfloat16)


def apply_rope(vectors, cos_t, sin_t):
    half_dim = vectors.shape[-1] // 2
    lower_half = vectors[..., :half_dim].astype(jnp.float32)
    upper_half = vectors[..., half_dim:].astype(jnp.float32)
    turned = jnp.concatenate([lower_half * cos_t - upper_half * sin_t, upper_half * cos_t + lower_half * sin_t], axis=-1)
    return turned.astype(jnp.bfloat16)


def project(x_in, pos_in_doc, norm_gain, w_q, w_k, w_v, inv_freq):
    num_rows = x_in.shape[0]
    head_dim = 2 * inv_freq.shape[0]
    kv_heads = w_k.shape[1] // head_dim
    group_size = w_q.shape[1] // (head_dim * kv_heads)
    normed = rms_norm(x_in, norm_gain)
    q_new = jnp.dot(normed, w_q, preferred_element_type=jnp.float32).astype(jnp.bfloat16).reshape(num_rows, kv_heads, group_size, head_dim)
    k_new = jnp.dot(normed, w_k, preferred_element_type=jnp.float32).astype(jnp.bfloat16).reshape(num_rows, kv_heads, head_dim)
    v_new = jnp.dot(normed, w_v, preferred_element_type=jnp.float32).astype(jnp.bfloat16).reshape(num_rows, kv_heads, head_dim)
    rope_angle = pos_in_doc.astype(jnp.float32)[:, None] * inv_freq[None, :]
    cos_t = jnp.cos(rope_angle)
    sin_t = jnp.sin(rope_angle)
    q_rot = apply_rope(q_new, cos_t[:, None, None, :], sin_t[:, None, None, :])
    k_rot = apply_rope(k_new, cos_t[:, None, :], sin_t[:, None, :])
    return q_rot, k_rot, v_new


def global_index(stored_pos, local_rows, cp_size):
    piece_len = local_rows // 2
    owner = stored_pos // local_rows
    within = stored_pos % local_rows
    piece_id = jnp.where(within < piece_len, owner, 2 * cp_size - 1 - owner)
    return piece_id * piece_len + within % piece_len


def attention(q_rot, key_rows, val_rows, q_doc, q_idx, key_doc, key_idx):
    local_rows, kv_heads, group_size, head_dim = q_rot.shape
    blocks = local_rows // QUERY_ROWS
    score_scale = head_dim ** -0.5

    def attend(block_args):
        q_blk, doc_blk, idx_blk = block_args
        scores = jnp.einsum('qngd,knd->ngqk', q_blk, key_rows, preferred_element_type=jnp.float32) * score_scale
        visible = (doc_blk[:, None] == key_doc[None, :]) & (key_idx[None, :] <= idx_blk[:, None])
        scores = jnp.where(visible, scores, -1e30)
        attn_probs = jax.nn.softmax(scores, axis=-1).astype(jnp.bfloat16)
        return jnp.einsum('ngqk,knd->qngd', attn_probs, val_rows, preferred_element_type=jnp.float32).astype(jnp.bfloat16)

    attn_out = lax.map(attend, (q_rot.reshape(blocks, QUERY_ROWS, kv_heads, group_size, head_dim), q_doc.reshape(blocks, QUERY_ROWS), q_idx.reshape(blocks, QUERY_ROWS)))
    return attn_out.reshape(local_rows, kv_heads * group_size * head_dim)


def solution(mesh):
    cp_size = mesh.shape['cp']

    def local_step(x_in, doc_id, pos_in_doc, norm_gain, w_q, w_k, w_v, w_o, inv_freq):
        local_rows = x_in.shape[0]
        tokens = local_rows * cp_size
        q_rot, k_rot, v_new = project(x_in, pos_in_doc, norm_gain, w_q, w_k, w_v, inv_freq)
        k_all = lax.all_gather(k_rot, 'cp', tiled=True)
        v_all = lax.all_gather(v_new, 'cp', tiled=True)
        doc_all = lax.all_gather(doc_id, 'cp', tiled=True)
        cp_index = lax.axis_index('cp')
        q_idx = global_index(cp_index * local_rows + jnp.arange(local_rows), local_rows, cp_size)
        key_idx = global_index(jnp.arange(tokens), local_rows, cp_size)
        attn_out = attention(q_rot, k_all, v_all, doc_id, q_idx, doc_all, key_idx)
        part_sum = jnp.dot(attn_out, w_o, preferred_element_type=jnp.float32)
        full_sum = lax.psum(part_sum, 'tp')
        y_out = (x_in.astype(jnp.float32) + full_sum).astype(jnp.bfloat16)
        return y_out, k_rot, v_new

    row_spec = P(('dp', 'cp'))
    in_specs = (P(('dp', 'cp'), None), row_spec, row_spec, P(), P(None, 'tp'), P(None, 'tp'), P(None, 'tp'), P('tp', None), P())
    out_specs = (P(('dp', 'cp'), None), P(('dp', 'cp'), 'tp', None), P(('dp', 'cp'), 'tp', None))
    return jax.shard_map(local_step, mesh=mesh, in_specs=in_specs, out_specs=out_specs, check_vma=False)
```

profile of v0, /device:TPU:0, one launch (start us, length us, event | category | flops | bytes accessed | tf_op | source)
XLA Modules:
  0.0 703.5 jit_solution(1880073812413967846)
XLA Ops:
  7.2 5.1 fusion.54
  12.9 10.4 %convolution_convert_fusion.2 = bf16[512,512]{0,1:T(8,128)(2,1)S(1)} fusion(bf16[8192,512]{1,0:T(8,128)(2,1)} %param.16, bf16[512,8192]{1,0:T(8,128)(2,1)} %param.11, f32[8192]{0:T(1024)S(1)} %copy-done.5, f32[512]{0:T(512)S(1)} %add_rsqrt_fusion), kind=kOutput, calls=%fused_computation.70 | convolution fusion | flops 4312006656 | bytes 17336320 | tf_op jit(solution)/shard_map/dot_general | solution.py:30
  25.0 10.4 %convolution_convert_fusion.1 = bf16[512,512]{0,1:T(8,128)(2,1)S(1)} fusion(bf16[8192,512]{1,0:T(8,128)(2,1)} %param.17, bf16[512,8192]{1,0:T(8,128)(2,1)} %param.11, f32[8192]{0:T(1024)S(1)} %copy-done.5, f32[512]{0:T(512)S(1)} %add_rsqrt_fusion), kind=kOutput, calls=%fused_computation.69 | convolution fusion | flops 4312006656 | bytes 17336320 | tf_op jit(solution)/shard_map/dot_general | solution.py:31
  37.0 44.7 %convolution_convert_fusion = bf16[512,4096]{1,0:T(8,128)(2,1)} fusion(bf16[8192,4096]{1,0:T(8,128)(2,1)} %param.15, bf16[512,8192]{1,0:T(8,128)(2,1)} %param.11, f32[8192]{0:T(1024)S(1)} %copy-done.5, f32[512]{0:T(512)S(1)} %add_rsqrt_fusion), kind=kOutput, calls=%fused_computation.59 | convolution fusion | flops 34378612736 | bytes 79726592 | tf_op jit(solution)/shard_map/dot_general | solution.py:29
  81.7 6.4 copy.50
  88.2 5.1 fusion.59
  93.2 4.0 concatenate.13
  97.2 2.1 concatenate.14
  99.3 6.9 pad_maximum_fusion
  106.2 7.5 %copy.43 = bf16[4,128,4,8,128]{4,1,3,2,0:T(8,128)(2,1)} copy(bf16[4,128,4,8,128]{1,0,4,3,2:T(4,128)(2,1)} %pad_maximum_fusion) | data formatting | bytes 8388608
  113.6 10.0 %all-gather = s32[4,1,512]{2,1,0:T(1,128)S(1)} all-gather(s32[1,1,512]{2,1,0:T(1,128)S(1)} %bitcast.92), channel_id=1, replica_groups=mesh['dp'=1,'tp'=2,'cp'=4] {'cp'}, dimensions={0}, use_global_device_ids=true | all-gather | bytes 10240 | tf_op jit(solution)/shard_map/all_gather | solution.py:74
  125.5 135.0 %while.11 = (s32[]{:T(128)}, bf16[4,128,4,8,128]{4,3,2,1,0:T(8,128)(2,1)}, s32[4,128]{1,0:T(4,128)S(1)}, s32[2048]{0:T(1024)S(1)}, s32[4,128]{1,0:T(4,128)S(1)},...) while((s32[]{:T(128)}, ...), condition=%wide.region_4.5_spmd.clone, body=%wide.region_1.4_spmd.clone.sunk | while | flops 4346669056 | bytes 76083296 | solution.py:61
  125.9 18.2 %fusion.101 = (f32[4,8,128]{2,1,0:T(8,128)S(1)}, f32[4,8,128,2048]{3,2,1,0:T(8,128)}) fusion(pred[128,2048]{1,0:T(8,128)(4,1)S(1)} %compare_and_fusion.2, bf16[2048,4,128]{2,0,1:T(8,128)(2,1)S(1)} %get-tuple-element.220, bf16[4,128,4,8,128]{4,1,3,2,0:T(8,128)(2,1)} %get-tuple-element.219, s32[]{:T(128)} %get-tuple-element.205), kind=kOutput, calls=%fused_computation.99.clone.1 | convolution fusion | flops 2181040128 | bytes 36979200 | tf_op jit(solution)/shard_map/while/body/eval_jaxpr/sub | solution.py:58
  144.1 13.6 %fusion.102 = bf16[1,128,4,8,128]{4,1,3,2,0:T(8,128)(2,1)S(1)} fusion(bf16[2048,4,128]{2,0,1:T(8,128)(2,1)} %get-tuple-element.221, f32[4,8,128,2048]{3,2,1,0:T(8,128)} %get-tuple-element.194, f32[4,8,128]{2,1,0:T(8,128)S(1)} %get-tuple-element.195), kind=kOutput, calls=%fused_computation.18.clone.1 | convolution fusion | flops 2164785152 | bytes 36716544 | tf_op jit(solution)/shard_map/while/body/eval_jaxpr/ngqk,knd->qngd/dot_general | solution.py:59
  159.6 18.2 %fusion.101 = (f32[4,8,128]{2,1,0:T(8,128)S(1)}, f32[4,8,128,2048]{3,2,1,0:T(8,128)}) fusion(pred[128,2048]{1,0:T(8,128)(4,1)S(1)} %compare_and_fusion.2, bf16[2048,4,128]{2,0,1:T(8,128)(2,1)S(1)} %get-tuple-element.220, bf16[4,128,4,8,128]{4,1,3,2,0:T(8,128)(2,1)} %get-tuple-element.219, s32[]{:T(128)} %get-tuple-element.205), kind=kOutput, calls=%fused_computation.99.clone.1 | convolution fusion | flops 2181040128 | bytes 36979200 | tf_op jit(solution)/shard_map/while/body/eval_jaxpr/sub | solution.py:58
  177.8 13.6 %fusion.102 = bf16[1,128,4,8,128]{4,1,3,2,0:T(8,128)(2,1)S(1)} fusion(bf16[2048,4,128]{2,0,1:T(8,128)(2,1)} %get-tuple-element.221, f32[4,8,128,2048]{3,2,1,0:T(8,128)} %get-tuple-element.194, f32[4,8,128]{2,1,0:T(8,128)S(1)} %get-tuple-element.195), kind=kOutput, calls=%fused_computation.18.clone.1 | convolution fusion | flops 2164785152 | bytes 36716544 | tf_op jit(solution)/shard_map/while/body/eval_jaxpr/ngqk,knd->qngd/dot_general | solution.py:59
  193.4 18.2 %fusion.101 = (f32[4,8,128]{2,1,0:T(8,128)S(1)}, f32[4,8,128,2048]{3,2,1,0:T(8,128)}) fusion(pred[128,2048]{1,0:T(8,128)(4,1)S(1)} %compare_and_fusion.2, bf16[2048,4,128]{2,0,1:T(8,128)(2,1)S(1)} %get-tuple-element.220, bf16[4,128,4,8,128]{4,1,3,2,0:T(8,128)(2,1)} %get-tuple-element.219, s32[]{:T(128)} %get-tuple-element.205), kind=kOutput, calls=%fused_computation.99.clone.1 | convolution fusion | flops 2181040128 | bytes 36979200 | tf_op jit(solution)/shard_map/while/body/eval_jaxpr/sub | solution.py:58
  211.6 13.6 %fusion.102 = bf16[1,128,4,8,128]{4,1,3,2,0:T(8,128)(2,1)S(1)} fusion(bf16[2048,4,128]{2,0,1:T(8,128)(2,1)} %get-tuple-element.221, f32[4,8,128,2048]{3,2,1,0:T(8,128)} %get-tuple-element.194, f32[4,8,128]{2,1,0:T(8,128)S(1)} %get-tuple-element.195), kind=kOutput, calls=%fused_computation.18.clone.1 | convolution fusion | flops 2164785152 | bytes 36716544 | tf_op jit(solution)/shard_map/while/body/eval_jaxpr/ngqk,knd->qngd/dot_general | solution.py:59
  227.1 18.2 %fusion.101 = (f32[4,8,128]{2,1,0:T(8,128)S(1)}, f32[4,8,128,2048]{3,2,1,0:T(8,128)}) fusion(pred[128,2048]{1,0:T(8,128)(4,1)S(1)} %compare_and_fusion.2, bf16[2048,4,128]{2,0,1:T(8,128)(2,1)S(1)} %get-tuple-element.220, bf16[4,128,4,8,128]{4,1,3,2,0:T(8,128)(2,1)} %get-tuple-element.219, s32[]{:T(128)} %get-tuple-element.205), kind=kOutput, calls=%fused_computation.99.clone.1 | convolution fusion | flops 2181040128 | bytes 36979200 | tf_op jit(solution)/shard_map/while/body/eval_jaxpr/sub | solution.py:58
  245.3 13.6 %fusion.102 = bf16[1,128,4,8,128]{4,1,3,2,0:T(8,128)(2,1)S(1)} fusion(bf16[2048,4,128]{2,0,1:T(8,128)(2,1)} %get-tuple-element.221, f32[4,8,128,2048]{3,2,1,0:T(8,128)} %get-tuple-element.194, f32[4,8,128]{2,1,0:T(8,128)S(1)} %get-tuple-element.195), kind=kOutput, calls=%fused_computation.18.clone.1 | convolution fusion | flops 2164785152 | bytes 36716544 | tf_op jit(solution)/shard_map/while/body/eval_jaxpr/ngqk,knd->qngd/dot_general | solution.py:59
  260.5 7.3 %reshape.131 = bf16[512,4096]{1,0:T(8,128)(2,1)} reshape(bf16[4,128,4,8,128]{4,3,2,1,0:T(8,128)(2,1)} %get-tuple-element.50) | data formatting | bytes 8388608 | tf_op jit(solution)/shard_map/reshape | solution.py:62
  267.8 44.4 %fusion.83 = f32[512,8192]{1,0:T(8,128)} fusion(bf16[512,4096]{1,0:T(8,128)(2,1)} %reshape.131, bf16[4096,8192]{1,0:T(8,128)(2,1)} %param.18), kind=kOutput, calls=%fused_computation.100 | convolution fusion | flops 34359738368 | bytes 88080384 | tf_op jit(solution)/shard_map/dot_general | solution.py:79
  314.3 370.3 %all-reduce.2.cloned.1.call-done = f32[512,8192]{1,0:T(8,128)} async-done(((f32[512,8192]{1,0:T(8,128)}), f32[512,8192]{1,0:T(8,128)}) %all-reduce.2.cloned.1.call-update) | async-done | bytes 16777232 | tf_op jit(solution)/shard_map/psum | solution.py:80
  684.6 12.1 %fusion.57 = bf16[512,8192]{1,0:T(8,128)(2,1)} fusion(f32[512,8192]{1,0:T(8,128)} %all-reduce.2.cloned.1.call-done, bf16[512,8192]{1,0:T(8,128)(2,1)} %param.11), kind=kLoop, calls=%fused_computation.58 | loop fusion | flops 12582912 | bytes 33554432 | tf_op jit(solution)/shard_map/convert_element_type | solution.py:81
  (47 shorter events, 15.6 us)
Async XLA Ops:
  7.2 5.2 copy-start.3
  7.2 5.2 copy-start.4
  7.2 5.7 copy-start.5
  7.2 116.4 %all-gather.4.cloned.1.call-start = ((), (), s32[]{:S(2)}) async-start(), calls=%async_computation | async-start | bytes 2621440 | tf_op jit(solution)/shard_map/all_gather | solution.py:72
  24.7 100.9 %all-gather.6.cloned.1.call-start = ((), (), s32[]{:S(2)}) async-start(), calls=%async_computation.1 | async-start | bytes 2621440 | tf_op jit(solution)/shard_map/all_gather | solution.py:73
  35.4 46.3 %copy-start = (bf16[512,512]{0,1:T(8,128)(2,1)}, bf16[512,512]{0,1:T(8,128)(2,1)S(1)}, u32[]{:S(2)}) copy-start(bf16[512,512]{0,1:T(8,128)(2,1)S(1)} %convolution_convert_fusion.1) | copy-start | bytes 1572868
  36.4 648.1 %all-reduce.2.cloned.1.call-start = ((), (), s32[]{:S(2)}) async-start(), calls=%async_computation.2 | async-start | bytes 33554432 | tf_op jit(solution)/shard_map/psum | solution.py:80
  99.3 14.3 %copy-start.2 = (s32[512]{0:T(512)S(1)}, s32[512]{0:T(512)}, u32[]{:S(2)}) copy-start(s32[512]{0:T(512)} %param.12) | copy-start | bytes 6148
  312.2 1.0 copy-start.1
Sparse Core Ops, SparseCore 0:
  24.8 22.3 all-gather.3
  49.3 19.5 all-gather.5
  312.4 372.1 all-reduce.1
where the time goes:
time: 710 us; the launch traced here: 703 us
  waiting for transfers between devices  370 us (52%)
  matrix products  237 us (33%)
  local copies, waits for them, and re-layouts  39.9 us (6%)
  other arithmetic  31.1 us (4%)
  between operations  14.1 us (2%)
  blocking collectives  9.97 us (1%)
    psum x1, waiting for transfers between devices, local_step(): full_sum = lax.psum(part_sum, 'tp')  370 us
    sub x4, matrix products, attend(): attn_probs = jax.nn.softmax(scores, axis=-1).astype(jnp.bfloat16)  72.9 us
    dot_general x4, matrix products, attend(): jnp.einsum('ngqk,knd->qngd', attn_probs, val_rows, preferred_element_type...  54.2 us
    dot_general x1, matrix products, project(): jnp.dot(normed, w_q, preferred_element_type=jnp.float32)  44.7 us
    dot_general x1, matrix products, local_step(): part_sum = jnp.dot(attn_out, w_o, preferred_element_type=jnp.float32)  44.4 us
  transfers between devices with their start and end apart: 3, of which 1 were waited for; matrix products, arithmetic and copies ran while one was open for 13% of the time, Pallas kernels for 0%

commit v1 on v0

v1 whole, which is shorter than its diff:
```python
import jax
import jax.numpy as jnp
from jax import lax
from jax.experimental import pallas as pl
from jax.experimental.pallas import tpu as pltpu
from jax.sharding import PartitionSpec as P


F32 = jnp.float32
BF16 = jnp.bfloat16
HEAD = 128
LANES = 128
VMEM_BYTES = 60 * 1024 * 1024
CHUNKS = ((512, 1024, 1024, 1536), (1536, 1024, 1024, 512))


def any_spec():
    return pl.BlockSpec(memory_space=pl.ANY)


def rope_head(vec, cos_t, sin_t):
    vec = vec.astype(BF16).astype(F32)
    return (vec * cos_t + pltpu.roll(vec, HEAD // 2, 1) * sin_t).astype(BF16)


def front(half, rows, x_in, gain, pos2, inv_freq, w_q, w_k, w_v):
    d_model = x_in.shape[1]
    kv_cols = w_k.shape[1]
    q_cols = w_q.shape[1]
    bn = kv_cols
    nq = q_cols // bn
    slots = 4
    nx = 4
    xr = rows // nx
    step = 32

    def kernel(x_hbm, gain_ref, pos_ref, freq_ref, wk_hbm, wv_hbm, wq_hbm, q_hbm, kv_ref, r1, r2, r3, x_buf, h_ref, ring, q_buf, cos_ref, sin_ref, freq2_ref, x_sem, w_sem, q_sem, s_sem, r_sem):
        me = lax.axis_index('cp')
        core, across = lax.bitwise_xor(me, 1), lax.bitwise_xor(me, 2)
        barrier = pltpu.get_barrier_semaphore()
        for peer in (core, across):
            pl.semaphore_signal(barrier, inc=1, device_id={'cp': peer}, device_id_type=pl.DeviceIdType.MESH)
        x_copies = [pltpu.make_async_copy(x_hbm.at[pl.ds(half * rows + i * xr, xr)], x_buf.at[pl.ds(i * xr, xr)], x_sem.at[i]) for i in range(nx)]
        for copy in x_copies:
            copy.start()

        def q_load(b):
            slot = lax.rem(b + 2, slots)
            return pltpu.make_async_copy(wq_hbm.at[:, pl.ds(pl.multiple_of(b * bn, bn), bn)], ring.at[slot], w_sem.at[slot])

        kv_loads = [pltpu.make_async_copy(wk_hbm, ring.at[0], w_sem.at[0]), pltpu.make_async_copy(wv_hbm, ring.at[1], w_sem.at[1])]
        for load in kv_loads:
            load.start()
        for b in range(slots - 2):
            q_load(b).start()

        half_dim = HEAD // 2
        freq2_ref[:, :half_dim] = freq_ref[...]
        freq2_ref[:, half_dim:] = freq_ref[...]
        sign = jnp.where(lax.broadcasted_iota(jnp.int32, (LANES, HEAD), 1) < half_dim, -1.0, 1.0)
        for b in range(rows // LANES):
            pos_row = pos_ref[half * (rows // LANES) + b:half * (rows // LANES) + b + 1, :].astype(F32)
            angle = jnp.transpose(jnp.broadcast_to(pos_row, (LANES, LANES))) * freq2_ref[...]
            cos_ref[b * LANES:(b + 1) * LANES, :] = jnp.cos(angle)
            sin_ref[b * LANES:(b + 1) * LANES, :] = jnp.sin(angle) * sign

        for i in range(nx):
            x_copies[i].wait()

            def norm(r, carry):
                at = pl.ds(pl.multiple_of(i * xr + r * step, step), step)
                total = jnp.zeros((step, LANES), F32)
                for c in range(d_model // LANES):
                    v = x_buf[at, c * LANES:(c + 1) * LANES].astype(F32)
                    total += v * v
                inv = lax.rsqrt(jnp.sum(total, axis=1, keepdims=True) / d_model + 1e-5)
                for c in range(d_model // LANES):
                    cols = slice(c * LANES, (c + 1) * LANES)
                    h_ref[at, cols] = (x_buf[at, cols].astype(F32) * inv * gain_ref[:, cols]).astype(BF16)
                return carry

            lax.fori_loop(0, xr // step, norm, 0)

        kv_loads[0].wait()
        acc = jnp.dot(h_ref[...], ring[0], preferred_element_type=F32)
        for g in range(bn // HEAD):
            cols = slice(g * HEAD, (g + 1) * HEAD)
            kv_ref[:, cols] = rope_head(acc[:, cols], cos_ref[...], sin_ref[...])
        q_load(slots - 2).start()
        kv_loads[1].wait()
        kv_ref[:, kv_cols:] = jnp.dot(h_ref[...], ring[1], preferred_element_type=F32).astype(BF16)
        q_load(slots - 1).start()

        pl.semaphore_wait(barrier, 2)
        sends = []
        for n, (dst, peer) in enumerate(((r2, across), (r1, core))):
            sends.append(pltpu.make_async_remote_copy(src_ref=kv_ref, dst_ref=dst, send_sem=s_sem.at[n], recv_sem=r_sem.at[n], device_id={'cp': peer}, device_id_type=pl.DeviceIdType.MESH))
            sends[-1].start()
        forward = pltpu.make_async_remote_copy(src_ref=r2, dst_ref=r3, send_sem=s_sem.at[2], recv_sem=r_sem.at[2], device_id={'cp': core}, device_id_type=pl.DeviceIdType.MESH)

        def q_store(b):
            cols = pl.ds(pl.multiple_of(b * bn, bn), bn)
            return pltpu.make_async_copy(q_buf.at[:, cols], q_hbm.at[:, cols], q_sem.at[b])

        def q_block(b, carry):
            slot = lax.rem(b + 2, slots)
            q_load(b).wait()
            acc = jnp.dot(h_ref[...], ring[slot], preferred_element_type=F32)
            for g in range(bn // HEAD):
                at = pl.ds(pl.multiple_of(b * bn + g * HEAD, HEAD), HEAD)
                q_buf[:, at] = rope_head(acc[:, g * HEAD:(g + 1) * HEAD], cos_ref[...], sin_ref[...])
            q_store(b).start()

            @pl.when(b + slots < nq)
            def _():
                q_load(b + slots).start()

            return carry

        lax.fori_loop(0, nq - 2, q_block, 0)
        sends[0].wait_recv()
        forward.start()
        lax.fori_loop(nq - 2, nq, q_block, 0)
        for b in range(nq):
            q_store(b).wait()
        sends[0].wait_send()
        sends[1].wait()
        forward.wait()

    whole = lambda arr: pl.BlockSpec(arr.shape, lambda i: (0, 0))
    kv_shape = jax.ShapeDtypeStruct((rows, 2 * kv_cols), BF16)
    return pl.pallas_call(
        kernel,
        grid=(1,),
        in_specs=[any_spec(), whole(gain), whole(pos2), whole(inv_freq), any_spec(), any_spec(), any_spec()],
        out_specs=[any_spec(), pl.BlockSpec(kv_shape.shape, lambda i: (0, 0)), any_spec(), any_spec(), any_spec()],
        out_shape=[jax.ShapeDtypeStruct((rows, q_cols), BF16), kv_shape, kv_shape, kv_shape, kv_shape],
        scratch_shapes=[
            pltpu.VMEM((rows, d_model), BF16),
            pltpu.VMEM((rows, d_model), BF16),
            pltpu.VMEM((slots, d_model, bn), BF16),
            pltpu.VMEM((rows, q_cols), BF16),
            pltpu.VMEM((rows, HEAD), F32),
            pltpu.VMEM((rows, HEAD), F32),
            pltpu.VMEM((1, HEAD), F32),
            pltpu.SemaphoreType.DMA((nx,)),
            pltpu.SemaphoreType.DMA((slots,)),
            pltpu.SemaphoreType.DMA((nq,)),
            pltpu.SemaphoreType.DMA((3,)),
            pltpu.SemaphoreType.DMA((3,)),
        ],
        compiler_params=pltpu.CompilerParams(vmem_limit_bytes=VMEM_BYTES, collective_id=half, has_side_effects=True),
        cost_estimate=pl.CostEstimate(flops=2 * rows * d_model * (2 * kv_cols + q_cols), bytes_accessed=2 * d_model * (rows + q_cols), transcendentals=0),
        name="front",
    )(x_in, gain, pos2, inv_freq, w_k, w_v, w_q)


def attend_send(half, rows, cp_size, ids, pos, pos2, q, kv_parts, w_o, cols):
    kv_heads = kv_parts[0].shape[1] // (2 * HEAD)
    group = q.shape[1] // (kv_heads * HEAD)
    qb = kb = 128
    steps = rows // qb
    keys = cp_size * rows * (1 + half)
    scale = HEAD ** -0.5
    parts = len(kv_parts)
    k_dim = q.shape[1]
    half_cols = w_o.shape[1] // 2

    def kernel(ids_ref, pos_ref, pos2_ref, q_hbm, w_hbm, *rest):
        kv_hbm = rest[:parts]
        o_ref, part_ref, kv_all, q_buf, w_buf, s_ref, p_ref, m_ref, l_ref, acc_ref, kv_sem, q_sem, w_sem = rest[parts:]
        dev, tp = ids_ref[0], ids_ref[1]
        copies = []
        for n in range(parts):
            owner = lax.bitwise_xor(dev, n % cp_size)
            piece = owner if n < cp_size else 2 * cp_size - 1 - owner
            copies.append(pltpu.make_async_copy(kv_hbm[n], kv_all.at[pl.ds(pl.multiple_of(piece * rows, rows), rows)], kv_sem.at[n]))
            copies[-1].start()

        def q_copy(n):
            at = pl.ds(pl.multiple_of(n * group * HEAD, group * HEAD), group * HEAD)
            return pltpu.make_async_copy(q_hbm.at[:, at], q_buf.at[:, at], q_sem.at[n])

        for n in range(kv_heads):
            q_copy(n).start()
        w_copy = pltpu.make_async_copy(w_hbm.at[:, pl.ds(pl.multiple_of((1 - tp) * half_cols, half_cols), cols)], w_buf, w_sem)
        w_copy.start()
        for c in copies: c.wait()
        piece = dev if half == 0 else 2 * cp_size - 1 - dev
        lane = lax.broadcasted_iota(jnp.int32, (qb, LANES), 1)
        row = lax.broadcasted_iota(jnp.int32, (qb, LANES), 0)

        def step_body(i, carry):
            n, b = lax.div(i, steps), lax.rem(i, steps)

            @pl.when(b == 0)
            def _(): q_copy(n).wait()

            t0 = piece * rows + b * qb
            p0 = pos_ref[half * rows + b * qb]
            q_rows = pl.ds(pl.multiple_of(b * qb, qb), qb)

            def head_cols(g): return pl.ds(pl.multiple_of((n * group + g) * HEAD, HEAD), HEAD)

            k_cols = pl.ds(pl.multiple_of(n * HEAD, HEAD), HEAD)
            v_cols = pl.ds(pl.multiple_of((kv_heads + n) * HEAD, HEAD), HEAD)
            pos_row = pos2_ref[pl.ds(half * steps + b, 1), :].astype(F32)
            pos_t = jnp.transpose(jnp.broadcast_to(pos_row, (qb, LANES))).astype(jnp.int32)
            t_idx = t0 + row
            first = t_idx - pos_t
            q_stack = jnp.concatenate([q_buf[q_rows, head_cols(g)] for g in range(group)], axis=0)

            @pl.when(p0 <= kb)
            def _():
                w0 = pl.multiple_of(jnp.maximum(t0 - kb, 0), kb)
                at = pl.ds(w0, 2 * kb)
                s_ref[...] = lax.dot_general(q_stack, kv_all[at, k_cols], (((1,), (1,)), ((), ())), preferred_element_type=F32)
                u = w0 + lane
                see = [(u >= first) & (u <= t_idx), (u + kb >= first) & (u + kb <= t_idx)]
                visible = jnp.concatenate(see, axis=1)
                for g in range(group):
                    at_g = slice(g * qb, (g + 1) * qb)
                    s = jnp.where(visible, s_ref[at_g] * scale, -1e30)
                    s_ref[at_g] = s
                    m_ref[g] = jnp.broadcast_to(jnp.max(s, axis=1, keepdims=True), (qb, LANES))
                for g in range(group):
                    at_g = slice(g * qb, (g + 1) * qb)
                    m = m_ref[g]
                    e = jnp.exp(s_ref[at_g] - jnp.concatenate([m, m], axis=1))
                    s_ref[at_g] = e
                    l_ref[g] = 1.0 / jnp.broadcast_to(jnp.sum(e, axis=1, keepdims=True), (qb, LANES))
                for g in range(group):
                    at_g = slice(g * qb, (g + 1) * qb)
                    l = l_ref[g]
                    p_ref[at_g] = (s_ref[at_g] * jnp.concatenate([l, l], axis=1)).astype(BF16)
                o = jnp.dot(p_ref[...], kv_all[at, v_cols], preferred_element_type=F32).astype(BF16)
                for g in range(group):
                    o_ref[q_rows, head_cols(g)] = o[g * qb:(g + 1) * qb]

            @pl.when(p0 > kb)
            def _():
                kb0 = lax.div(t0 - p0, kb)
                kb1 = lax.div(t0, kb) + 1
                m_ref[...] = jnp.full_like(m_ref, -1e30)
                l_ref[...] = jnp.zeros_like(l_ref)
                acc_ref[...] = jnp.zeros_like(acc_ref)

                def block(j):
                    at = pl.ds(pl.multiple_of(j * kb, kb), kb)
                    u = j * kb + lane
                    s_ref[:, :kb] = lax.dot_general(q_stack, kv_all[at, k_cols], (((1,), (1,)), ((), ())), preferred_element_type=F32)
                    return at, (u >= first) & (u <= t_idx)

                def stats(j, carry):
                    _, visible = block(j)
                    for g in range(group):
                        s = jnp.where(visible, s_ref[g * qb:(g + 1) * qb, :kb] * scale, -1e30)
                        m_old = m_ref[g]
                        m_new = jnp.maximum(m_old, jnp.max(s, axis=1, keepdims=True))
                        l_ref[g] = l_ref[g] * jnp.exp(m_old - m_new) + jnp.sum(jnp.exp(s - m_new), axis=1, keepdims=True)
                        m_ref[g] = m_new
                    return carry

                def weigh(j, carry):
                    at, visible = block(j)
                    for g in range(group):
                        at_g = slice(g * qb, (g + 1) * qb)
                        s = jnp.where(visible, s_ref[at_g, :kb] * scale, -1e30)
                        p_ref[at_g, :kb] = (jnp.exp(s - m_ref[g]) / l_ref[g]).astype(BF16)
                    acc_ref[...] += jnp.dot(p_ref[:, :kb], kv_all[at, v_cols], preferred_element_type=F32)
                    return carry

                lax.fori_loop(kb0, kb1, stats, 0)
                lax.fori_loop(kb0, kb1, weigh, 0)
                for g in range(group):
                    o_ref[q_rows, head_cols(g)] = acc_ref[g * qb:(g + 1) * qb].astype(BF16)

            return carry

        lax.fori_loop(0, kv_heads * steps, step_body, 0)
        w_copy.wait()
        part_ref[...] = jnp.dot(o_ref[...], w_buf[...], preferred_element_type=F32)

    whole = lambda shape: pl.BlockSpec(shape, lambda i, *_: (0, 0))
    return pl.pallas_call(
        kernel,
        grid_spec=pltpu.PrefetchScalarGridSpec(
            num_scalar_prefetch=2, grid=(1,),
            in_specs=[whole(pos2.shape), any_spec(), any_spec()] + [any_spec()] * parts,
            out_specs=[whole(q.shape), whole((rows, cols))],
            scratch_shapes=[
                pltpu.VMEM((keys, kv_parts[0].shape[1]), BF16), pltpu.VMEM(q.shape, BF16), pltpu.VMEM((k_dim, cols), BF16),
                pltpu.VMEM((group * qb, 2 * kb), F32), pltpu.VMEM((group * qb, 2 * kb), BF16),
                pltpu.VMEM((group, qb, LANES), F32), pltpu.VMEM((group, qb, LANES), F32), pltpu.VMEM((group * qb, HEAD), F32),
                pltpu.SemaphoreType.DMA((parts,)), pltpu.SemaphoreType.DMA((kv_heads,)), pltpu.SemaphoreType.DMA,
            ]),
        out_shape=[jax.ShapeDtypeStruct(q.shape, BF16), jax.ShapeDtypeStruct((rows, cols), F32)],
        compiler_params=pltpu.CompilerParams(vmem_limit_bytes=VMEM_BYTES),
        cost_estimate=pl.CostEstimate(flops=4 * rows * q.shape[1] * 512 + 2 * rows * k_dim * cols, bytes_accessed=2 * k_dim * cols, transcendentals=0),
        name="attend_send")(ids, pos, pos2, q, w_o, *kv_parts)


def out_send(rows, tp_me, o, w_o, col0, cols):
    k_dim = o.shape[1]
    bn = 512
    own_blocks = w_o.shape[1] // 2 // bn

    def kernel(tp_ref, o_ref, w_ref, *rest):
        rest[-1][...] = jnp.dot(o_ref[...], w_ref[...], preferred_element_type=F32)

    return pl.pallas_call(
        kernel,
        grid_spec=pltpu.PrefetchScalarGridSpec(
            num_scalar_prefetch=1,
            grid=(cols // bn,),
            in_specs=[pl.BlockSpec((rows, k_dim), lambda i, tp: (0, 0)), pl.BlockSpec((k_dim, bn), lambda i, tp: (0, (1 - tp[0]) * own_blocks + col0 // bn + i))],
            out_specs=pl.BlockSpec((rows, bn), lambda i, tp: (0, i)),
        ),
        out_shape=jax.ShapeDtypeStruct((rows, cols), F32),
        compiler_params=pltpu.CompilerParams(vmem_limit_bytes=VMEM_BYTES),
        cost_estimate=pl.CostEstimate(flops=2 * rows * k_dim * cols, bytes_accessed=2 * k_dim * (rows + cols), transcendentals=0),
        name="out_send",
    )(tp_me, o, w_o)


def out_own(half, rows, tp_me, o, w_o, x_in, recv, y_buf, col0, cols):
    k_dim = o.shape[1]
    bn = 512
    own_blocks = w_o.shape[1] // 2 // bn

    def col(i, tp):
        return tp[0] * own_blocks + col0 // bn + i

    def kernel(tp_ref, o_ref, w_ref, x_ref, r_ref, *rest):
        y_ref, c_ref = rest[-2:]
        acc = jnp.dot(o_ref[...], w_ref[...], preferred_element_type=F32)
        out = (x_ref[...].astype(F32) + (acc + r_ref[...])).astype(BF16)
        y_ref[...] = out
        c_ref[...] = out

    ins = [o, w_o, x_in, recv] + ([] if y_buf is None else [y_buf])
    wide = pl.BlockSpec((rows, bn), lambda i, tp: (half, col(i, tp)))
    narrow = pl.BlockSpec((rows, bn), lambda i, tp: (0, i))
    return pl.pallas_call(
        kernel,
        grid_spec=pltpu.PrefetchScalarGridSpec(
            num_scalar_prefetch=1,
            grid=(cols // bn,),
            in_specs=[pl.BlockSpec((rows, k_dim), lambda i, tp: (0, 0)), pl.BlockSpec((k_dim, bn), lambda i, tp: (0, col(i, tp))), wide, narrow] + [any_spec()] * (len(ins) - 4),
            out_specs=[wide, narrow],
        ),
        out_shape=[jax.ShapeDtypeStruct(x_in.shape, BF16), jax.ShapeDtypeStruct((rows, cols), BF16)],
        input_output_aliases={} if y_buf is None else {5: 0},
        compiler_params=pltpu.CompilerParams(vmem_limit_bytes=VMEM_BYTES),
        cost_estimate=pl.CostEstimate(flops=2 * rows * k_dim * cols, bytes_accessed=2 * k_dim * (rows + cols), transcendentals=0),
        name="out_own",
    )(tp_me, *ins)


def place(half, rows, tp_me, recv, y_buf, col0, cols):
    bn = 512
    own_blocks = y_buf.shape[1] // 2 // bn

    def kernel(tp_ref, r_ref, y_in, y_ref):
        y_ref[...] = r_ref[...]

    return pl.pallas_call(
        kernel,
        grid_spec=pltpu.PrefetchScalarGridSpec(
            num_scalar_prefetch=1,
            grid=(cols // bn,),
            in_specs=[pl.BlockSpec((rows, bn), lambda i, tp: (0, i)), any_spec()],
            out_specs=pl.BlockSpec((rows, bn), lambda i, tp: (half, (1 - tp[0]) * own_blocks + col0 // bn + i)),
        ),
        out_shape=jax.ShapeDtypeStruct(y_buf.shape, BF16),
        input_output_aliases={2: 0},
        compiler_params=pltpu.CompilerParams(vmem_limit_bytes=VMEM_BYTES),
        cost_estimate=pl.CostEstimate(flops=rows * cols, bytes_accessed=4 * rows * cols, transcendentals=0),
        name="place",
    )(tp_me, recv, y_buf)


def solution(mesh):
    cp_size = mesh.shape['cp']
    tp_size = mesh.shape['tp']
    swap_tp = [(j, tp_size - 1 - j) for j in range(tp_size)]

    def local_step(x_in, doc_id, pos_in_doc, norm_gain, w_q, w_k, w_v, w_o, inv_freq):
        local_rows, d_model = x_in.shape
        rows = local_rows // 2
        kv_cols = w_k.shape[1]
        me = lax.axis_index('cp').astype(jnp.int32)
        tp_one = lax.axis_index('tp').astype(jnp.int32)
        ids = jnp.stack([me, tp_one])
        tp_me = tp_one.reshape(1)
        gain = norm_gain.reshape(1, d_model)
        pos2 = pos_in_doc.reshape(local_rows // LANES, LANES)
        freq = inv_freq.reshape(1, HEAD // 2)

        kv_parts, sent, attn = [], [], []
        for half in range(2):
            q, *parts = front(half, rows, x_in, gain, pos2, freq, w_q, w_k, w_v)
            kv_parts += parts
            sizes = CHUNKS[half]
            o, part = attend_send(half, rows, cp_size, ids, pos_in_doc, pos2, q, kv_parts, w_o, sizes[0])
            attn.append(o)
            col0 = 0
            for c, cols in enumerate(sizes):
                if c:
                    part = out_send(rows, tp_me, o, w_o, col0, cols)
                sent.append(lax.ppermute(part, 'tp', swap_tp))
                col0 += cols

        y_buf = None
        results = []
        where = [(half, sum(CHUNKS[half][:c]), cols) for half in range(2) for c, cols in enumerate(CHUNKS[half])]
        for n, (half, col0, cols) in enumerate(where):
            y_buf, block = out_own(half, rows, tp_me, attn[half], w_o, x_in, sent[n], y_buf, col0, cols)
            results.append(lax.ppermute(block, 'tp', swap_tp))
        for n, (half, col0, cols) in enumerate(where):
            y_buf = place(half, rows, tp_me, results[n], y_buf, col0, cols)
        kv_all = jnp.concatenate([kv_parts[0], kv_parts[cp_size]], axis=0)
        k_out = kv_all[:, :kv_cols].reshape(local_rows, kv_cols // HEAD, HEAD)
        v_out = kv_all[:, kv_cols:].reshape(local_rows, kv_cols // HEAD, HEAD)
        return y_buf, k_out, v_out

    row_spec = P(('dp', 'cp'))
    in_specs = (P(('dp', 'cp'), None), row_spec, row_spec, P(), P(None, 'tp'), P(None, 'tp'), P(None, 'tp'), P('tp', None), P())
    out_specs = (P(('dp', 'cp'), None), P(('dp', 'cp'), 'tp', None), P(('dp', 'cp'), 'tp', None))

    return jax.shard_map(local_step, mesh=mesh, in_specs=in_specs, out_specs=out_specs, check_vma=False)
```

time: 710 us -> 344 us (0.48)
  waiting for transfers between devices: 370 us -> 102 us
  matrix products: 237 us -> 0 us
  Pallas kernels: 0 us -> 214 us
  local copies, waits for them, and re-layouts: 39.9 us -> 4.69 us
  other arithmetic: 31.1 us -> 0.59 us
  starting transfers between devices: 0.94 us -> 20.6 us
  between operations: 14.1 us -> 0.75 us
  blocking collectives: 9.97 us -> 0 us
    psum x1 -> x0, waiting for transfers between devices: 370 us -> none  [local_step(): full_sum = lax.psum(part_sum, 'tp')]
    pallas_call x0 -> x26, Pallas kernels: none -> 214 us  [the longest x2 74.3 us: front(): pl.pallas_call(kernel, grid=(1,), in_specs=[any_spec(), whole(gain), whol...]
    dot_general x8 -> x0, matrix products: 164 us -> none  [the longest x4 54.2 us: attend(): jnp.einsum('ngqk,knd->qngd', attn_probs, val_rows, preferred_element_type...]
    ppermute x0 -> x16, waiting for transfers between devices: none -> 102 us  [the longest x8 51.9 us: local_step(): sent.append(lax.ppermute(part, 'tp', swap_tp))]
    sub x4 -> x0, matrix products: 72.9 us -> none  [attend(): attn_probs = jax.nn.softmax(scores, axis=-1).astype(jnp.bfloat16)]
    ppermute x0 -> x16, starting transfers between devices: none -> 20.6 us  [the longest x8 10.6 us: local_step(): sent.append(lax.ppermute(part, 'tp', swap_tp))]
    reshape x3 -> x2, local copies, waits for them, and re-layouts: 14.7 us -> 1.83 us  [the longest x1 0.92 us: local_step(): k_out = kv_all[:, :kv_cols].reshape(local_rows, kv_cols // HEAD, HEAD)]
    convert_element_type x2 -> x0, other arithmetic: 12.1 us -> none  [the longest x1 12.1 us: local_step(): y_out = (x_in.astype(jnp.float32) + full_sum).astype(jnp.bfloat16)]
  transfers between devices with their start and end apart: 3 -> 16, of which waited for: 1 -> 9; matrix products, arithmetic and copies ran while one was open for 13% -> 1% of each run, Pallas kernels for 0% -> 45%
where the time goes in v1:
time: 344 us; the launch traced here: 343 us
  Pallas kernels  214 us (62%)
  waiting for transfers between devices  102 us (30%)
  starting transfers between devices  20.6 us (6%)
  local copies, waits for them, and re-layouts  4.69 us (1%)
    pallas_call x2, Pallas kernels, front(): pl.pallas_call(kernel, grid=(1,), in_specs=[any_spec(), whole(gain), whol...  74.3 us
    pallas_call x8, Pallas kernels, out_own(): pl.pallas_call(kernel, grid_spec=pltpu.PrefetchScalarGridSpec(num_scalar_...  55.2 us
    ppermute x8, waiting for transfers between devices, local_step(): sent.append(lax.ppermute(part, 'tp', swap_tp))  51.9 us
    ppermute x8, waiting for transfers between devices, local_step(): results.append(lax.ppermute(block, 'tp', swap_tp))  50.4 us
    pallas_call x6, Pallas kernels, out_send(): pl.pallas_call(kernel, grid_spec=pltpu.PrefetchScalarGridSpec(num_scalar_...  38.6 us
    pallas_call x2, Pallas kernels, attend_send(): pl.pallas_call(kernel, grid_spec=pltpu.PrefetchScalarGridSpec(num_scalar_...  29.7 us
    pallas_call x8, Pallas kernels, place(): pl.pallas_call(kernel, grid_spec=pltpu.PrefetchScalarGridSpec(num_scalar_...  16.1 us
    ppermute x8, starting transfers between devices, local_step(): sent.append(lax.ppermute(part, 'tp', swap_tp))  10.6 us
  transfers between devices with their start and end apart: 16, of which 9 were waited for; matrix products, arithmetic and copies ran while one was open for 1% of the time, Pallas kernels for 45%

profile of v1, /device:TPU:0, one launch (start us, length us, event | category | flops | bytes accessed | tf_op | source)
XLA Modules:
  0.0 342.9 jit_solution(13134076734698276840)
XLA Ops:
  1.2 37.5 %front.3 = (bf16[256,4096]{1,0:T(8,128)(2,1)}, bf16[256,1024]{1,0:T(8,128)(2,1)}, bf16[256,1024]{1,0:T(8,128)(2,1)}, bf16[256,1024]{1,0:T(8,128)(2,1)}, bf16[256,1024]{1,0:T(8,128)(2,1)}) custom-call(bf16[512,8192]{1,0:T(8,128)(2,1)} %x_ref.15, f32[1,8192]{1,0:T(1,128)} %bitcast.5, s32[4,128]{1,0:T(4,128)} %bitcast.7, f32[1,64]{1,0:T(1,128)} %bitcast.11, ...), custom_call_target="tpu_custom_call" | custom-call | flops 21474836480 | bytes 71303168 | tf_op jit(solution)/shard_map/front/pallas_call | solution.py:132
  38.7 13.2 %attend_send.3 = (bf16[256,4096]{1,0:T(8,128)(2,1)}, f32[256,512]{1,0:T(8,128)}) custom-call(s32[2]{0:T(128)} %pad_add_fusion.ids_ref, s32[512]{0:T(512)} %pos_ref.3, s32[4,128]{1,0:T(4,128)} %bitcast.8, bf16[256,4096]{1,0:T(8,128)(2,1)} %get-tuple-element.44.q_hbm, bf16[4096,8192]{1,0:T(8,128)(2,1)} %w_ref.27, bf16[256,1024]{1,0:T(8,128)(2,1)} %get-tuple-element.34.rest_0_, ...), custom_call_target="tpu_custom_call" | custom-call | flops 3221225472 | bytes 4194304 | tf_op jit(solution)/shard_map/attend_send/pallas_call | solution.py:285
  52.0 6.2 %out_send.11 = f32[256,1024]{1,0:T(8,128)} custom-call(s32[1]{0:T(128)} %bitcast.tp_ref, bf16[256,4096]{1,0:T(8,128)(2,1)} %get-tuple-element.45.o_ref, bf16[4096,8192]{1,0:T(8,128)(2,1)} %w_ref.27), custom_call_target="tpu_custom_call" | custom-call | flops 2147483648 | bytes 10485760 | tf_op jit(solution)/shard_map/out_send/pallas_call | solution.py:311
  61.0 8.8 %out_send.9 = f32[256,1536]{1,0:T(8,128)} custom-call(s32[1]{0:T(128)} %bitcast.tp_ref, bf16[256,4096]{1,0:T(8,128)(2,1)} %get-tuple-element.45.o_ref, bf16[4096,8192]{1,0:T(8,128)(2,1)} %w_ref.27), custom_call_target="tpu_custom_call" | custom-call | flops 3221225472 | bytes 14680064 | tf_op jit(solution)/shard_map/out_send/pallas_call | solution.py:311
  69.8 36.9 %front.2 = (bf16[256,4096]{1,0:T(8,128)(2,1)}, bf16[256,1024]{1,0:T(8,128)(2,1)}, bf16[256,1024]{1,0:T(8,128)(2,1)}, bf16[256,1024]{1,0:T(8,128)(2,1)}, bf16[256,1024]{1,0:T(8,128)(2,1)}) custom-call(bf16[512,8192]{1,0:T(8,128)(2,1)} %x_ref.15, f32[1,8192]{1,0:T(1,128)} %bitcast.6, s32[4,128]{1,0:T(4,128)} %bitcast.9, f32[1,64]{1,0:T(1,128)} %bitcast.12, ...), custom_call_target="tpu_custom_call" | custom-call | flops 21474836480 | bytes 71303168 | tf_op jit(solution)/shard_map/front/pallas_call | solution.py:132
  106.7 16.4 %attend_send.2 = (bf16[256,4096]{1,0:T(8,128)(2,1)}, f32[256,1536]{1,0:T(8,128)}) custom-call(s32[2]{0:T(128)} %pad_add_fusion.ids_ref, s32[512]{0:T(512)} %pos_ref.3, s32[4,128]{1,0:T(4,128)} %bitcast.10, bf16[256,4096]{1,0:T(8,128)(2,1)} %get-tuple-element.33.q_hbm, bf16[4096,8192]{1,0:T(8,128)(2,1)} %w_ref.27, ...), custom_call_target="tpu_custom_call" | custom-call | flops 5368709120 | bytes 12582912 | tf_op jit(solution)/shard_map/attend_send/pallas_call | solution.py:285
  125.2 6.2 %out_send.10 = f32[256,1024]{1,0:T(8,128)} custom-call(s32[1]{0:T(128)} %bitcast.tp_ref, bf16[256,4096]{1,0:T(8,128)(2,1)} %get-tuple-element.45.o_ref, bf16[4096,8192]{1,0:T(8,128)(2,1)} %w_ref.27), custom_call_target="tpu_custom_call" | custom-call | flops 2147483648 | bytes 10485760 | tf_op jit(solution)/shard_map/out_send/pallas_call | solution.py:311
  138.3 6.3 %out_send.8 = f32[256,1024]{1,0:T(8,128)} custom-call(s32[1]{0:T(128)} %bitcast.tp_ref, bf16[256,4096]{1,0:T(8,128)(2,1)} %get-tuple-element.42.o_ref, bf16[4096,8192]{1,0:T(8,128)(2,1)} %w_ref.27), custom_call_target="tpu_custom_call" | custom-call | flops 2147483648 | bytes 10485760 | tf_op jit(solution)/shard_map/out_send/pallas_call | solution.py:311
  144.5 6.2 %out_send.7 = f32[256,1024]{1,0:T(8,128)} custom-call(s32[1]{0:T(128)} %bitcast.tp_ref, bf16[256,4096]{1,0:T(8,128)(2,1)} %get-tuple-element.42.o_ref, bf16[4096,8192]{1,0:T(8,128)(2,1)} %w_ref.27), custom_call_target="tpu_custom_call" | custom-call | flops 2147483648 | bytes 10485760 | tf_op jit(solution)/shard_map/out_send/pallas_call | solution.py:311
  150.7 42.2 %collective-permute-done.7.r_ref = f32[256,512]{1,0:T(8,128)S(1)} collective-permute-done((f32[256,512]{1,0:T(8,128)S(1)}, f32[256,512]{1,0:T(8,128)S(1)}, u32[]{:S(2)}, u32[]{:S(2)}) %collective-permute-start.7) | collective-permute-done | bytes 524320 | tf_op jit(solution)/shard_map/ppermute | solution.py:411
  194.7 5.0 %out_own.8 = (bf16[512,8192]{1,0:T(8,128)(2,1)}, bf16[256,512]{1,0:T(8,128)(2,1)}) custom-call(s32[1]{0:T(128)} %bitcast.tp_ref, bf16[256,4096]{1,0:T(8,128)(2,1)} %get-tuple-element.45.o_ref, bf16[4096,8192]{1,0:T(8,128)(2,1)} %w_ref.27, bf16[512,8192]{1,0:T(8,128)(2,1)} %x_ref.15, f32[256,512]{1,0:T(8,128)} %copy-done.8), custom_call_target="tpu_custom_call" | custom-call | flops 1073741824 | bytes 6291456 | tf_op jit(solution)/shard_map/out_own/pallas_call | solution.py:344
  200.5 6.6 %out_own.9 = (bf16[512,8192]{1,0:T(8,128)(2,1)}, bf16[256,1024]{1,0:T(8,128)(2,1)}) custom-call(s32[1]{0:T(128)} %bitcast.tp_ref, bf16[256,4096]{1,0:T(8,128)(2,1)} %get-tuple-element.45.o_ref, bf16[4096,8192]{1,0:T(8,128)(2,1)} %w_ref.27, bf16[512,8192]{1,0:T(8,128)(2,1)} %x_ref.15, ...), custom_call_target="tpu_custom_call", output_to_operand_aliasing={{0}: (5, {})} | custom-call | flops 2147483648 | bytes 10485760 | tf_op jit(solution)/shard_map/out_own/pallas_call | solution.py:344
  208.3 6.6 %out_own.10 = (bf16[512,8192]{1,0:T(8,128)(2,1)}, bf16[256,1024]{1,0:T(8,128)(2,1)}) custom-call(s32[1]{0:T(128)} %bitcast.tp_ref, bf16[256,4096]{1,0:T(8,128)(2,1)} %get-tuple-element.45.o_ref, bf16[4096,8192]{1,0:T(8,128)(2,1)} %w_ref.27, bf16[512,8192]{1,0:T(8,128)(2,1)} %x_ref.15, f32[256,1024]{1,0:T(8,128)} %copy-done.4, ...), custom_call_target="tpu_custom_call", output_to_operand_aliasing={{0}: (5, {})} | custom-call | flops 2147483648 | bytes 10485760 | tf_op jit(solution)/shard_map/out_own/pallas_call | solution.py:344
  215.9 9.3 %out_own.11 = (bf16[512,8192]{1,0:T(8,128)(2,1)}, bf16[256,1536]{1,0:T(8,128)(2,1)}) custom-call(s32[1]{0:T(128)} %bitcast.tp_ref, bf16[256,4096]{1,0:T(8,128)(2,1)} %get-tuple-element.45.o_ref, bf16[4096,8192]{1,0:T(8,128)(2,1)} %w_ref.27, bf16[512,8192]{1,0:T(8,128)(2,1)} %x_ref.15, ...), custom_call_target="tpu_custom_call", output_to_operand_aliasing={{0}: (5, {})} | custom-call | flops 3221225472 | bytes 14680064 | tf_op jit(solution)/shard_map/out_own/pallas_call | solution.py:344
  226.3 9.3 %out_own.12 = (bf16[512,8192]{1,0:T(8,128)(2,1)}, bf16[256,1536]{1,0:T(8,128)(2,1)}) custom-call(s32[1]{0:T(128)} %bitcast.tp_ref, bf16[256,4096]{1,0:T(8,128)(2,1)} %get-tuple-element.42.o_ref, bf16[4096,8192]{1,0:T(8,128)(2,1)} %w_ref.27, bf16[512,8192]{1,0:T(8,128)(2,1)} %x_ref.15, ...), custom_call_target="tpu_custom_call", output_to_operand_aliasing={{0}: (5, {})} | custom-call | flops 3221225472 | bytes 14680064 | tf_op jit(solution)/shard_map/out_own/pallas_call | solution.py:344
  236.6 6.6 %out_own.13 = (bf16[512,8192]{1,0:T(8,128)(2,1)}, bf16[256,1024]{1,0:T(8,128)(2,1)}) custom-call(s32[1]{0:T(128)} %bitcast.tp_ref, bf16[256,4096]{1,0:T(8,128)(2,1)} %get-tuple-element.42.o_ref, bf16[4096,8192]{1,0:T(8,128)(2,1)} %w_ref.27, bf16[512,8192]{1,0:T(8,128)(2,1)} %x_ref.15, f32[256,1024]{1,0:T(8,128)} %copy-done.3, ...), custom_call_target="tpu_custom_call", output_to_operand_aliasing={{0}: (5, {})} | custom-call | flops 2147483648 | bytes 10485760 | tf_op jit(solution)/shard_map/out_own/pallas_call | solution.py:344
  243.2 9.7 %collective-permute-done.r_ref = f32[256,512]{1,0:T(8,128)S(1)} collective-permute-done((f32[256,512]{1,0:T(8,128)}, f32[256,512]{1,0:T(8,128)S(1)}, u32[]{:S(2)}, u32[]{:S(2)}) %collective-permute-start) | collective-permute-done | bytes 524320 | tf_op jit(solution)/shard_map/ppermute | solution.py:411
  255.6 6.7 %out_own.14 = (bf16[512,8192]{1,0:T(8,128)(2,1)}, bf16[256,1024]{1,0:T(8,128)(2,1)}) custom-call(s32[1]{0:T(128)} %bitcast.tp_ref, bf16[256,4096]{1,0:T(8,128)(2,1)} %get-tuple-element.42.o_ref, bf16[4096,8192]{1,0:T(8,128)(2,1)} %w_ref.27, bf16[512,8192]{1,0:T(8,128)(2,1)} %x_ref.15, f32[256,1024]{1,0:T(8,128)} %copy-done.2, ...), custom_call_target="tpu_custom_call", output_to_operand_aliasing={{0}: (5, {})} | custom-call | flops 2147483648 | bytes 10485760 | tf_op jit(solution)/shard_map/out_own/pallas_call | solution.py:344
  263.4 6.5 %collective-permute-done.14.r_ref = bf16[256,1024]{1,0:T(8,128)(2,1)} collective-permute-done((bf16[256,1024]{1,0:T(8,128)(2,1)}, bf16[256,1024]{1,0:T(8,128)(2,1)}, u32[]{:S(2)}, u32[]{:S(2)}) %collective-permute-start.14) | collective-permute-done | bytes 524320 | tf_op jit(solution)/shard_map/ppermute | solution.py:419
  271.7 5.0 %out_own.15 = (bf16[512,8192]{1,0:T(8,128)(2,1)}, bf16[256,512]{1,0:T(8,128)(2,1)}) custom-call(s32[1]{0:T(128)} %bitcast.tp_ref, bf16[256,4096]{1,0:T(8,128)(2,1)} %get-tuple-element.42.o_ref, bf16[4096,8192]{1,0:T(8,128)(2,1)} %w_ref.27, bf16[512,8192]{1,0:T(8,128)(2,1)} %x_ref.15, f32[256,512]{1,0:T(8,128)} %copy-done.7, ...), custom_call_target="tpu_custom_call", output_to_operand_aliasing={{0}: (5, {})} | custom-call | flops 1073741824 | bytes 6291456 | tf_op jit(solution)/shard_map/out_own/pallas_call | solution.py:344
  289.9 7.9 %collective-permute-done.12.r_ref = bf16[256,1536]{1,0:T(8,128)(2,1)S(1)} collective-permute-done((bf16[256,1536]{1,0:T(8,128)(2,1)}, bf16[256,1536]{1,0:T(8,128)(2,1)S(1)}, u32[]{:S(2)}, u32[]{:S(2)}) %collective-permute-start.12) | collective-permute-done | bytes 786464 | tf_op jit(solution)/shard_map/ppermute | solution.py:419
  301.6 13.1 %collective-permute-done.11.r_ref = bf16[256,1536]{1,0:T(8,128)(2,1)S(1)} collective-permute-done((bf16[256,1536]{1,0:T(8,128)(2,1)}, bf16[256,1536]{1,0:T(8,128)(2,1)S(1)}, u32[]{:S(2)}, u32[]{:S(2)}) %collective-permute-start.11) | collective-permute-done | bytes 786464 | tf_op jit(solution)/shard_map/ppermute | solution.py:419
  318.4 7.6 %collective-permute-done.10.r_ref = bf16[256,1024]{1,0:T(8,128)(2,1)} collective-permute-done((bf16[256,1024]{1,0:T(8,128)(2,1)}, bf16[256,1024]{1,0:T(8,128)(2,1)}, u32[]{:S(2)}, u32[]{:S(2)}) %collective-permute-start.10) | collective-permute-done | bytes 524320 | tf_op jit(solution)/shard_map/ppermute | solution.py:419
  327.8 9.5 %collective-permute-done.9.r_ref = bf16[256,1024]{1,0:T(8,128)(2,1)} collective-permute-done((bf16[256,1024]{1,0:T(8,128)(2,1)}, bf16[256,1024]{1,0:T(8,128)(2,1)}, u32[]{:S(2)}, u32[]{:S(2)}) %collective-permute-start.9) | collective-permute-done | bytes 524320 | tf_op jit(solution)/shard_map/ppermute | solution.py:419
  (64 shorter events, 52.7 us)
Async XLA Ops:
  58.2 141.5 %collective-permute-start.6 = (f32[256,1024]{1,0:T(8,128)}, f32[256,1024]{1,0:T(8,128)}, u32[]{:S(2)}, u32[]{:S(2)}) collective-permute-start(f32[256,1024]{1,0:T(8,128)} %out_send.11), channel_id=1, source_target_pairs={{0,4},{4,0},{1,5},{5,1},{2,6},{6,2},{3,7},{7,3}} | collective-permute-start | bytes 3145736 | tf_op jit(solution)/shard_map/ppermute | solution.py:411
  69.8 145.1 %collective-permute-start.4 = (f32[256,1536]{1,0:T(8,128)}, f32[256,1536]{1,0:T(8,128)}, u32[]{:S(2)}, u32[]{:S(2)}) collective-permute-start(f32[256,1536]{1,0:T(8,128)} %out_send.9), channel_id=1, source_target_pairs={{0,4},{4,0},{1,5},{5,1},{2,6},{6,2},{3,7},{7,3}} | collective-permute-start | bytes 4718600 | tf_op jit(solution)/shard_map/ppermute | solution.py:411
  123.1 8.3 %copy-start.11 = (f32[256,512]{1,0:T(8,128)S(1)}, f32[256,512]{1,0:T(8,128)}, u32[]{:S(2)}) copy-start(f32[256,512]{1,0:T(8,128)} %get-tuple-element.46) | copy-start | bytes 1572868
  123.1 102.1 %collective-permute-start.3 = (f32[256,1536]{1,0:T(8,128)}, f32[256,1536]{1,0:T(8,128)}, u32[]{:S(2)}, u32[]{:S(2)}) collective-permute-start(f32[256,1536]{1,0:T(8,128)} %get-tuple-element.43), channel_id=1, source_target_pairs={{0,4},{4,0},{1,5},{5,1},{2,6},{6,2},{3,7},{7,3}} | collective-permute-start | bytes 4718600 | tf_op jit(solution)/shard_map/ppermute | solution.py:411
  131.4 75.7 %collective-permute-start.5 = (f32[256,1024]{1,0:T(8,128)}, f32[256,1024]{1,0:T(8,128)S(1)}, u32[]{:S(2)}, u32[]{:S(2)}) collective-permute-start(f32[256,1024]{1,0:T(8,128)} %out_send.10), channel_id=1, source_target_pairs={{0,4},{4,0},{1,5},{5,1},{2,6},{6,2},{3,7},{7,3}} | collective-permute-start | bytes 3145736 | tf_op jit(solution)/shard_map/ppermute | solution.py:411
  131.5 61.5 %collective-permute-start.7 = (f32[256,512]{1,0:T(8,128)S(1)}, f32[256,512]{1,0:T(8,128)S(1)}, u32[]{:S(2)}, u32[]{:S(2)}) collective-permute-start(f32[256,512]{1,0:T(8,128)S(1)} %copy-done.11), channel_id=1, source_target_pairs={{0,4},{4,0},{1,5},{5,1},{2,6},{6,2},{3,7},{7,3}} | collective-permute-start | bytes 1572872 | tf_op jit(solution)/shard_map/ppermute | solution.py:411
  192.9 1.7 copy-start.8
  192.9 42.7 %collective-permute-start.2 = (f32[256,1024]{1,0:T(8,128)}, f32[256,1024]{1,0:T(8,128)S(1)}, u32[]{:S(2)}, u32[]{:S(2)}) collective-permute-start(f32[256,1024]{1,0:T(8,128)} %out_send.8), channel_id=1, source_target_pairs={{0,4},{4,0},{1,5},{5,1},{2,6},{6,2},{3,7},{7,3}} | collective-permute-start | bytes 3145736 | tf_op jit(solution)/shard_map/ppermute | solution.py:411
  199.7 54.9 %collective-permute-start.1 = (f32[256,1024]{1,0:T(8,128)}, f32[256,1024]{1,0:T(8,128)S(1)}, u32[]{:S(2)}, u32[]{:S(2)}) collective-permute-start(f32[256,1024]{1,0:T(8,128)} %out_send.7), channel_id=1, source_target_pairs={{0,4},{4,0},{1,5},{5,1},{2,6},{6,2},{3,7},{7,3}} | collective-permute-start | bytes 3145736 | tf_op jit(solution)/shard_map/ppermute | solution.py:411
  207.1 1.3 copy-start.4
  207.1 45.8 %collective-permute-start = (f32[256,512]{1,0:T(8,128)}, f32[256,512]{1,0:T(8,128)S(1)}, u32[]{:S(2)}, u32[]{:S(2)}) collective-permute-start(f32[256,512]{1,0:T(8,128)} %out_send.6), channel_id=1, source_target_pairs={{0,4},{4,0},{1,5},{5,1},{2,6},{6,2},{3,7},{7,3}} | collective-permute-start | bytes 1572872 | tf_op jit(solution)/shard_map/ppermute | solution.py:411
  214.9 47.3 %collective-permute-start.15 = (bf16[256,512]{1,0:T(8,128)(2,1)}, bf16[256,512]{1,0:T(8,128)(2,1)S(1)}, u32[]{:S(2)}, u32[]{:S(2)}) collective-permute-start(bf16[256,512]{1,0:T(8,128)(2,1)} %get-tuple-element.61), channel_id=1, source_target_pairs={{0,4},{4,0},{1,5},{5,1},{2,6},{6,2},{3,7},{7,3}} | collective-permute-start | bytes 786440 | tf_op jit(solution)/shard_map/ppermute | solution.py:419
  225.2 44.6 %collective-permute-start.14 = (bf16[256,1024]{1,0:T(8,128)(2,1)}, bf16[256,1024]{1,0:T(8,128)(2,1)}, u32[]{:S(2)}, u32[]{:S(2)}) collective-permute-start(bf16[256,1024]{1,0:T(8,128)(2,1)} %get-tuple-element.60), channel_id=1, source_target_pairs={{0,4},{4,0},{1,5},{5,1},{2,6},{6,2},{3,7},{7,3}} | collective-permute-start | bytes 1572872 | tf_op jit(solution)/shard_map/ppermute | solution.py:419
  235.6 1.0 copy-start.3
  235.6 45.5 %collective-permute-start.13 = (bf16[256,1024]{1,0:T(8,128)(2,1)}, bf16[256,1024]{1,0:T(8,128)(2,1)}, u32[]{:S(2)}, u32[]{:S(2)}) collective-permute-start(bf16[256,1024]{1,0:T(8,128)(2,1)} %get-tuple-element.59), channel_id=1, source_target_pairs={{0,4},{4,0},{1,5},{5,1},{2,6},{6,2},{3,7},{7,3}} | collective-permute-start | bytes 1572872 | tf_op jit(solution)/shard_map/ppermute | solution.py:419
  252.9 1.7 copy-start.7
  252.9 44.9 %collective-permute-start.12 = (bf16[256,1536]{1,0:T(8,128)(2,1)}, bf16[256,1536]{1,0:T(8,128)(2,1)S(1)}, u32[]{:S(2)}, u32[]{:S(2)}) collective-permute-start(bf16[256,1536]{1,0:T(8,128)(2,1)} %get-tuple-element.58), channel_id=1, source_target_pairs={{0,4},{4,0},{1,5},{5,1},{2,6},{6,2},{3,7},{7,3}} | collective-permute-start | bytes 2359304 | tf_op jit(solution)/shard_map/ppermute | solution.py:419
  254.6 60.1 %collective-permute-start.11 = (bf16[256,1536]{1,0:T(8,128)(2,1)}, bf16[256,1536]{1,0:T(8,128)(2,1)S(1)}, u32[]{:S(2)}, u32[]{:S(2)}) collective-permute-start(bf16[256,1536]{1,0:T(8,128)(2,1)} %get-tuple-element.57), channel_id=1, source_target_pairs={{0,4},{4,0},{1,5},{5,1},{2,6},{6,2},{3,7},{7,3}} | collective-permute-start | bytes 2359304 | tf_op jit(solution)/shard_map/ppermute | solution.py:419
  255.6 16.0 %copy-start = (bf16[256,1024]{1,0:T(8,128)(2,1)S(1)}, bf16[256,1024]{1,0:T(8,128)(2,1)}, u32[]{:S(2)}) copy-start(bf16[256,1024]{1,0:T(8,128)(2,1)} %get-tuple-element.34.rest_0_) | copy-start | bytes 1572868
  255.6 16.0 %copy-start.1 = (bf16[256,1024]{1,0:T(8,128)(2,1)S(1)}, bf16[256,1024]{1,0:T(8,128)(2,1)}, u32[]{:S(2)}) copy-start(bf16[256,1024]{1,0:T(8,128)(2,1)} %get-tuple-element.38.rest_4_) | copy-start | bytes 1572868
  262.3 14.4 %copy-start.9 = (bf16[256,512]{1,0:T(8,128)(2,1)}, bf16[256,512]{1,0:T(8,128)(2,1)S(1)}, u32[]{:S(2)}) copy-start(bf16[256,512]{1,0:T(8,128)(2,1)S(1)} %collective-permute-done.15.r_ref) | copy-start | bytes 786436
  262.3 63.7 %collective-permute-start.10 = (bf16[256,1024]{1,0:T(8,128)(2,1)}, bf16[256,1024]{1,0:T(8,128)(2,1)}, u32[]{:S(2)}, u32[]{:S(2)}) collective-permute-start(bf16[256,1024]{1,0:T(8,128)(2,1)} %get-tuple-element.56), channel_id=1, source_target_pairs={{0,4},{4,0},{1,5},{5,1},{2,6},{6,2},{3,7},{7,3}} | collective-permute-start | bytes 1572872 | tf_op jit(solution)/shard_map/ppermute | solution.py:419
  269.9 67.4 %collective-permute-start.9 = (bf16[256,1024]{1,0:T(8,128)(2,1)}, bf16[256,1024]{1,0:T(8,128)(2,1)}, u32[]{:S(2)}, u32[]{:S(2)}) collective-permute-start(bf16[256,1024]{1,0:T(8,128)(2,1)} %get-tuple-element.55), channel_id=1, source_target_pairs={{0,4},{4,0},{1,5},{5,1},{2,6},{6,2},{3,7},{7,3}} | collective-permute-start | bytes 1572872 | tf_op jit(solution)/shard_map/ppermute | solution.py:419
  281.1 59.4 %collective-permute-start.8 = (bf16[256,512]{1,0:T(8,128)(2,1)}, bf16[256,512]{1,0:T(8,128)(2,1)S(1)}, u32[]{:S(2)}, u32[]{:S(2)}) collective-permute-start(bf16[256,512]{1,0:T(8,128)(2,1)} %get-tuple-element.54), channel_id=1, source_target_pairs={{0,4},{4,0},{1,5},{5,1},{2,6},{6,2},{3,7},{7,3}} | collective-permute-start | bytes 786440 | tf_op jit(solution)/shard_map/ppermute | solution.py:419
  (4 other events, 3.5 us)

commit v2 on v1

v2 whole, which is shorter than its diff:
```python
import jax
import jax.numpy as jnp
from jax import lax
from jax.experimental import pallas as pl
from jax.experimental.pallas import tpu as pltpu
from jax.sharding import PartitionSpec as P


F32 = jnp.float32
BF16 = jnp.bfloat16
HEAD = 128
LANES = 128
VMEM_BYTES = 60 * 1024 * 1024
ROWS = 128
CHUNKS = ((1024, 3072), (1024, 3072), (1024, 3072), (1024, 2048, 512, 512))
PLAN = (("make", 0, 0, 2), ("make", 1, 0, 2), ("own", 0, 0, 2), ("make", 2, 0, 2), ("own", 1, 0, 2), ("make", 3, 0, 4), ("own", 2, 0, 2), ("own", 3, 0, 1), ("own", 3, 1, 2), ("own", 3, 2, 3), ("own", 3, 3, 4))


def any_spec():
    return pl.BlockSpec(memory_space=pl.ANY)


def rope_head(vec, cos_t, sin_t):
    vec = vec.astype(BF16).astype(F32)
    return (vec * cos_t + pltpu.roll(vec, HEAD // 2, 1) * sin_t).astype(BF16)


def front(group, with_kv, x_in, gain, pos2, inv_freq, w_q, w_k, w_v):
    d_model = x_in.shape[1]
    kv_cols = w_k.shape[1]
    q_cols = w_q.shape[1]
    bn = kv_cols
    nq = q_cols // bn
    slots = 4
    xr = 64
    rows = 2 * ROWS if with_kv else ROWS
    nx = rows // xr
    step = 32
    lead = 2 if with_kv else 0

    def kernel(x_hbm, gain_ref, pos_ref, freq_ref, wq_hbm, *rest):
        if with_kv:
            wk_hbm, wv_hbm, q_hbm, kv_ref, r1, r2, r3 = rest[:7]
            s_sem, r_sem = rest[-2:]
            rest = rest[7:-2]
            me = lax.axis_index('cp')
            core, across = lax.bitwise_xor(me, 1), lax.bitwise_xor(me, 2)
            barrier = pltpu.get_barrier_semaphore()
            for peer in (core, across):
                pl.semaphore_signal(barrier, inc=1, device_id={'cp': peer}, device_id_type=pl.DeviceIdType.MESH)
        else:
            q_hbm = rest[0]
            rest = rest[1:]
        x_buf, h_ref, ring, q_buf, cos_ref, sin_ref, freq2_ref, x_sem, w_sem, q_sem = rest
        x_copies = [pltpu.make_async_copy(x_hbm.at[pl.ds(group * ROWS + i * xr, xr)], x_buf.at[pl.ds(i * xr, xr)], x_sem.at[i]) for i in range(nx)]
        for copy in x_copies:
            copy.start()

        def q_load(b):
            slot = lax.rem(b + lead, slots)
            return pltpu.make_async_copy(wq_hbm.at[:, pl.ds(pl.multiple_of(b * bn, bn), bn)], ring.at[slot], w_sem.at[slot])

        kv_loads = [pltpu.make_async_copy(w_hbm, ring.at[n], w_sem.at[n]) for n, w_hbm in enumerate((wk_hbm, wv_hbm))] if with_kv else []
        for load in kv_loads:
            load.start()
        for b in range(slots - lead):
            q_load(b).start()

        half_dim = HEAD // 2
        freq2_ref[:, :half_dim] = freq_ref[...]
        freq2_ref[:, half_dim:] = freq_ref[...]
        sign = jnp.where(lax.broadcasted_iota(jnp.int32, (LANES, HEAD), 1) < half_dim, -1.0, 1.0)
        for b in range(rows // LANES):
            pos_row = pos_ref[group + b:group + b + 1, :].astype(F32)
            angle = jnp.transpose(jnp.broadcast_to(pos_row, (LANES, LANES))) * freq2_ref[...]
            cos_ref[b * LANES:(b + 1) * LANES, :] = jnp.cos(angle)
            sin_ref[b * LANES:(b + 1) * LANES, :] = jnp.sin(angle) * sign

        def norm(r, carry):
            at = pl.ds(pl.multiple_of(r * step, step), step)
            total = jnp.zeros((step, LANES), F32)
            for c in range(d_model // LANES):
                v = x_buf[at, c * LANES:(c + 1) * LANES].astype(F32)
                total += v * v
            inv = lax.rsqrt(jnp.sum(total, axis=1, keepdims=True) / d_model + 1e-5)
            for c in range(d_model // LANES):
                cols = slice(c * LANES, (c + 1) * LANES)
                h_ref[at, cols] = (x_buf[at, cols].astype(F32) * inv * gain_ref[:, cols]).astype(BF16)
            return carry

        def norm_part(i, carry):
            pltpu.make_async_copy(x_hbm.at[pl.ds(group * ROWS + i * xr, xr)], x_buf.at[pl.ds(i * xr, xr)], x_sem.at[i]).wait()
            return lax.fori_loop(i * (xr // step), (i + 1) * (xr // step), norm, carry)

        lax.fori_loop(0, nx, norm_part, 0)

        if with_kv:
            kv_loads[0].wait()
            acc = jnp.dot(h_ref[...], ring[0], preferred_element_type=F32)
            for g in range(bn // HEAD):
                cols = slice(g * HEAD, (g + 1) * HEAD)
                kv_ref[:, cols] = rope_head(acc[:, cols], cos_ref[...], sin_ref[...])
            q_load(slots - 2).start()
            kv_loads[1].wait()
            kv_ref[:, kv_cols:] = jnp.dot(h_ref[...], ring[1], preferred_element_type=F32).astype(BF16)
            q_load(slots - 1).start()
            pl.semaphore_wait(barrier, 2)
            sends = []
            for n, (dst, peer) in enumerate(((r2, across), (r1, core))):
                sends.append(pltpu.make_async_remote_copy(src_ref=kv_ref, dst_ref=dst, send_sem=s_sem.at[n], recv_sem=r_sem.at[n], device_id={'cp': peer}, device_id_type=pl.DeviceIdType.MESH))
                sends[-1].start()
            forward = pltpu.make_async_remote_copy(src_ref=r2, dst_ref=r3, send_sem=s_sem.at[2], recv_sem=r_sem.at[2], device_id={'cp': core}, device_id_type=pl.DeviceIdType.MESH)

        def q_store(b):
            cols = pl.ds(pl.multiple_of(b * bn, bn), bn)
            return pltpu.make_async_copy(q_buf.at[:, cols], q_hbm.at[:, cols], q_sem.at[b])

        def q_block(b, carry):
            slot = lax.rem(b + lead, slots)
            q_load(b).wait()
            acc = jnp.dot(h_ref[:ROWS], ring[slot], preferred_element_type=F32)

            @pl.when(b + slots < nq)
            def _():
                q_load(b + slots).start()

            for g in range(bn // HEAD):
                at = pl.ds(pl.multiple_of(b * bn + g * HEAD, HEAD), HEAD)
                q_buf[:, at] = rope_head(acc[:, g * HEAD:(g + 1) * HEAD], cos_ref[:ROWS], sin_ref[:ROWS])
            q_store(b).start()
            if with_kv:
                @pl.when(b == nq - 2)
                def _():
                    sends[0].wait_recv()
                    forward.start()

            return carry

        lax.fori_loop(0, nq, q_block, 0)
        for b in range(nq):
            q_store(b).wait()
        if with_kv:
            sends[0].wait_send()
            sends[1].wait()
            forward.wait()

    whole = lambda arr: pl.BlockSpec(arr.shape, lambda i: (0, 0))
    kv_shape = jax.ShapeDtypeStruct((rows, 2 * kv_cols), BF16)
    kv_out = [kv_shape] * 4 if with_kv else []
    return pl.pallas_call(
        kernel,
        grid=(1,),
        in_specs=[any_spec(), whole(gain), whole(pos2), whole(inv_freq), any_spec()] + [any_spec()] * lead,
        out_specs=[any_spec()] + ([pl.BlockSpec(kv_shape.shape, lambda i: (0, 0)), any_spec(), any_spec(), any_spec()] if with_kv else []),
        out_shape=[jax.ShapeDtypeStruct((ROWS, q_cols), BF16)] + kv_out,
        scratch_shapes=[
            pltpu.VMEM((rows, d_model), BF16),
            pltpu.VMEM((rows, d_model), BF16),
            pltpu.VMEM((slots, d_model, bn), BF16),
            pltpu.VMEM((ROWS, q_cols), BF16),
            pltpu.VMEM((rows, HEAD), F32),
            pltpu.VMEM((rows, HEAD), F32),
            pltpu.VMEM((1, HEAD), F32),
            pltpu.SemaphoreType.DMA((nx,)),
            pltpu.SemaphoreType.DMA((slots,)),
            pltpu.SemaphoreType.DMA((nq,)),
        ] + ([pltpu.SemaphoreType.DMA((3,))] * 2 if with_kv else []),
        compiler_params=pltpu.CompilerParams(vmem_limit_bytes=VMEM_BYTES, collective_id=group, has_side_effects=True) if with_kv else pltpu.CompilerParams(vmem_limit_bytes=VMEM_BYTES),
        cost_estimate=pl.CostEstimate(flops=2 * rows * d_model * (2 * kv_cols + q_cols), bytes_accessed=2 * d_model * (rows + q_cols), transcendentals=0),
        name="front",
    )(x_in, gain, pos2, inv_freq, w_q, *((w_k, w_v) if with_kv else ()))


def attend_send(row_group, cp_size, pos, pos2, q, kv_parts, w_o, cols):
    half = row_group // 2
    qb = kb = ROWS
    rows = 2 * ROWS
    kv_heads = kv_parts[0].shape[1] // (2 * HEAD)
    group = q.shape[1] // (kv_heads * HEAD)
    keys = cp_size * rows * (1 + half)
    scale = HEAD ** -0.5
    parts = len(kv_parts)
    k_dim = q.shape[1]
    half_cols = w_o.shape[1] // 2
    bn = 512

    def kernel(pos_ref, pos2_ref, q_hbm, w_hbm, *rest):
        kv_hbm = rest[:parts]
        o_ref, part_ref, kv_all, q_buf, w_buf, s_ref, p_ref, m_ref, l_ref, acc_ref, kv_sem, q_sem, w_sem = rest[parts:]
        dev, tp = lax.axis_index('cp'), lax.axis_index('tp')
        copies = []
        for n in range(parts):
            owner = lax.bitwise_xor(dev, n % cp_size)
            piece = owner if n < cp_size else 2 * cp_size - 1 - owner
            copies.append(pltpu.make_async_copy(kv_hbm[n], kv_all.at[pl.ds(pl.multiple_of(piece * rows, rows), rows)], kv_sem.at[n]))
            copies[-1].start()

        def q_copy(n):
            at = pl.ds(pl.multiple_of(n * group * HEAD, group * HEAD), group * HEAD)
            return pltpu.make_async_copy(q_hbm.at[:, at], q_buf.at[:, at], q_sem.at[n])

        for n in range(kv_heads):
            q_copy(n).start()

        def w_copy(j):
            at = pl.ds(pl.multiple_of((1 - tp) * half_cols + j * bn, bn), bn)
            return pltpu.make_async_copy(w_hbm.at[:, at], w_buf.at[j], w_sem.at[j])

        for j in range(cols // bn):
            w_copy(j).start()
        for copy in copies:
            copy.wait()
        piece = dev if half == 0 else 2 * cp_size - 1 - dev
        lane = lax.broadcasted_iota(jnp.int32, (qb, LANES), 1)
        t0 = piece * rows + (row_group % 2) * qb
        p0 = pos_ref[row_group * qb]
        t_idx = t0 + lax.broadcasted_iota(jnp.int32, (qb, LANES), 0)
        pos_row = pos2_ref[row_group:row_group + 1, :].astype(F32)
        first = t_idx - jnp.transpose(jnp.broadcast_to(pos_row, (qb, LANES))).astype(jnp.int32)

        def kv_head(n, carry):
            q_copy(n).wait()

            def head_cols(g):
                return pl.ds(pl.multiple_of((n * group + g) * HEAD, HEAD), HEAD)

            k_cols = pl.ds(pl.multiple_of(n * HEAD, HEAD), HEAD)
            v_cols = pl.ds(pl.multiple_of((kv_heads + n) * HEAD, HEAD), HEAD)
            q_stack = jnp.concatenate([q_buf[:, head_cols(g)] for g in range(group)], axis=0)

            @pl.when(p0 <= kb)
            def _():
                w0 = pl.multiple_of(jnp.maximum(t0 - kb, 0), kb)
                at = pl.ds(w0, 2 * kb)
                s_ref[...] = lax.dot_general(q_stack, kv_all[at, k_cols], (((1,), (1,)), ((), ())), preferred_element_type=F32)
                u = w0 + lane
                visible = jnp.concatenate([(u >= first) & (u <= t_idx), (u + kb >= first) & (u + kb <= t_idx)], axis=1)
                for g in range(group):
                    at_g = slice(g * qb, (g + 1) * qb)
                    s = jnp.where(visible, s_ref[at_g] * scale, -1e30)
                    s_ref[at_g] = s
                    m_ref[g] = jnp.broadcast_to(jnp.max(s, axis=1, keepdims=True), (qb, LANES))
                for g in range(group):
                    at_g = slice(g * qb, (g + 1) * qb)
                    m = m_ref[g]
                    e = jnp.exp(s_ref[at_g] - jnp.concatenate([m, m], axis=1))
                    s_ref[at_g] = e
                    l_ref[g] = 1.0 / jnp.broadcast_to(jnp.sum(e, axis=1, keepdims=True), (qb, LANES))
                for g in range(group):
                    at_g = slice(g * qb, (g + 1) * qb)
                    inv = l_ref[g]
                    p_ref[at_g] = (s_ref[at_g] * jnp.concatenate([inv, inv], axis=1)).astype(BF16)
                o = jnp.dot(p_ref[...], kv_all[at, v_cols], preferred_element_type=F32).astype(BF16)
                for g in range(group):
                    o_ref[:, head_cols(g)] = o[g * qb:(g + 1) * qb]

            @pl.when(p0 > kb)
            def _():
                kb0 = lax.div(t0 - p0, kb)
                kb1 = lax.div(t0, kb) + 1
                m_ref[...] = jnp.full_like(m_ref, -1e30)
                l_ref[...] = jnp.zeros_like(l_ref)
                acc_ref[...] = jnp.zeros_like(acc_ref)

                def block(j):
                    at = pl.ds(pl.multiple_of(j * kb, kb), kb)
                    u = j * kb + lane
                    s_ref[:, :kb] = lax.dot_general(q_stack, kv_all[at, k_cols], (((1,), (1,)), ((), ())), preferred_element_type=F32)
                    return at, (u >= first) & (u <= t_idx)

                def head_scores(g, visible):
                    at_g = pl.ds(pl.multiple_of(g * qb, qb), qb)
                    return at_g, jnp.where(visible, s_ref[at_g, :kb] * scale, -1e30)

                def stats(j, carry):
                    _, visible = block(j)

                    def one(g, inner):
                        _, s = head_scores(g, visible)
                        m_old = m_ref[g]
                        m_new = jnp.maximum(m_old, jnp.max(s, axis=1, keepdims=True))
                        l_ref[g] = l_ref[g] * jnp.exp(m_old - m_new) + jnp.sum(jnp.exp(s - m_new), axis=1, keepdims=True)
                        m_ref[g] = m_new
                        return inner

                    return lax.fori_loop(0, group, one, carry)

                def weigh(j, carry):
                    at, visible = block(j)

                    def one(g, inner):
                        at_g, s = head_scores(g, visible)
                        p_ref[at_g, :kb] = (jnp.exp(s - m_ref[g]) / l_ref[g]).astype(BF16)
                        return inner

                    lax.fori_loop(0, group, one, 0)
                    acc_ref[...] += jnp.dot(p_ref[:, :kb], kv_all[at, v_cols], preferred_element_type=F32)
                    return carry

                lax.fori_loop(kb0, kb1, stats, 0)
                lax.fori_loop(kb0, kb1, weigh, 0)
                for g in range(group):
                    o_ref[:, head_cols(g)] = acc_ref[g * qb:(g + 1) * qb].astype(BF16)

            return carry

        lax.fori_loop(0, kv_heads, kv_head, 0)

        def product(j, carry):
            w_copy(j).wait()
            part_ref[:, pl.ds(pl.multiple_of(j * bn, bn), bn)] = jnp.dot(o_ref[...], w_buf[j], preferred_element_type=F32)
            return carry

        lax.fori_loop(0, cols // bn, product, 0)

    whole = lambda shape: pl.BlockSpec(shape, lambda i, *_: (0, 0))
    return pl.pallas_call(
        kernel,
        grid_spec=pltpu.PrefetchScalarGridSpec(
            num_scalar_prefetch=1,
            grid=(1,),
            in_specs=[whole(pos2.shape), any_spec(), any_spec()] + [any_spec()] * parts,
            out_specs=[whole(q.shape), whole((ROWS, cols))],
            scratch_shapes=[
                pltpu.VMEM((keys, kv_parts[0].shape[1]), BF16),
                pltpu.VMEM(q.shape, BF16),
                pltpu.VMEM((cols // bn, k_dim, bn), BF16),
                pltpu.VMEM((group * qb, 2 * kb), F32),
                pltpu.VMEM((group * qb, 2 * kb), BF16),
                pltpu.VMEM((group, qb, LANES), F32),
                pltpu.VMEM((group, qb, LANES), F32),
                pltpu.VMEM((group * qb, HEAD), F32),
                pltpu.SemaphoreType.DMA((parts,)),
                pltpu.SemaphoreType.DMA((kv_heads,)),
                pltpu.SemaphoreType.DMA((cols // bn,)),
            ],
        ),
        out_shape=[jax.ShapeDtypeStruct(q.shape, BF16), jax.ShapeDtypeStruct((ROWS, cols), F32)],
        compiler_params=pltpu.CompilerParams(vmem_limit_bytes=VMEM_BYTES),
        cost_estimate=pl.CostEstimate(flops=4 * ROWS * k_dim * 512 + 2 * ROWS * k_dim * cols, bytes_accessed=2 * k_dim * cols, transcendentals=0),
        name="attend_send",
    )(pos, pos2, q, w_o, *kv_parts)


def out_send(tp_me, o, w_o, col0, cols):
    rows, k_dim = o.shape
    bn = 512
    own_blocks = w_o.shape[1] // 2 // bn

    def kernel(tp_ref, o_ref, w_ref, part_ref):
        part_ref[...] = jnp.dot(o_ref[...], w_ref[...], preferred_element_type=F32)

    return pl.pallas_call(
        kernel,
        grid_spec=pltpu.PrefetchScalarGridSpec(
            num_scalar_prefetch=1,
            grid=(cols // bn,),
            in_specs=[pl.BlockSpec((rows, k_dim), lambda i, tp: (0, 0)), pl.BlockSpec((k_dim, bn), lambda i, tp: (0, (1 - tp[0]) * own_blocks + col0 // bn + i))],
            out_specs=pl.BlockSpec((rows, bn), lambda i, tp: (0, i)),
        ),
        out_shape=jax.ShapeDtypeStruct((rows, cols), F32),
        compiler_params=pltpu.CompilerParams(vmem_limit_bytes=VMEM_BYTES),
        cost_estimate=pl.CostEstimate(flops=2 * rows * k_dim * cols, bytes_accessed=2 * k_dim * (rows + cols), transcendentals=0),
        name="out_send",
    )(tp_me, o, w_o)


def out_own(row_group, tp_me, o, w_o, x_in, recvs, y_buf, col0):
    rows, k_dim = o.shape
    bn = 512
    own_blocks = w_o.shape[1] // 2 // bn
    starts = [sum(r.shape[1] for r in recvs[:n]) // bn for n in range(len(recvs) + 1)]
    cols = starts[-1] * bn

    def col(i, tp):
        return tp[0] * own_blocks + col0 // bn + i

    def kernel(tp_ref, o_ref, w_ref, x_ref, *rest):
        y_ref, c_ref = rest[-2:]
        acc = jnp.dot(o_ref[...], w_ref[...], preferred_element_type=F32)
        step = pl.program_id(0)
        for n in range(len(recvs)):
            @pl.when((step >= starts[n]) & (step < starts[n + 1]))
            def _():
                out = (x_ref[...].astype(F32) + (acc + rest[n][...])).astype(BF16)
                y_ref[...] = out
                c_ref[...] = out

    def recv_spec(n):
        return pl.BlockSpec((rows, bn), lambda i, tp: (0, jnp.clip(i - starts[n], 0, starts[n + 1] - starts[n] - 1)))

    ins = [o, w_o, x_in] + list(recvs) + ([] if y_buf is None else [y_buf])
    wide = pl.BlockSpec((rows, bn), lambda i, tp: (row_group, col(i, tp)))
    narrow = pl.BlockSpec((rows, bn), lambda i, tp: (0, i))
    return pl.pallas_call(
        kernel,
        grid_spec=pltpu.PrefetchScalarGridSpec(
            num_scalar_prefetch=1,
            grid=(cols // bn,),
            in_specs=[pl.BlockSpec((rows, k_dim), lambda i, tp: (0, 0)), pl.BlockSpec((k_dim, bn), lambda i, tp: (0, col(i, tp))), wide] + [recv_spec(n) for n in range(len(recvs))] + ([] if y_buf is None else [any_spec()]),
            out_specs=[wide, narrow],
        ),
        out_shape=[jax.ShapeDtypeStruct(x_in.shape, BF16), jax.ShapeDtypeStruct((rows, cols), BF16)],
        input_output_aliases={} if y_buf is None else {len(ins): 0},
        compiler_params=pltpu.CompilerParams(vmem_limit_bytes=VMEM_BYTES),
        cost_estimate=pl.CostEstimate(flops=2 * rows * k_dim * cols, bytes_accessed=2 * k_dim * (rows + cols), transcendentals=0),
        name="out_own",
    )(tp_me, *ins)


def place(row_group, tp_me, recv, y_buf, col0):
    rows, cols = recv.shape
    bn = 512
    own_blocks = y_buf.shape[1] // 2 // bn

    def kernel(tp_ref, r_ref, y_in, y_ref):
        y_ref[...] = r_ref[...]

    return pl.pallas_call(
        kernel,
        grid_spec=pltpu.PrefetchScalarGridSpec(
            num_scalar_prefetch=1,
            grid=(cols // bn,),
            in_specs=[pl.BlockSpec((rows, bn), lambda i, tp: (0, i)), any_spec()],
            out_specs=pl.BlockSpec((rows, bn), lambda i, tp: (row_group, (1 - tp[0]) * own_blocks + col0 // bn + i)),
        ),
        out_shape=jax.ShapeDtypeStruct(y_buf.shape, BF16),
        input_output_aliases={2: 0},
        cost_estimate=pl.CostEstimate(flops=rows * cols, bytes_accessed=4 * rows * cols, transcendentals=0),
        name="place",
    )(tp_me, recv, y_buf)


def solution(mesh):
    cp_size = mesh.shape['cp']
    tp_size = mesh.shape['tp']
    swap_tp = [(j, tp_size - 1 - j) for j in range(tp_size)]

    def local_step(x_in, doc_id, pos_in_doc, norm_gain, w_q, w_k, w_v, w_o, inv_freq):
        local_rows, d_model = x_in.shape
        kv_cols = w_k.shape[1]
        groups = local_rows // ROWS
        tp_me = lax.axis_index('tp').astype(jnp.int32).reshape(1)
        gain = norm_gain.reshape(1, d_model)
        pos2 = pos_in_doc.reshape(groups, LANES)
        freq = inv_freq.reshape(1, HEAD // 2)
        kv_parts = []
        attn, sent, results = {}, {}, []
        y_buf = None

        def swap(value):
            return lax.ppermute(value, 'tp', swap_tp)

        def make(r):
            q, *parts = front(r, r % 2 == 0, x_in, gain, pos2, freq, w_q, w_k, w_v)
            kv_parts.extend(parts)
            sizes = CHUNKS[r]
            attn[r], part = attend_send(r, cp_size, pos_in_doc, pos2, q, kv_parts, w_o, sizes[0])
            sent[r] = [swap(part)]
            for c in range(1, len(sizes)):
                part = out_send(tp_me, attn[r], w_o, sum(sizes[:c]), sizes[c])
                sent[r].append(swap(part))

        for kind, r, c0, c1 in PLAN:
            if kind == "make":
                make(r)
                continue
            col0 = sum(CHUNKS[r][:c0])
            y_buf, block = out_own(r, tp_me, attn[r], w_o, x_in, sent[r][c0:c1], y_buf, col0)
            results.append((r, col0, swap(block)))
        for r, col0, block in results:
            y_buf = place(r, tp_me, block, y_buf, col0)
        kv_all = jnp.concatenate([kv_parts[0], kv_parts[cp_size]], axis=0)
        k_out = kv_all[:, :kv_cols].reshape(local_rows, kv_cols // HEAD, HEAD)
        v_out = kv_all[:, kv_cols:].reshape(local_rows, kv_cols // HEAD, HEAD)
        return y_buf, k_out, v_out

    row_spec = P(('dp', 'cp'))
    in_specs = (P(('dp', 'cp'), None), row_spec, row_spec, P(), P(None, 'tp'), P(None, 'tp'), P(None, 'tp'), P('tp', None), P())
    out_specs = (P(('dp', 'cp'), None), P(('dp', 'cp'), 'tp', None), P(('dp', 'cp'), 'tp', None))

    return jax.shard_map(local_step, mesh=mesh, in_specs=in_specs, out_specs=out_specs, check_vma=False)
```

time: 344 us -> 373 us (1.084)
  Pallas kernels: 214 us -> 304 us
  waiting for transfers between devices: 102 us -> 42.4 us
    ppermute x16 -> x17, waiting for transfers between devices: 102 us -> 42.4 us  [swap(): return lax.ppermute(value, 'tp', swap_tp)]
    pallas_call x2 -> x4, Pallas kernels: 74.3 us -> 115 us  [front(): pl.pallas_call(kernel, grid=(1,), in_specs=[any_spec(), whole(gain), whol...]
    pallas_call x8 -> x7, Pallas kernels: 55.2 us -> 70.5 us  [out_own(): pl.pallas_call(kernel, grid_spec=pltpu.PrefetchScalarGridSpec(num_scalar_...]
    pallas_call x2 -> x4, Pallas kernels: 29.7 us -> 43.4 us  [attend_send(): pl.pallas_call(kernel, grid_spec=pltpu.PrefetchScalarGridSpec(num_scalar_...]
    pallas_call x6, Pallas kernels: 38.6 us -> 51.9 us  [out_send(): pl.pallas_call(kernel, grid_spec=pltpu.PrefetchScalarGridSpec(num_scalar_...]
    pallas_call x8 -> x7, Pallas kernels: 16.1 us -> 23.4 us  [place(): pl.pallas_call(kernel, grid_spec=pltpu.PrefetchScalarGridSpec(num_scalar_...]
    ppermute x16 -> x17, starting transfers between devices: 20.6 us -> 17.4 us  [swap(): return lax.ppermute(value, 'tp', swap_tp)]
  transfers between devices with their start and end apart: 16 -> 17, of which waited for: 9 -> 2; matrix products, arithmetic and copies ran while one was open for 1% -> 1% of each run, Pallas kernels for 45% -> 66%
where the time goes in v2:
time: 373 us; the launch traced here: 371 us
  Pallas kernels  304 us (82%)
  waiting for transfers between devices  42.4 us (11%)
  starting transfers between devices  17.4 us (5%)
  local copies, waits for them, and re-layouts  7.01 us (2%)
    pallas_call x4, Pallas kernels, front(): pl.pallas_call(kernel, grid=(1,), in_specs=[any_spec(), whole(gain), whol...  115 us
    pallas_call x7, Pallas kernels, out_own(): pl.pallas_call(kernel, grid_spec=pltpu.PrefetchScalarGridSpec(num_scalar_...  70.5 us
    pallas_call x6, Pallas kernels, out_send(): pl.pallas_call(kernel, grid_spec=pltpu.PrefetchScalarGridSpec(num_scalar_...  51.9 us
    pallas_call x4, Pallas kernels, attend_send(): pl.pallas_call(kernel, grid_spec=pltpu.PrefetchScalarGridSpec(num_scalar_...  43.4 us
    ppermute x17, waiting for transfers between devices, swap(): return lax.ppermute(value, 'tp', swap_tp)  42.4 us
    pallas_call x7, Pallas kernels, place(): pl.pallas_call(kernel, grid_spec=pltpu.PrefetchScalarGridSpec(num_scalar_...  23.4 us
    ppermute x17, starting transfers between devices, swap(): return lax.ppermute(value, 'tp', swap_tp)  17.4 us
  transfers between devices with their start and end apart: 17, of which 2 were waited for; matrix products, arithmetic and copies ran while one was open for 1% of the time, Pallas kernels for 66%

profile of v2, /device:TPU:0, one launch (start us, length us, event | category | flops | bytes accessed | tf_op | source)
XLA Modules:
  0.0 371.4 jit_solution(2099227499042294850)
XLA Ops:
  0.6 33.9 %front.5 = (bf16[128,4096]{1,0:T(8,128)(2,1)}, bf16[256,1024]{1,0:T(8,128)(2,1)}, bf16[256,1024]{1,0:T(8,128)(2,1)}, bf16[256,1024]{1,0:T(8,128)(2,1)}, bf16[256,1024]{1,0:T(8,128)(2,1)}) custom-call(bf16[512,8192]{1,0:T(8,128)(2,1)} %x_ref.13, f32[1,8192]{1,0:T(1,128)} %bitcast.4, s32[4,128]{1,0:T(4,128)} %bitcast.8, f32[1,64]{1,0:T(1,128)} %bitcast.16, ...), custom_call_target="tpu_custom_call" | custom-call | flops 21474836480 | bytes 71303168 | tf_op jit(solution)/shard_map/front/pallas_call | solution.py:150
  34.5 10.5 %attend_send.7 = (bf16[128,4096]{1,0:T(8,128)(2,1)}, f32[128,1024]{1,0:T(8,128)}) custom-call(s32[512]{0:T(512)} %pos_ref.7, s32[4,128]{1,0:T(4,128)} %bitcast.9, bf16[128,4096]{1,0:T(8,128)(2,1)} %get-tuple-element.50.q_hbm, bf16[4096,8192]{1,0:T(8,128)(2,1)} %w_ref.25, bf16[256,1024]{1,0:T(8,128)(2,1)} %get-tuple-element.35.rest_0_, ...), custom_call_target="tpu_custom_call" | custom-call | flops 2147483648 | bytes 8388608 | tf_op jit(solution)/shard_map/attend_send/pallas_call | solution.py:317
  45.0 11.8 %out_send.11 = f32[128,3072]{1,0:T(8,128)} custom-call(s32[1]{0:T(128)} %bitcast.tp_ref, bf16[128,4096]{1,0:T(8,128)(2,1)} %get-tuple-element.51.o_ref, bf16[4096,8192]{1,0:T(8,128)(2,1)} %w_ref.25), custom_call_target="tpu_custom_call" | custom-call | flops 3221225472 | bytes 26214400 | tf_op jit(solution)/shard_map/out_send/pallas_call | solution.py:353
  58.8 24.6 %front.7.q_hbm = bf16[128,4096]{1,0:T(8,128)(2,1)} custom-call(bf16[512,8192]{1,0:T(8,128)(2,1)} %x_ref.13, f32[1,8192]{1,0:T(1,128)} %bitcast.5, s32[4,128]{1,0:T(4,128)} %bitcast.10, f32[1,64]{1,0:T(1,128)} %bitcast.17, bf16[8192,4096]{1,0:T(8,128)(2,1)} %wq_hbm.7), custom_call_target="tpu_custom_call" | custom-call | flops 10737418240 | bytes 69206016 | tf_op jit(solution)/shard_map/front/pallas_call | solution.py:150
  83.4 10.5 %attend_send.6 = (bf16[128,4096]{1,0:T(8,128)(2,1)}, f32[128,1024]{1,0:T(8,128)}) custom-call(s32[512]{0:T(512)} %pos_ref.7, s32[4,128]{1,0:T(4,128)} %bitcast.11, bf16[128,4096]{1,0:T(8,128)(2,1)} %front.7.q_hbm, bf16[4096,8192]{1,0:T(8,128)(2,1)} %w_ref.25, bf16[256,1024]{1,0:T(8,128)(2,1)} %get-tuple-element.35.rest_0_, ...), custom_call_target="tpu_custom_call" | custom-call | flops 2147483648 | bytes 8388608 | tf_op jit(solution)/shard_map/attend_send/pallas_call | solution.py:317
  94.0 11.8 %out_send.10 = f32[128,3072]{1,0:T(8,128)} custom-call(s32[1]{0:T(128)} %bitcast.tp_ref, bf16[128,4096]{1,0:T(8,128)(2,1)} %get-tuple-element.48.o_ref, bf16[4096,8192]{1,0:T(8,128)(2,1)} %w_ref.25), custom_call_target="tpu_custom_call" | custom-call | flops 3221225472 | bytes 26214400 | tf_op jit(solution)/shard_map/out_send/pallas_call | solution.py:353
  107.8 31.8 %front.6 = (bf16[128,4096]{1,0:T(8,128)(2,1)}, bf16[256,1024]{1,0:T(8,128)(2,1)}, bf16[256,1024]{1,0:T(8,128)(2,1)}, bf16[256,1024]{1,0:T(8,128)(2,1)}, bf16[256,1024]{1,0:T(8,128)(2,1)}) custom-call(bf16[512,8192]{1,0:T(8,128)(2,1)} %x_ref.13, f32[1,8192]{1,0:T(1,128)} %bitcast.6, s32[4,128]{1,0:T(4,128)} %bitcast.12, f32[1,64]{1,0:T(1,128)} %bitcast.18, ...), custom_call_target="tpu_custom_call" | custom-call | flops 21474836480 | bytes 71303168 | tf_op jit(solution)/shard_map/front/pallas_call | solution.py:150
  139.6 11.2 %attend_send.5 = (bf16[128,4096]{1,0:T(8,128)(2,1)}, f32[128,1024]{1,0:T(8,128)}) custom-call(s32[512]{0:T(512)} %pos_ref.7, s32[4,128]{1,0:T(4,128)} %bitcast.13, bf16[128,4096]{1,0:T(8,128)(2,1)} %get-tuple-element.45.q_hbm, bf16[4096,8192]{1,0:T(8,128)(2,1)} %w_ref.25, bf16[256,1024]{1,0:T(8,128)(2,1)} %get-tuple-element.35.rest_0_, ...), custom_call_target="tpu_custom_call" | custom-call | flops 2147483648 | bytes 8388608 | tf_op jit(solution)/shard_map/attend_send/pallas_call | solution.py:317
  150.8 11.8 %out_send.9 = f32[128,3072]{1,0:T(8,128)} custom-call(s32[1]{0:T(128)} %bitcast.tp_ref, bf16[128,4096]{1,0:T(8,128)(2,1)} %get-tuple-element.46.o_ref, bf16[4096,8192]{1,0:T(8,128)(2,1)} %w_ref.25), custom_call_target="tpu_custom_call" | custom-call | flops 3221225472 | bytes 26214400 | tf_op jit(solution)/shard_map/out_send/pallas_call | solution.py:353
  164.1 24.4 %front.4.q_hbm = bf16[128,4096]{1,0:T(8,128)(2,1)} custom-call(bf16[512,8192]{1,0:T(8,128)(2,1)} %x_ref.13, f32[1,8192]{1,0:T(1,128)} %bitcast.7, s32[4,128]{1,0:T(4,128)} %bitcast.14, f32[1,64]{1,0:T(1,128)} %bitcast.19, bf16[8192,4096]{1,0:T(8,128)(2,1)} %wq_hbm.7), custom_call_target="tpu_custom_call" | custom-call | flops 10737418240 | bytes 69206016 | tf_op jit(solution)/shard_map/front/pallas_call | solution.py:150
  188.5 11.2 %attend_send.4 = (bf16[128,4096]{1,0:T(8,128)(2,1)}, f32[128,1024]{1,0:T(8,128)}) custom-call(s32[512]{0:T(512)} %pos_ref.7, s32[4,128]{1,0:T(4,128)} %bitcast.15, bf16[128,4096]{1,0:T(8,128)(2,1)} %front.4.q_hbm, bf16[4096,8192]{1,0:T(8,128)(2,1)} %w_ref.25, bf16[256,1024]{1,0:T(8,128)(2,1)} %get-tuple-element.35.rest_0_, ...), custom_call_target="tpu_custom_call" | custom-call | flops 2147483648 | bytes 8388608 | tf_op jit(solution)/shard_map/attend_send/pallas_call | solution.py:317
  199.7 8.6 %out_send.8 = f32[128,2048]{1,0:T(8,128)} custom-call(s32[1]{0:T(128)} %bitcast.tp_ref, bf16[128,4096]{1,0:T(8,128)(2,1)} %get-tuple-element.43.o_ref, bf16[4096,8192]{1,0:T(8,128)(2,1)} %w_ref.25), custom_call_target="tpu_custom_call" | custom-call | flops 2147483648 | bytes 17825792 | tf_op jit(solution)/shard_map/out_send/pallas_call | solution.py:353
  210.3 15.7 %out_own.7 = (bf16[512,8192]{1,0:T(8,128)(2,1)}, bf16[128,4096]{1,0:T(8,128)(2,1)}) custom-call(s32[1]{0:T(128)} %bitcast.tp_ref, bf16[128,4096]{1,0:T(8,128)(2,1)} %get-tuple-element.51.o_ref, bf16[4096,8192]{1,0:T(8,128)(2,1)} %w_ref.25, bf16[512,8192]{1,0:T(8,128)(2,1)} %x_ref.13, f32[128,1024]{1,0:T(8,128)} %collective-permute-done.8.rest_0_, ...), custom_call_target="tpu_custom_call" | custom-call | flops 4294967296 | bytes 34603008 | tf_op jit(solution)/shard_map/out_own/pallas_call | solution.py:395
  228.0 15.7 %out_own.8 = (bf16[512,8192]{1,0:T(8,128)(2,1)}, bf16[128,4096]{1,0:T(8,128)(2,1)}) custom-call(s32[1]{0:T(128)} %bitcast.tp_ref, bf16[128,4096]{1,0:T(8,128)(2,1)} %get-tuple-element.48.o_ref, bf16[4096,8192]{1,0:T(8,128)(2,1)} %w_ref.25, bf16[512,8192]{1,0:T(8,128)(2,1)} %x_ref.13, f32[128,1024]{1,0:T(8,128)} %copy-done.5, ...), custom_call_target="tpu_custom_call", output_to_operand_aliasing={{0}: (6, {})} | custom-call | flops 4294967296 | bytes 34603008 | tf_op jit(solution)/shard_map/out_own/pallas_call | solution.py:395
  246.1 15.7 %out_own.9 = (bf16[512,8192]{1,0:T(8,128)(2,1)}, bf16[128,4096]{1,0:T(8,128)(2,1)}) custom-call(s32[1]{0:T(128)} %bitcast.tp_ref, bf16[128,4096]{1,0:T(8,128)(2,1)} %get-tuple-element.46.o_ref, bf16[4096,8192]{1,0:T(8,128)(2,1)} %w_ref.25, bf16[512,8192]{1,0:T(8,128)(2,1)} %x_ref.13, ...), custom_call_target="tpu_custom_call", output_to_operand_aliasing={{0}: (6, {})} | custom-call | flops 4294967296 | bytes 34603008 | tf_op jit(solution)/shard_map/out_own/pallas_call | solution.py:395
  266.6 4.0 %out_send.6 = f32[128,512]{1,0:T(8,128)} custom-call(s32[1]{0:T(128)} %bitcast.tp_ref, bf16[128,4096]{1,0:T(8,128)(2,1)} %get-tuple-element.43.o_ref, bf16[4096,8192]{1,0:T(8,128)(2,1)} %w_ref.25), custom_call_target="tpu_custom_call" | custom-call | flops 536870912 | bytes 5242880 | tf_op jit(solution)/shard_map/out_send/pallas_call | solution.py:353
  271.7 5.8 %out_own.10 = (bf16[512,8192]{1,0:T(8,128)(2,1)}, bf16[128,1024]{1,0:T(8,128)(2,1)}) custom-call(s32[1]{0:T(128)} %bitcast.tp_ref, bf16[128,4096]{1,0:T(8,128)(2,1)} %get-tuple-element.43.o_ref, bf16[4096,8192]{1,0:T(8,128)(2,1)} %w_ref.25, bf16[512,8192]{1,0:T(8,128)(2,1)} %x_ref.13, ...), custom_call_target="tpu_custom_call", output_to_operand_aliasing={{0}: (5, {})} | custom-call | flops 1073741824 | bytes 9437184 | tf_op jit(solution)/shard_map/out_own/pallas_call | solution.py:395
  278.4 9.6 %out_own.11 = (bf16[512,8192]{1,0:T(8,128)(2,1)}, bf16[128,2048]{1,0:T(8,128)(2,1)}) custom-call(s32[1]{0:T(128)} %bitcast.tp_ref, bf16[128,4096]{1,0:T(8,128)(2,1)} %get-tuple-element.43.o_ref, bf16[4096,8192]{1,0:T(8,128)(2,1)} %w_ref.25, bf16[512,8192]{1,0:T(8,128)(2,1)} %x_ref.13, ...), custom_call_target="tpu_custom_call", output_to_operand_aliasing={{0}: (5, {})} | custom-call | flops 2147483648 | bytes 17825792 | tf_op jit(solution)/shard_map/out_own/pallas_call | solution.py:395
  288.1 41.9 %collective-permute-done.1.rest_0_ = f32[128,512]{1,0:T(8,128)S(1)} collective-permute-done((f32[128,512]{1,0:T(8,128)S(1)}, f32[128,512]{1,0:T(8,128)S(1)}, u32[]{:S(2)}, u32[]{:S(2)}) %collective-permute-start.1) | collective-permute-done | bytes 262176 | tf_op jit(solution)/shard_map/ppermute | solution.py:452
  331.3 4.0 %out_own.12 = (bf16[512,8192]{1,0:T(8,128)(2,1)}, bf16[128,512]{1,0:T(8,128)(2,1)}) custom-call(s32[1]{0:T(128)} %bitcast.tp_ref, bf16[128,4096]{1,0:T(8,128)(2,1)} %get-tuple-element.43.o_ref, bf16[4096,8192]{1,0:T(8,128)(2,1)} %w_ref.25, bf16[512,8192]{1,0:T(8,128)(2,1)} %x_ref.13, f32[128,512]{1,0:T(8,128)} %copy-done.9, ...), custom_call_target="tpu_custom_call", output_to_operand_aliasing={{0}: (5, {})} | custom-call | flops 536870912 | bytes 5242880 | tf_op jit(solution)/shard_map/out_own/pallas_call | solution.py:395
  336.9 4.0 %out_own.13 = (bf16[512,8192]{1,0:T(8,128)(2,1)}, bf16[128,512]{1,0:T(8,128)(2,1)}) custom-call(s32[1]{0:T(128)} %bitcast.tp_ref, bf16[128,4096]{1,0:T(8,128)(2,1)} %get-tuple-element.43.o_ref, bf16[4096,8192]{1,0:T(8,128)(2,1)} %w_ref.25, bf16[512,8192]{1,0:T(8,128)(2,1)} %x_ref.13, ...), custom_call_target="tpu_custom_call", output_to_operand_aliasing={{0}: (5, {})} | custom-call | flops 536870912 | bytes 5242880 | tf_op jit(solution)/shard_map/out_own/pallas_call | solution.py:395
  344.8 5.2 %place.7.y_in = bf16[512,8192]{1,0:T(8,128)(2,1)} custom-call(s32[1]{0:T(128)} %bitcast.tp_ref, bf16[128,4096]{1,0:T(8,128)(2,1)} %collective-permute-done.16.r_ref, bf16[512,8192]{1,0:T(8,128)(2,1)} %get-tuple-element.66.y_in), custom_call_target="tpu_custom_call", output_to_operand_aliasing={{}: (2, {})} | custom-call | flops 524288 | bytes 2097152 | tf_op jit(solution)/shard_map/place/pallas_call | solution.py:419
  350.0 5.2 %place.8.y_in = bf16[512,8192]{1,0:T(8,128)(2,1)} custom-call(s32[1]{0:T(128)} %bitcast.tp_ref, bf16[128,4096]{1,0:T(8,128)(2,1)} %collective-permute-done.15.r_ref, bf16[512,8192]{1,0:T(8,128)(2,1)} %place.7.y_in), custom_call_target="tpu_custom_call", output_to_operand_aliasing={{}: (2, {})} | custom-call | flops 524288 | bytes 2097152 | tf_op jit(solution)/shard_map/place/pallas_call | solution.py:419
  356.2 5.2 %place.9.y_in = bf16[512,8192]{1,0:T(8,128)(2,1)} custom-call(s32[1]{0:T(128)} %bitcast.tp_ref, bf16[128,4096]{1,0:T(8,128)(2,1)} %copy-done.4, bf16[512,8192]{1,0:T(8,128)(2,1)} %place.8.y_in), custom_call_target="tpu_custom_call", output_to_operand_aliasing={{}: (2, {})} | custom-call | flops 524288 | bytes 2097152 | tf_op jit(solution)/shard_map/place/pallas_call | solution.py:419
  (67 shorter events, 36.7 us)
Async XLA Ops:
  56.8 152.0 %collective-permute-start.9 = (f32[128,3072]{1,0:T(8,128)}, f32[128,3072]{1,0:T(8,128)}, u32[]{:S(2)}, u32[]{:S(2)}) collective-permute-start(f32[128,3072]{1,0:T(8,128)} %out_send.11), channel_id=1, source_target_pairs={{0,4},{4,0},{1,5},{5,1},{2,6},{6,2},{3,7},{7,3}} | collective-permute-start | bytes 4718600 | tf_op jit(solution)/shard_map/ppermute | solution.py:452
  58.3 150.0 %collective-permute-start.8 = (f32[128,1024]{1,0:T(8,128)}, f32[128,1024]{1,0:T(8,128)}, u32[]{:S(2)}, u32[]{:S(2)}) collective-permute-start(f32[128,1024]{1,0:T(8,128)} %get-tuple-element.52), channel_id=1, source_target_pairs={{0,4},{4,0},{1,5},{5,1},{2,6},{6,2},{3,7},{7,3}} | collective-permute-start | bytes 1572872 | tf_op jit(solution)/shard_map/ppermute | solution.py:452
  105.8 120.7 %collective-permute-start.7 = (f32[128,3072]{1,0:T(8,128)}, f32[128,3072]{1,0:T(8,128)S(1)}, u32[]{:S(2)}, u32[]{:S(2)}) collective-permute-start(f32[128,3072]{1,0:T(8,128)} %out_send.10), channel_id=1, source_target_pairs={{0,4},{4,0},{1,5},{5,1},{2,6},{6,2},{3,7},{7,3}} | collective-permute-start | bytes 4718600 | tf_op jit(solution)/shard_map/ppermute | solution.py:452
  107.3 118.7 %collective-permute-start.6 = (f32[128,1024]{1,0:T(8,128)}, f32[128,1024]{1,0:T(8,128)S(1)}, u32[]{:S(2)}, u32[]{:S(2)}) collective-permute-start(f32[128,1024]{1,0:T(8,128)} %get-tuple-element.49), channel_id=1, source_target_pairs={{0,4},{4,0},{1,5},{5,1},{2,6},{6,2},{3,7},{7,3}} | collective-permute-start | bytes 1572872 | tf_op jit(solution)/shard_map/ppermute | solution.py:452
  162.6 82.4 %collective-permute-start.5 = (f32[128,3072]{1,0:T(8,128)}, f32[128,3072]{1,0:T(8,128)S(1)}, u32[]{:S(2)}, u32[]{:S(2)}) collective-permute-start(f32[128,3072]{1,0:T(8,128)} %out_send.9), channel_id=1, source_target_pairs={{0,4},{4,0},{1,5},{5,1},{2,6},{6,2},{3,7},{7,3}} | collective-permute-start | bytes 4718600 | tf_op jit(solution)/shard_map/ppermute | solution.py:452
  208.3 35.5 %collective-permute-start.4 = (f32[128,1024]{1,0:T(8,128)}, f32[128,1024]{1,0:T(8,128)}, u32[]{:S(2)}, u32[]{:S(2)}) collective-permute-start(f32[128,1024]{1,0:T(8,128)} %get-tuple-element.47), channel_id=1, source_target_pairs={{0,4},{4,0},{1,5},{5,1},{2,6},{6,2},{3,7},{7,3}} | collective-permute-start | bytes 1572872 | tf_op jit(solution)/shard_map/ppermute | solution.py:452
  208.8 68.7 %collective-permute-start.2 = (f32[128,2048]{1,0:T(8,128)}, f32[128,2048]{1,0:T(8,128)}, u32[]{:S(2)}, u32[]{:S(2)}) collective-permute-start(f32[128,2048]{1,0:T(8,128)} %out_send.8), channel_id=1, source_target_pairs={{0,4},{4,0},{1,5},{5,1},{2,6},{6,2},{3,7},{7,3}} | collective-permute-start | bytes 3145736 | tf_op jit(solution)/shard_map/ppermute | solution.py:452
  226.0 2.1 copy-start.5
  226.0 44.6 %collective-permute-start.3 = (f32[128,1024]{1,0:T(8,128)}, f32[128,1024]{1,0:T(8,128)}, u32[]{:S(2)}, u32[]{:S(2)}) collective-permute-start(f32[128,1024]{1,0:T(8,128)} %get-tuple-element.44), channel_id=1, source_target_pairs={{0,4},{4,0},{1,5},{5,1},{2,6},{6,2},{3,7},{7,3}} | collective-permute-start | bytes 1572872 | tf_op jit(solution)/shard_map/ppermute | solution.py:452
  226.5 1.5 copy-start.2
  226.5 114.3 %collective-permute-start.16 = (bf16[128,4096]{1,0:T(8,128)(2,1)}, bf16[128,4096]{1,0:T(8,128)(2,1)}, u32[]{:S(2)}, u32[]{:S(2)}) collective-permute-start(bf16[128,4096]{1,0:T(8,128)(2,1)} %get-tuple-element.65), channel_id=1, source_target_pairs={{0,4},{4,0},{1,5},{5,1},{2,6},{6,2},{3,7},{7,3}} | collective-permute-start | bytes 3145736 | tf_op jit(solution)/shard_map/ppermute | solution.py:452
  243.8 98.0 %collective-permute-start.15 = (bf16[128,4096]{1,0:T(8,128)(2,1)}, bf16[128,4096]{1,0:T(8,128)(2,1)}, u32[]{:S(2)}, u32[]{:S(2)}) collective-permute-start(bf16[128,4096]{1,0:T(8,128)(2,1)} %get-tuple-element.64), channel_id=1, source_target_pairs={{0,4},{4,0},{1,5},{5,1},{2,6},{6,2},{3,7},{7,3}} | collective-permute-start | bytes 3145736 | tf_op jit(solution)/shard_map/ppermute | solution.py:452
  244.9 1.2 copy-start.3
  261.8 93.3 %collective-permute-start.14 = (bf16[128,4096]{1,0:T(8,128)(2,1)}, bf16[128,4096]{1,0:T(8,128)(2,1)S(1)}, u32[]{:S(2)}, u32[]{:S(2)}) collective-permute-start(bf16[128,4096]{1,0:T(8,128)(2,1)} %get-tuple-element.63), channel_id=1, source_target_pairs={{0,4},{4,0},{1,5},{5,1},{2,6},{6,2},{3,7},{7,3}} | collective-permute-start | bytes 3145736 | tf_op jit(solution)/shard_map/ppermute | solution.py:452
  266.6 4.0 %copy-start.10 = (f32[128,512]{1,0:T(8,128)S(1)}, f32[128,512]{1,0:T(8,128)}, u32[]{:S(2)}) copy-start(f32[128,512]{1,0:T(8,128)} %out_send.7) | copy-start | bytes 786436
  270.6 59.4 %collective-permute-start.1 = (f32[128,512]{1,0:T(8,128)S(1)}, f32[128,512]{1,0:T(8,128)S(1)}, u32[]{:S(2)}, u32[]{:S(2)}) collective-permute-start(f32[128,512]{1,0:T(8,128)S(1)} %copy-done.10), channel_id=1, source_target_pairs={{0,4},{4,0},{1,5},{5,1},{2,6},{6,2},{3,7},{7,3}} | collective-permute-start | bytes 786440 | tf_op jit(solution)/shard_map/ppermute | solution.py:452
  271.7 5.8 %copy-start.8 = (f32[128,512]{1,0:T(8,128)S(1)}, f32[128,512]{1,0:T(8,128)}, u32[]{:S(2)}) copy-start(f32[128,512]{1,0:T(8,128)} %out_send.6) | copy-start | bytes 786436
  277.5 58.2 %collective-permute-start = (f32[128,512]{1,0:T(8,128)S(1)}, f32[128,512]{1,0:T(8,128)}, u32[]{:S(2)}, u32[]{:S(2)}) collective-permute-start(f32[128,512]{1,0:T(8,128)S(1)} %copy-done.8), channel_id=1, source_target_pairs={{0,4},{4,0},{1,5},{5,1},{2,6},{6,2},{3,7},{7,3}} | collective-permute-start | bytes 786440 | tf_op jit(solution)/shard_map/ppermute | solution.py:452
  278.4 52.8 %copy-start = (bf16[256,1024]{1,0:T(8,128)(2,1)S(1)}, bf16[256,1024]{1,0:T(8,128)(2,1)}, u32[]{:S(2)}) copy-start(bf16[256,1024]{1,0:T(8,128)(2,1)} %get-tuple-element.35.rest_0_) | copy-start | bytes 1572868
  278.4 52.8 %copy-start.1 = (bf16[256,1024]{1,0:T(8,128)(2,1)S(1)}, bf16[256,1024]{1,0:T(8,128)(2,1)}, u32[]{:S(2)}) copy-start(bf16[256,1024]{1,0:T(8,128)(2,1)} %get-tuple-element.39.rest_4_) | copy-start | bytes 1572868
  330.7 32.9 %collective-permute-start.12 = (bf16[128,2048]{1,0:T(8,128)(2,1)}, bf16[128,2048]{1,0:T(8,128)(2,1)S(1)}, u32[]{:S(2)}, u32[]{:S(2)}) collective-permute-start(bf16[128,2048]{1,0:T(8,128)(2,1)} %get-tuple-element.61), channel_id=1, source_target_pairs={{0,4},{4,0},{1,5},{5,1},{2,6},{6,2},{3,7},{7,3}} | collective-permute-start | bytes 1572872 | tf_op jit(solution)/shard_map/ppermute | solution.py:452
  335.7 25.6 %collective-permute-start.13 = (bf16[128,1024]{1,0:T(8,128)(2,1)}, bf16[128,1024]{1,0:T(8,128)(2,1)S(1)}, u32[]{:S(2)}, u32[]{:S(2)}) collective-permute-start(bf16[128,1024]{1,0:T(8,128)(2,1)} %get-tuple-element.62), channel_id=1, source_target_pairs={{0,4},{4,0},{1,5},{5,1},{2,6},{6,2},{3,7},{7,3}} | collective-permute-start | bytes 786440 | tf_op jit(solution)/shard_map/ppermute | solution.py:452
  340.9 26.7 %collective-permute-start.11 = (bf16[128,512]{1,0:T(8,128)(2,1)}, bf16[128,512]{1,0:T(8,128)(2,1)S(1)}, u32[]{:S(2)}, u32[]{:S(2)}) collective-permute-start(bf16[128,512]{1,0:T(8,128)(2,1)} %get-tuple-element.60), channel_id=1, source_target_pairs={{0,4},{4,0},{1,5},{5,1},{2,6},{6,2},{3,7},{7,3}} | collective-permute-start | bytes 393224 | tf_op jit(solution)/shard_map/ppermute | solution.py:452
  341.8 28.1 %collective-permute-start.10 = (bf16[128,512]{1,0:T(8,128)(2,1)}, bf16[128,512]{1,0:T(8,128)(2,1)}, u32[]{:S(2)}, u32[]{:S(2)}) collective-permute-start(bf16[128,512]{1,0:T(8,128)(2,1)} %get-tuple-element.59), channel_id=1, source_target_pairs={{0,4},{4,0},{1,5},{5,1},{2,6},{6,2},{3,7},{7,3}} | collective-permute-start | bytes 393224 | tf_op jit(solution)/shard_map/ppermute | solution.py:452
  (5 other events, 3.8 us)

commit v3 on v2

--- a/solution.py
+++ b/solution.py
@@ -12,7 +12,7 @@
 LANES = 128
 VMEM_BYTES = 60 * 1024 * 1024
 ROWS = 128
-CHUNKS = ((1024, 3072), (1024, 3072), (1024, 3072), (1024, 2048, 512, 512))
+CHUNKS = ((1024, 3072), (1024, 3072), (1024, 3072), (2048, 1024, 512, 512))
 PLAN = (("make", 0, 0, 2), ("make", 1, 0, 2), ("own", 0, 0, 2), ("make", 2, 0, 2), ("own", 1, 0, 2), ("make", 3, 0, 4), ("own", 2, 0, 2), ("own", 3, 0, 1), ("own", 3, 1, 2), ("own", 3, 2, 3), ("own", 3, 3, 4))
 
 
@@ -183,10 +183,11 @@
     k_dim = q.shape[1]
     half_cols = w_o.shape[1] // 2
     bn = 512
+    unroll = 2 if row_group == 0 else 1
 
     def kernel(pos_ref, pos2_ref, q_hbm, w_hbm, *rest):
         kv_hbm = rest[:parts]
-        o_ref, part_ref, kv_all, q_buf, w_buf, s_ref, p_ref, m_ref, l_ref, acc_ref, kv_sem, q_sem, w_sem = rest[parts:]
+        o_hbm, part_hbm, kv_all, q_buf, o_buf, part_buf, w_buf, s_ref, p_ref, m_ref, l_ref, acc_ref, kv_sem, q_sem, w_sem, o_sem, p_sem = rest[parts:]
         dev, tp = lax.axis_index('cp'), lax.axis_index('tp')
         copies = []
         for n in range(parts):
@@ -218,46 +219,59 @@
         pos_row = pos2_ref[row_group:row_group + 1, :].astype(F32)
         first = t_idx - jnp.transpose(jnp.broadcast_to(pos_row, (qb, LANES))).astype(jnp.int32)
 
-        def kv_head(n, carry):
-            q_copy(n).wait()
-
-            def head_cols(g):
-                return pl.ds(pl.multiple_of((n * group + g) * HEAD, HEAD), HEAD)
-
-            k_cols = pl.ds(pl.multiple_of(n * HEAD, HEAD), HEAD)
-            v_cols = pl.ds(pl.multiple_of((kv_heads + n) * HEAD, HEAD), HEAD)
-            q_stack = jnp.concatenate([q_buf[:, head_cols(g)] for g in range(group)], axis=0)
-
-            @pl.when(p0 <= kb)
-            def _():
-                w0 = pl.multiple_of(jnp.maximum(t0 - kb, 0), kb)
-                at = pl.ds(w0, 2 * kb)
-                s_ref[...] = lax.dot_general(q_stack, kv_all[at, k_cols], (((1,), (1,)), ((), ())), preferred_element_type=F32)
-                u = w0 + lane
-                visible = jnp.concatenate([(u >= first) & (u <= t_idx), (u + kb >= first) & (u + kb <= t_idx)], axis=1)
-                for g in range(group):
-                    at_g = slice(g * qb, (g + 1) * qb)
-                    s = jnp.where(visible, s_ref[at_g] * scale, -1e30)
-                    s_ref[at_g] = s
-                    m_ref[g] = jnp.broadcast_to(jnp.max(s, axis=1, keepdims=True), (qb, LANES))
-                for g in range(group):
-                    at_g = slice(g * qb, (g + 1) * qb)
-                    m = m_ref[g]
-                    e = jnp.exp(s_ref[at_g] - jnp.concatenate([m, m], axis=1))
-                    s_ref[at_g] = e
-                    l_ref[g] = 1.0 / jnp.broadcast_to(jnp.sum(e, axis=1, keepdims=True), (qb, LANES))
-                for g in range(group):
-                    at_g = slice(g * qb, (g + 1) * qb)
-                    inv = l_ref[g]
-                    p_ref[at_g] = (s_ref[at_g] * jnp.concatenate([inv, inv], axis=1)).astype(BF16)
-                o = jnp.dot(p_ref[...], kv_all[at, v_cols], preferred_element_type=F32).astype(BF16)
-                for g in range(group):
-                    o_ref[:, head_cols(g)] = o[g * qb:(g + 1) * qb]
-
-            @pl.when(p0 > kb)
-            def _():
-                kb0 = lax.div(t0 - p0, kb)
-                kb1 = lax.div(t0, kb) + 1
+        def head_cols(n, g):
+            return pl.ds(pl.multiple_of((n * group + g) * HEAD, HEAD), HEAD)
+
+        def kv_cols(n):
+            return pl.ds(pl.multiple_of(n * HEAD, HEAD), HEAD)
+
+        def stack(n):
+            return jnp.concatenate([q_buf[:, head_cols(n, g)] for g in range(group)], axis=0)
+
+        @pl.when(p0 <= kb)
+        def _():
+            w0 = pl.multiple_of(jnp.maximum(t0 - kb, 0), kb)
+            at = pl.ds(w0, 2 * kb)
+            u = w0 + lane
+            visible = jnp.concatenate([(u >= first) & (u <= t_idx), (u + kb >= first) & (u + kb <= t_idx)], axis=1)
+
+            def some_heads(i, carry):
+                for j in range(unroll):
+                    n = i * unroll + j
+                    q_copy(n).wait()
+                    s_ref[j] = lax.dot_general(stack(n), kv_all[at, kv_cols(n)], (((1,), (1,)), ((), ())), preferred_element_type=F32)
+                for j in range(unroll):
+                    for g in range(group):
+                        at_g = slice(g * qb, (g + 1) * qb)
+                        s = jnp.where(visible, s_ref[j, at_g] * scale, -1e30)
+                        s_ref[j, at_g] = s
+                        m_ref[g] = jnp.broadcast_to(jnp.max(s, axis=1, keepdims=True), (qb, LANES))
+                    for g in range(group):
+                        at_g = slice(g * qb, (g + 1) * qb)
+                        m = m_ref[g]
+                        e = jnp.exp(s_ref[j, at_g] - jnp.concatenate([m, m], axis=1))
+                        s_ref[j, at_g] = e
+                        l_ref[g] = 1.0 / jnp.broadcast_to(jnp.sum(e, axis=1, keepdims=True), (qb, LANES))
+                    for g in range(group):
+                        at_g = slice(g * qb, (g + 1) * qb)
+                        inv = l_ref[g]
+                        p_ref[j, at_g] = (s_ref[j, at_g] * jnp.concatenate([inv, inv], axis=1)).astype(BF16)
+                    n = i * unroll + j
+                    o = jnp.dot(p_ref[j], kv_all[at, kv_cols(kv_heads + n)], preferred_element_type=F32).astype(BF16)
+                    for g in range(group):
+                        o_buf[:, head_cols(n, g)] = o[g * qb:(g + 1) * qb]
+                return carry
+
+            lax.fori_loop(0, kv_heads // unroll, some_heads, 0)
+
+        @pl.when(p0 > kb)
+        def _():
+            kb0 = lax.div(t0 - p0, kb)
+            kb1 = lax.div(t0, kb) + 1
+
+            def kv_head(n, carry):
+                q_copy(n).wait()
+                q_stack = stack(n)
                 m_ref[...] = jnp.full_like(m_ref, -1e30)
                 l_ref[...] = jnp.zeros_like(l_ref)
                 acc_ref[...] = jnp.zeros_like(acc_ref)
@@ -265,53 +279,63 @@
                 def block(j):
                     at = pl.ds(pl.multiple_of(j * kb, kb), kb)
                     u = j * kb + lane
-                    s_ref[:, :kb] = lax.dot_general(q_stack, kv_all[at, k_cols], (((1,), (1,)), ((), ())), preferred_element_type=F32)
+                    s_ref[0, :, :kb] = lax.dot_general(q_stack, kv_all[at, kv_cols(n)], (((1,), (1,)), ((), ())), preferred_element_type=F32)
                     return at, (u >= first) & (u <= t_idx)
 
                 def head_scores(g, visible):
                     at_g = pl.ds(pl.multiple_of(g * qb, qb), qb)
-                    return at_g, jnp.where(visible, s_ref[at_g, :kb] * scale, -1e30)
-
-                def stats(j, carry):
+                    return at_g, jnp.where(visible, s_ref[0, at_g, :kb] * scale, -1e30)
+
+                def stats(j, inner):
                     _, visible = block(j)
 
-                    def one(g, inner):
+                    def one(g, c):
                         _, s = head_scores(g, visible)
                         m_old = m_ref[g]
                         m_new = jnp.maximum(m_old, jnp.max(s, axis=1, keepdims=True))
                         l_ref[g] = l_ref[g] * jnp.exp(m_old - m_new) + jnp.sum(jnp.exp(s - m_new), axis=1, keepdims=True)
                         m_ref[g] = m_new
-                        return inner
-
-                    return lax.fori_loop(0, group, one, carry)
-
-                def weigh(j, carry):
+                        return c
+
+                    return lax.fori_loop(0, group, one, inner)
+
+                def weigh(j, inner):
                     at, visible = block(j)
 
-                    def one(g, inner):
+                    def one(g, c):
                         at_g, s = head_scores(g, visible)
-                        p_ref[at_g, :kb] = (jnp.exp(s - m_ref[g]) / l_ref[g]).astype(BF16)
-                        return inner
+                        p_ref[0, at_g, :kb] = (jnp.exp(s - m_ref[g]) / l_ref[g]).astype(BF16)
+                        return c
 
                     lax.fori_loop(0, group, one, 0)
-                    acc_ref[...] += jnp.dot(p_ref[:, :kb], kv_all[at, v_cols], preferred_element_type=F32)
-                    return carry
+                    acc_ref[...] += jnp.dot(p_ref[0, :, :kb], kv_all[at, kv_cols(kv_heads + n)], preferred_element_type=F32)
+                    return inner
 
                 lax.fori_loop(kb0, kb1, stats, 0)
                 lax.fori_loop(kb0, kb1, weigh, 0)
                 for g in range(group):
-                    o_ref[:, head_cols(g)] = acc_ref[g * qb:(g + 1) * qb].astype(BF16)
-
-            return carry
-
-        lax.fori_loop(0, kv_heads, kv_head, 0)
+                    o_buf[:, head_cols(n, g)] = acc_ref[g * qb:(g + 1) * qb].astype(BF16)
+                return carry
+
+            lax.fori_loop(0, kv_heads, kv_head, 0)
+
+        o_copy = pltpu.make_async_copy(o_buf, o_hbm, o_sem)
+        o_copy.start()
+
+        def part_copy(j):
+            at = pl.ds(pl.multiple_of(j * bn, bn), bn)
+            return pltpu.make_async_copy(part_buf.at[:, at], part_hbm.at[:, at], p_sem.at[j])
 
         def product(j, carry):
             w_copy(j).wait()
-            part_ref[:, pl.ds(pl.multiple_of(j * bn, bn), bn)] = jnp.dot(o_ref[...], w_buf[j], preferred_element_type=F32)
+            part_buf[:, pl.ds(pl.multiple_of(j * bn, bn), bn)] = jnp.dot(o_buf[...], w_buf[j], preferred_element_type=F32)
+            part_copy(j).start()
             return carry
 
         lax.fori_loop(0, cols // bn, product, 0)
+        o_copy.wait()
+        for j in range(cols // bn):
+            part_copy(j).wait()
 
     whole = lambda shape: pl.BlockSpec(shape, lambda i, *_: (0, 0))
     return pl.pallas_call(
@@ -320,18 +344,22 @@
             num_scalar_prefetch=1,
             grid=(1,),
             in_specs=[whole(pos2.shape), any_spec(), any_spec()] + [any_spec()] * parts,
-            out_specs=[whole(q.shape), whole((ROWS, cols))],
+            out_specs=[any_spec(), any_spec()],
             scratch_shapes=[
                 pltpu.VMEM((keys, kv_parts[0].shape[1]), BF16),
                 pltpu.VMEM(q.shape, BF16),
+                pltpu.VMEM(q.shape, BF16),
+                pltpu.VMEM((ROWS, cols), F32),
                 pltpu.VMEM((cols // bn, k_dim, bn), BF16),
-                pltpu.VMEM((group * qb, 2 * kb), F32),
-                pltpu.VMEM((group * qb, 2 * kb), BF16),
+                pltpu.VMEM((unroll, group * qb, 2 * kb), F32),
+                pltpu.VMEM((unroll, group * qb, 2 * kb), BF16),
                 pltpu.VMEM((group, qb, LANES), F32),
                 pltpu.VMEM((group, qb, LANES), F32),
                 pltpu.VMEM((group * qb, HEAD), F32),
                 pltpu.SemaphoreType.DMA((parts,)),
                 pltpu.SemaphoreType.DMA((kv_heads,)),
+                pltpu.SemaphoreType.DMA((cols // bn,)),
+                pltpu.SemaphoreType.DMA,
                 pltpu.SemaphoreType.DMA((cols // bn,)),
             ],
         ),
@@ -342,76 +370,98 @@
     )(pos, pos2, q, w_o, *kv_parts)
 
 
-def out_send(tp_me, o, w_o, col0, cols):
+def out_cols(row_group, o, w_o, col0, cols, x_in=None, recvs=(), y_buf=None):
     rows, k_dim = o.shape
     bn = 512
-    own_blocks = w_o.shape[1] // 2 // bn
-
-    def kernel(tp_ref, o_ref, w_ref, part_ref):
-        part_ref[...] = jnp.dot(o_ref[...], w_ref[...], preferred_element_type=F32)
-
+    nb = cols // bn
+    half_cols = w_o.shape[1] // 2
+    own = bool(recvs)
+    starts = [sum(r.shape[1] for r in recvs[:n]) for n in range(len(recvs))]
+
+    def kernel(o_hbm, w_hbm, *rest):
+        if own:
+            x_hbm, recv_hbm = rest[0], rest[1:1 + len(recvs)]
+            rest = rest[1 + len(recvs) + (y_buf is not None):]
+            y_hbm, c_hbm, o_buf, w_buf, c_buf, o_sem, w_sem, c_sem, x_buf, r_buf, x_sem, r_sem, y_sem = rest
+        else:
+            c_hbm, o_buf, w_buf, c_buf, o_sem, w_sem, c_sem = rest
+        tp = lax.axis_index('tp')
+        side = tp if own else 1 - tp
+        base = side * half_cols + col0
+
+        def w_copy(j):
+            return pltpu.make_async_copy(w_hbm.at[:, pl.ds(pl.multiple_of(base + j * bn, bn), bn)], w_buf.at[j], w_sem.at[j])
+
+        def out_copies(j):
+            at = pl.ds(pl.multiple_of(j * bn, bn), bn)
+            copies = [pltpu.make_async_copy(c_buf.at[:, at], c_hbm.at[:, at], c_sem.at[j])]
+            if own:
+                to = y_hbm.at[pl.ds(row_group * ROWS, rows), pl.ds(pl.multiple_of(base + j * bn, bn), bn)]
+                copies.append(pltpu.make_async_copy(c_buf.at[:, at], to, y_sem.at[j]))
+            return copies
+
+        o_copy = pltpu.make_async_copy(o_hbm, o_buf, o_sem)
+        o_copy.start()
+        w_copy(0).start()
+        extra = []
+        if own:
+            extra.append(pltpu.make_async_copy(x_hbm.at[pl.ds(row_group * ROWS, rows), pl.ds(pl.multiple_of(base, bn), cols)], x_buf, x_sem))
+            for n, recv in enumerate(recv_hbm):
+                extra.append(pltpu.make_async_copy(recv, r_buf.at[:, starts[n]:starts[n] + recv.shape[1]], r_sem.at[n]))
+            for copy in extra:
+                copy.start()
+        for j in range(1, nb):
+            w_copy(j).start()
+        o_copy.wait()
+        for copy in extra:
+            copy.wait()
+
+        def block(j, carry):
+            at = pl.ds(pl.multiple_of(j * bn, bn), bn)
+            w_copy(j).wait()
+            acc = jnp.dot(o_buf[...], w_buf[j], preferred_element_type=F32)
+            if own:
+                c_buf[:, at] = (x_buf[:, at].astype(F32) + (acc + r_buf[:, at])).astype(BF16)
+            else:
+                c_buf[:, at] = acc
+            for copy in out_copies(j):
+                copy.start()
+            return carry
+
+        lax.fori_loop(0, nb, block, 0)
+
+        def finish(j, carry):
+            for copy in out_copies(j):
+                copy.wait()
+            return carry
+
+        lax.fori_loop(0, nb, finish, 0)
+
+    kind = BF16 if own else F32
+    chunk = jax.ShapeDtypeStruct((rows, cols), kind)
+    ins = [o, w_o] + ([x_in, *recvs] if own else []) + ([] if y_buf is None else [y_buf])
+    sems = [pltpu.SemaphoreType.DMA, pltpu.SemaphoreType.DMA((nb,)), pltpu.SemaphoreType.DMA((nb,))]
+    scratch = [pltpu.VMEM((rows, k_dim), BF16), pltpu.VMEM((nb, k_dim, bn), BF16), pltpu.VMEM((rows, cols), kind)] + sems
+    if own:
+        scratch += [pltpu.VMEM((rows, cols), BF16), pltpu.VMEM((rows, cols), F32), pltpu.SemaphoreType.DMA, pltpu.SemaphoreType.DMA((len(recvs),)), pltpu.SemaphoreType.DMA((nb,))]
     return pl.pallas_call(
         kernel,
-        grid_spec=pltpu.PrefetchScalarGridSpec(
-            num_scalar_prefetch=1,
-            grid=(cols // bn,),
-            in_specs=[pl.BlockSpec((rows, k_dim), lambda i, tp: (0, 0)), pl.BlockSpec((k_dim, bn), lambda i, tp: (0, (1 - tp[0]) * own_blocks + col0 // bn + i))],
-            out_specs=pl.BlockSpec((rows, bn), lambda i, tp: (0, i)),
-        ),
-        out_shape=jax.ShapeDtypeStruct((rows, cols), F32),
+        grid=(1,),
+        in_specs=[any_spec()] * len(ins),
+        out_specs=[any_spec()] * (2 if own else 1),
+        out_shape=([jax.ShapeDtypeStruct(x_in.shape, BF16)] if own else []) + [chunk],
+        scratch_shapes=scratch,
+        input_output_aliases={} if y_buf is None else {len(ins) - 1: 0},
         compiler_params=pltpu.CompilerParams(vmem_limit_bytes=VMEM_BYTES),
         cost_estimate=pl.CostEstimate(flops=2 * rows * k_dim * cols, bytes_accessed=2 * k_dim * (rows + cols), transcendentals=0),
-        name="out_send",
-    )(tp_me, o, w_o)
-
-
-def out_own(row_group, tp_me, o, w_o, x_in, recvs, y_buf, col0):
-    rows, k_dim = o.shape
-    bn = 512
-    own_blocks = w_o.shape[1] // 2 // bn
-    starts = [sum(r.shape[1] for r in recvs[:n]) // bn for n in range(len(recvs) + 1)]
-    cols = starts[-1] * bn
-
-    def col(i, tp):
-        return tp[0] * own_blocks + col0 // bn + i
-
-    def kernel(tp_ref, o_ref, w_ref, x_ref, *rest):
-        y_ref, c_ref = rest[-2:]
-        acc = jnp.dot(o_ref[...], w_ref[...], preferred_element_type=F32)
-        step = pl.program_id(0)
-        for n in range(len(recvs)):
-            @pl.when((step >= starts[n]) & (step < starts[n + 1]))
-            def _():
-                out = (x_ref[...].astype(F32) + (acc + rest[n][...])).astype(BF16)
-                y_ref[...] = out
-                c_ref[...] = out
-
-    def recv_spec(n):
-        return pl.BlockSpec((rows, bn), lambda i, tp: (0, jnp.clip(i - starts[n], 0, starts[n + 1] - starts[n] - 1)))
-
-    ins = [o, w_o, x_in] + list(recvs) + ([] if y_buf is None else [y_buf])
-    wide = pl.BlockSpec((rows, bn), lambda i, tp: (row_group, col(i, tp)))
-    narrow = pl.BlockSpec((rows, bn), lambda i, tp: (0, i))
-    return pl.pallas_call(
-        kernel,
-        grid_spec=pltpu.PrefetchScalarGridSpec(
-            num_scalar_prefetch=1,
-            grid=(cols // bn,),
-            in_specs=[pl.BlockSpec((rows, k_dim), lambda i, tp: (0, 0)), pl.BlockSpec((k_dim, bn), lambda i, tp: (0, col(i, tp))), wide] + [recv_spec(n) for n in range(len(recvs))] + ([] if y_buf is None else [any_spec()]),
-            out_specs=[wide, narrow],
-        ),
-        out_shape=[jax.ShapeDtypeStruct(x_in.shape, BF16), jax.ShapeDtypeStruct((rows, cols), BF16)],
-        input_output_aliases={} if y_buf is None else {len(ins): 0},
-        compiler_params=pltpu.CompilerParams(vmem_limit_bytes=VMEM_BYTES),
-        cost_estimate=pl.CostEstimate(flops=2 * rows * k_dim * cols, bytes_accessed=2 * k_dim * (rows + cols), transcendentals=0),
-        name="out_own",
-    )(tp_me, *ins)
+        name="out_own" if own else "out_send",
+    )(*ins)
 
 
 def place(row_group, tp_me, recv, y_buf, col0):
     rows, cols = recv.shape
-    bn = 512
-    own_blocks = y_buf.shape[1] // 2 // bn
+    half_cols = y_buf.shape[1] // 2
+    bn = min(cols, 2048)
 
     def kernel(tp_ref, r_ref, y_in, y_ref):
         y_ref[...] = r_ref[...]
@@ -422,10 +472,11 @@
             num_scalar_prefetch=1,
             grid=(cols // bn,),
             in_specs=[pl.BlockSpec((rows, bn), lambda i, tp: (0, i)), any_spec()],
-            out_specs=pl.BlockSpec((rows, bn), lambda i, tp: (row_group, (1 - tp[0]) * own_blocks + col0 // bn + i)),
+            out_specs=pl.BlockSpec((rows, bn), lambda i, tp: (row_group, ((1 - tp[0]) * half_cols + col0) // bn + i)),
         ),
         out_shape=jax.ShapeDtypeStruct(y_buf.shape, BF16),
         input_output_aliases={2: 0},
+        compiler_params=pltpu.CompilerParams(vmem_limit_bytes=8 * 1024 * 1024),
         cost_estimate=pl.CostEstimate(flops=rows * cols, bytes_accessed=4 * rows * cols, transcendentals=0),
         name="place",
     )(tp_me, recv, y_buf)
@@ -458,7 +509,7 @@
             attn[r], part = attend_send(r, cp_size, pos_in_doc, pos2, q, kv_parts, w_o, sizes[0])
             sent[r] = [swap(part)]
             for c in range(1, len(sizes)):
-                part = out_send(tp_me, attn[r], w_o, sum(sizes[:c]), sizes[c])
+                part, = out_cols(r, attn[r], w_o, sum(sizes[:c]), sizes[c])
                 sent[r].append(swap(part))
 
         for kind, r, c0, c1 in PLAN:
@@ -466,7 +517,7 @@
                 make(r)
                 continue
             col0 = sum(CHUNKS[r][:c0])
-            y_buf, block = out_own(r, tp_me, attn[r], w_o, x_in, sent[r][c0:c1], y_buf, col0)
+            y_buf, block = out_cols(r, attn[r], w_o, col0, sum(CHUNKS[r][c0:c1]), x_in, sent[r][c0:c1], y_buf)
             results.append((r, col0, swap(block)))
         for r, col0, block in results:
             y_buf = place(r, tp_me, block, y_buf, col0)

time: 373 us -> 362 us (0.971)
  Pallas kernels: 304 us -> 295 us
    pallas_call x7, Pallas kernels: 23.4 us -> 8.06 us  [place(): pl.pallas_call(kernel, grid_spec=pltpu.PrefetchScalarGridSpec(num_scalar_...]
    unnamed x25 -> x17, local copies, waits for them, and re-layouts: 5.06 us -> 1.26 us
  transfers between devices with their start and end apart: 17 -> 17, of which waited for: 2 -> 1; matrix products, arithmetic and copies ran while one was open for 1% -> 1% of each run, Pallas kernels for 66% -> 66%
where the time goes in v3:
time: 362 us; the launch traced here: 361 us
  Pallas kernels  295 us (81%)
  waiting for transfers between devices  41.3 us (11%)
  starting transfers between devices  17.8 us (5%)
  local copies, waits for them, and re-layouts  6.26 us (2%)
    pallas_call x13, Pallas kernels, out_cols(): pl.pallas_call(kernel, grid=(1,), in_specs=[any_spec()] * len(ins), out_s...  126 us
    pallas_call x4, Pallas kernels, front(): pl.pallas_call(kernel, grid=(1,), in_specs=[any_spec(), whole(gain), whol...  115 us
    pallas_call x4, Pallas kernels, attend_send(): pl.pallas_call(kernel, grid_spec=pltpu.PrefetchScalarGridSpec(num_scalar_...  45.9 us
    ppermute x17, waiting for transfers between devices, swap(): return lax.ppermute(value, 'tp', swap_tp)  41.3 us
    ppermute x17, starting transfers between devices, swap(): return lax.ppermute(value, 'tp', swap_tp)  17.8 us
    pallas_call x7, Pallas kernels, place(): pl.pallas_call(kernel, grid_spec=pltpu.PrefetchScalarGridSpec(num_scalar_...  8.06 us
  transfers between devices with their start and end apart: 17, of which 1 were waited for; matrix products, arithmetic and copies ran while one was open for 1% of the time, Pallas kernels for 66%

profile of v3, /device:TPU:0, one launch (start us, length us, event | category | flops | bytes accessed | tf_op | source)
XLA Modules:
  0.0 360.8 jit_solution(15045947080138343603)
XLA Ops:
  0.6 33.9 %front.5 = (bf16[128,4096]{1,0:T(8,128)(2,1)}, bf16[256,1024]{1,0:T(8,128)(2,1)}, bf16[256,1024]{1,0:T(8,128)(2,1)}, bf16[256,1024]{1,0:T(8,128)(2,1)}, bf16[256,1024]{1,0:T(8,128)(2,1)}) custom-call(bf16[512,8192]{1,0:T(8,128)(2,1)} %rest_0_.17, f32[1,8192]{1,0:T(1,128)} %bitcast.4, s32[4,128]{1,0:T(4,128)} %bitcast.8, f32[1,64]{1,0:T(1,128)} %bitcast.16, ...), custom_call_target="tpu_custom_call" | custom-call | flops 21474836480 | bytes 71303168 | tf_op jit(solution)/shard_map/front/pallas_call | solution.py:150
  34.5 9.6 %attend_send.7 = (bf16[128,4096]{1,0:T(8,128)(2,1)}, f32[128,1024]{1,0:T(8,128)}) custom-call(s32[512]{0:T(512)} %pos_ref.7, s32[4,128]{1,0:T(4,128)} %bitcast.9, bf16[128,4096]{1,0:T(8,128)(2,1)} %get-tuple-element.50.q_hbm, bf16[4096,8192]{1,0:T(8,128)(2,1)} %w_hbm.33, bf16[256,1024]{1,0:T(8,128)(2,1)} %get-tuple-element.35.rest_0_, ...), custom_call_target="tpu_custom_call" | custom-call | flops 2147483648 | bytes 8388608 | tf_op jit(solution)/shard_map/attend_send/pallas_call | solution.py:341
  44.1 12.5 %out_send.11 = f32[128,3072]{1,0:T(8,128)} custom-call(bf16[128,4096]{1,0:T(8,128)(2,1)} %get-tuple-element.51.o_hbm, bf16[4096,8192]{1,0:T(8,128)(2,1)} %w_hbm.33), custom_call_target="tpu_custom_call" | custom-call | flops 3221225472 | bytes 26214400 | tf_op jit(solution)/shard_map/out_send/pallas_call | solution.py:447
  58.6 24.6 %front.7.q_hbm = bf16[128,4096]{1,0:T(8,128)(2,1)} custom-call(bf16[512,8192]{1,0:T(8,128)(2,1)} %rest_0_.17, f32[1,8192]{1,0:T(1,128)} %bitcast.5, s32[4,128]{1,0:T(4,128)} %bitcast.10, f32[1,64]{1,0:T(1,128)} %bitcast.17, bf16[8192,4096]{1,0:T(8,128)(2,1)} %wq_hbm.7), custom_call_target="tpu_custom_call" | custom-call | flops 10737418240 | bytes 69206016 | tf_op jit(solution)/shard_map/front/pallas_call | solution.py:150
  83.2 10.4 %attend_send.6 = (bf16[128,4096]{1,0:T(8,128)(2,1)}, f32[128,1024]{1,0:T(8,128)}) custom-call(s32[512]{0:T(512)} %pos_ref.7, s32[4,128]{1,0:T(4,128)} %bitcast.11, bf16[128,4096]{1,0:T(8,128)(2,1)} %front.7.q_hbm, bf16[4096,8192]{1,0:T(8,128)(2,1)} %w_hbm.33, bf16[256,1024]{1,0:T(8,128)(2,1)} %get-tuple-element.35.rest_0_, ...), custom_call_target="tpu_custom_call" | custom-call | flops 2147483648 | bytes 8388608 | tf_op jit(solution)/shard_map/attend_send/pallas_call | solution.py:341
  93.7 12.5 %out_send.10 = f32[128,3072]{1,0:T(8,128)} custom-call(bf16[128,4096]{1,0:T(8,128)(2,1)} %get-tuple-element.48.o_hbm, bf16[4096,8192]{1,0:T(8,128)(2,1)} %w_hbm.33), custom_call_target="tpu_custom_call" | custom-call | flops 3221225472 | bytes 26214400 | tf_op jit(solution)/shard_map/out_send/pallas_call | solution.py:447
  108.3 31.7 %front.6 = (bf16[128,4096]{1,0:T(8,128)(2,1)}, bf16[256,1024]{1,0:T(8,128)(2,1)}, bf16[256,1024]{1,0:T(8,128)(2,1)}, bf16[256,1024]{1,0:T(8,128)(2,1)}, bf16[256,1024]{1,0:T(8,128)(2,1)}) custom-call(bf16[512,8192]{1,0:T(8,128)(2,1)} %rest_0_.17, f32[1,8192]{1,0:T(1,128)} %bitcast.6, s32[4,128]{1,0:T(4,128)} %bitcast.12, f32[1,64]{1,0:T(1,128)} %bitcast.18, ...), custom_call_target="tpu_custom_call" | custom-call | flops 21474836480 | bytes 71303168 | tf_op jit(solution)/shard_map/front/pallas_call | solution.py:150
  140.0 10.9 %attend_send.5 = (bf16[128,4096]{1,0:T(8,128)(2,1)}, f32[128,1024]{1,0:T(8,128)}) custom-call(s32[512]{0:T(512)} %pos_ref.7, s32[4,128]{1,0:T(4,128)} %bitcast.13, bf16[128,4096]{1,0:T(8,128)(2,1)} %get-tuple-element.45.q_hbm, bf16[4096,8192]{1,0:T(8,128)(2,1)} %w_hbm.33, bf16[256,1024]{1,0:T(8,128)(2,1)} %get-tuple-element.35.rest_0_, ...), custom_call_target="tpu_custom_call" | custom-call | flops 2147483648 | bytes 8388608 | tf_op jit(solution)/shard_map/attend_send/pallas_call | solution.py:341
  150.9 12.5 %out_send.9 = f32[128,3072]{1,0:T(8,128)} custom-call(bf16[128,4096]{1,0:T(8,128)(2,1)} %get-tuple-element.46.o_hbm, bf16[4096,8192]{1,0:T(8,128)(2,1)} %w_hbm.33), custom_call_target="tpu_custom_call" | custom-call | flops 3221225472 | bytes 26214400 | tf_op jit(solution)/shard_map/out_send/pallas_call | solution.py:447
  165.0 24.4 %front.4.q_hbm = bf16[128,4096]{1,0:T(8,128)(2,1)} custom-call(bf16[512,8192]{1,0:T(8,128)(2,1)} %rest_0_.17, f32[1,8192]{1,0:T(1,128)} %bitcast.7, s32[4,128]{1,0:T(4,128)} %bitcast.14, f32[1,64]{1,0:T(1,128)} %bitcast.19, bf16[8192,4096]{1,0:T(8,128)(2,1)} %wq_hbm.7), custom_call_target="tpu_custom_call" | custom-call | flops 10737418240 | bytes 69206016 | tf_op jit(solution)/shard_map/front/pallas_call | solution.py:150
  189.4 15.0 %attend_send.4 = (bf16[128,4096]{1,0:T(8,128)(2,1)}, f32[128,2048]{1,0:T(8,128)}) custom-call(s32[512]{0:T(512)} %pos_ref.7, s32[4,128]{1,0:T(4,128)} %bitcast.15, bf16[128,4096]{1,0:T(8,128)(2,1)} %front.4.q_hbm, bf16[4096,8192]{1,0:T(8,128)(2,1)} %w_hbm.33, bf16[256,1024]{1,0:T(8,128)(2,1)} %get-tuple-element.35.rest_0_, ...), custom_call_target="tpu_custom_call" | custom-call | flops 3221225472 | bytes 16777216 | tf_op jit(solution)/shard_map/attend_send/pallas_call | solution.py:341
  204.5 5.2 %out_send.8 = f32[128,1024]{1,0:T(8,128)} custom-call(bf16[128,4096]{1,0:T(8,128)(2,1)} %get-tuple-element.43.o_hbm, bf16[4096,8192]{1,0:T(8,128)(2,1)} %w_hbm.33), custom_call_target="tpu_custom_call" | custom-call | flops 1073741824 | bytes 9437184 | tf_op jit(solution)/shard_map/out_send/pallas_call | solution.py:447
  211.8 17.5 %out_own.7 = (bf16[512,8192]{1,0:T(8,128)(2,1)}, bf16[128,4096]{1,0:T(8,128)(2,1)}) custom-call(bf16[128,4096]{1,0:T(8,128)(2,1)} %get-tuple-element.51.o_hbm, bf16[4096,8192]{1,0:T(8,128)(2,1)} %w_hbm.33, bf16[512,8192]{1,0:T(8,128)(2,1)} %rest_0_.17, f32[128,1024]{1,0:T(8,128)} %collective-permute-done.8.rest_1_, f32[128,3072]{1,0:T(8,128)} %collective-permute-done.9.rest_2_), custom_call_target="tpu_custom_call" | custom-call | flops 4294967296 | bytes 34603008 | tf_op jit(solution)/shard_map/out_own/pallas_call | solution.py:447
  231.3 17.4 %out_own.8 = (bf16[512,8192]{1,0:T(8,128)(2,1)}, bf16[128,4096]{1,0:T(8,128)(2,1)}) custom-call(bf16[128,4096]{1,0:T(8,128)(2,1)} %get-tuple-element.48.o_hbm, bf16[4096,8192]{1,0:T(8,128)(2,1)} %w_hbm.33, bf16[512,8192]{1,0:T(8,128)(2,1)} %rest_0_.17, f32[128,1024]{1,0:T(8,128)} %collective-permute-done.6.rest_1_, ...), custom_call_target="tpu_custom_call", output_to_operand_aliasing={{0}: (5, {})} | custom-call | flops 4294967296 | bytes 34603008 | tf_op jit(solution)/shard_map/out_own/pallas_call | solution.py:447
  251.4 17.5 %out_own.9 = (bf16[512,8192]{1,0:T(8,128)(2,1)}, bf16[128,4096]{1,0:T(8,128)(2,1)}) custom-call(bf16[128,4096]{1,0:T(8,128)(2,1)} %get-tuple-element.46.o_hbm, bf16[4096,8192]{1,0:T(8,128)(2,1)} %w_hbm.33, bf16[512,8192]{1,0:T(8,128)(2,1)} %rest_0_.17, f32[128,1024]{1,0:T(8,128)} %collective-permute-done.4.rest_1_, ...), custom_call_target="tpu_custom_call", output_to_operand_aliasing={{0}: (5, {})} | custom-call | flops 4294967296 | bytes 34603008 | tf_op jit(solution)/shard_map/out_own/pallas_call | solution.py:447
  269.7 4.0 %out_send.7 = f32[128,512]{1,0:T(8,128)} custom-call(bf16[128,4096]{1,0:T(8,128)(2,1)} %get-tuple-element.43.o_hbm, bf16[4096,8192]{1,0:T(8,128)(2,1)} %w_hbm.33), custom_call_target="tpu_custom_call" | custom-call | flops 536870912 | bytes 5242880 | tf_op jit(solution)/shard_map/out_send/pallas_call | solution.py:447
  274.9 4.0 %out_send.6 = f32[128,512]{1,0:T(8,128)} custom-call(bf16[128,4096]{1,0:T(8,128)(2,1)} %get-tuple-element.43.o_hbm, bf16[4096,8192]{1,0:T(8,128)(2,1)} %w_hbm.33), custom_call_target="tpu_custom_call" | custom-call | flops 536870912 | bytes 5242880 | tf_op jit(solution)/shard_map/out_send/pallas_call | solution.py:447
  278.9 9.2 %out_own.10 = (bf16[512,8192]{1,0:T(8,128)(2,1)}, bf16[128,2048]{1,0:T(8,128)(2,1)}) custom-call(bf16[128,4096]{1,0:T(8,128)(2,1)} %get-tuple-element.43.o_hbm, bf16[4096,8192]{1,0:T(8,128)(2,1)} %w_hbm.33, bf16[512,8192]{1,0:T(8,128)(2,1)} %rest_0_.17, f32[128,2048]{1,0:T(8,128)} %collective-permute-done.3.rest_1_, ...), custom_call_target="tpu_custom_call", output_to_operand_aliasing={{0}: (4, {})} | custom-call | flops 2147483648 | bytes 17825792 | tf_op jit(solution)/shard_map/out_own/pallas_call | solution.py:447
  288.1 41.3 %collective-permute-done.1.rest_1_ = f32[128,512]{1,0:T(8,128)S(1)} collective-permute-done((f32[128,512]{1,0:T(8,128)}, f32[128,512]{1,0:T(8,128)S(1)}, u32[]{:S(2)}, u32[]{:S(2)}) %collective-permute-start.1) | collective-permute-done | bytes 262176 | tf_op jit(solution)/shard_map/ppermute | solution.py:503
  331.4 5.5 %out_own.11 = (bf16[512,8192]{1,0:T(8,128)(2,1)}, bf16[128,1024]{1,0:T(8,128)(2,1)}) custom-call(bf16[128,4096]{1,0:T(8,128)(2,1)} %get-tuple-element.43.o_hbm, bf16[4096,8192]{1,0:T(8,128)(2,1)} %w_hbm.33, bf16[512,8192]{1,0:T(8,128)(2,1)} %rest_0_.17, f32[128,1024]{1,0:T(8,128)} %collective-permute-done.2.rest_1_, ...), custom_call_target="tpu_custom_call", output_to_operand_aliasing={{0}: (4, {})} | custom-call | flops 1073741824 | bytes 9437184 | tf_op jit(solution)/shard_map/out_own/pallas_call | solution.py:447
  337.0 4.1 %out_own.12 = (bf16[512,8192]{1,0:T(8,128)(2,1)}, bf16[128,512]{1,0:T(8,128)(2,1)}) custom-call(bf16[128,4096]{1,0:T(8,128)(2,1)} %get-tuple-element.43.o_hbm, bf16[4096,8192]{1,0:T(8,128)(2,1)} %w_hbm.33, bf16[512,8192]{1,0:T(8,128)(2,1)} %rest_0_.17, f32[128,512]{1,0:T(8,128)} %copy-done.5, ...), custom_call_target="tpu_custom_call", output_to_operand_aliasing={{0}: (4, {})} | custom-call | flops 536870912 | bytes 5242880 | tf_op jit(solution)/shard_map/out_own/pallas_call | solution.py:447
  341.6 4.1 %out_own.13 = (bf16[512,8192]{1,0:T(8,128)(2,1)}, bf16[128,512]{1,0:T(8,128)(2,1)}) custom-call(bf16[128,4096]{1,0:T(8,128)(2,1)} %get-tuple-element.43.o_hbm, bf16[4096,8192]{1,0:T(8,128)(2,1)} %w_hbm.33, bf16[512,8192]{1,0:T(8,128)(2,1)} %rest_0_.17, f32[128,512]{1,0:T(8,128)} %collective-permute-done.rest_1_, ...), custom_call_target="tpu_custom_call", output_to_operand_aliasing={{0}: (4, {})} | custom-call | flops 536870912 | bytes 5242880 | tf_op jit(solution)/shard_map/out_own/pallas_call | solution.py:447
  352.7 2.0 place.7.y_in
  354.8 2.0 place.8.y_in
  (59 shorter events, 28.0 us)
Async XLA Ops:
  56.6 153.6 %collective-permute-start.9 = (f32[128,3072]{1,0:T(8,128)}, f32[128,3072]{1,0:T(8,128)}, u32[]{:S(2)}, u32[]{:S(2)}) collective-permute-start(f32[128,3072]{1,0:T(8,128)} %out_send.11), channel_id=1, source_target_pairs={{0,4},{4,0},{1,5},{5,1},{2,6},{6,2},{3,7},{7,3}} | collective-permute-start | bytes 4718600 | tf_op jit(solution)/shard_map/ppermute | solution.py:503
  58.1 151.6 %collective-permute-start.8 = (f32[128,1024]{1,0:T(8,128)}, f32[128,1024]{1,0:T(8,128)}, u32[]{:S(2)}, u32[]{:S(2)}) collective-permute-start(f32[128,1024]{1,0:T(8,128)} %get-tuple-element.52), channel_id=1, source_target_pairs={{0,4},{4,0},{1,5},{5,1},{2,6},{6,2},{3,7},{7,3}} | collective-permute-start | bytes 1572872 | tf_op jit(solution)/shard_map/ppermute | solution.py:503
  106.2 123.7 %collective-permute-start.7 = (f32[128,3072]{1,0:T(8,128)}, f32[128,3072]{1,0:T(8,128)S(1)}, u32[]{:S(2)}, u32[]{:S(2)}) collective-permute-start(f32[128,3072]{1,0:T(8,128)} %out_send.10), channel_id=1, source_target_pairs={{0,4},{4,0},{1,5},{5,1},{2,6},{6,2},{3,7},{7,3}} | collective-permute-start | bytes 4718600 | tf_op jit(solution)/shard_map/ppermute | solution.py:503
  107.8 121.5 %collective-permute-start.6 = (f32[128,1024]{1,0:T(8,128)}, f32[128,1024]{1,0:T(8,128)}, u32[]{:S(2)}, u32[]{:S(2)}) collective-permute-start(f32[128,1024]{1,0:T(8,128)} %get-tuple-element.49), channel_id=1, source_target_pairs={{0,4},{4,0},{1,5},{5,1},{2,6},{6,2},{3,7},{7,3}} | collective-permute-start | bytes 1572872 | tf_op jit(solution)/shard_map/ppermute | solution.py:503
  163.5 86.7 %collective-permute-start.5 = (f32[128,3072]{1,0:T(8,128)}, f32[128,3072]{1,0:T(8,128)S(1)}, u32[]{:S(2)}, u32[]{:S(2)}) collective-permute-start(f32[128,3072]{1,0:T(8,128)} %out_send.9), channel_id=1, source_target_pairs={{0,4},{4,0},{1,5},{5,1},{2,6},{6,2},{3,7},{7,3}} | collective-permute-start | bytes 4718600 | tf_op jit(solution)/shard_map/ppermute | solution.py:503
  209.7 39.0 %collective-permute-start.4 = (f32[128,1024]{1,0:T(8,128)}, f32[128,1024]{1,0:T(8,128)}, u32[]{:S(2)}, u32[]{:S(2)}) collective-permute-start(f32[128,1024]{1,0:T(8,128)} %get-tuple-element.47), channel_id=1, source_target_pairs={{0,4},{4,0},{1,5},{5,1},{2,6},{6,2},{3,7},{7,3}} | collective-permute-start | bytes 1572872 | tf_op jit(solution)/shard_map/ppermute | solution.py:503
  210.2 19.0 %copy-start.4 = (f32[128,1024]{1,0:T(8,128)S(1)}, f32[128,1024]{1,0:T(8,128)}, u32[]{:S(2)}) copy-start(f32[128,1024]{1,0:T(8,128)} %out_send.8) | copy-start | bytes 1572868
  210.2 63.4 %collective-permute-start.3 = (f32[128,2048]{1,0:T(8,128)}, f32[128,2048]{1,0:T(8,128)}, u32[]{:S(2)}, u32[]{:S(2)}) collective-permute-start(f32[128,2048]{1,0:T(8,128)} %get-tuple-element.44), channel_id=1, source_target_pairs={{0,4},{4,0},{1,5},{5,1},{2,6},{6,2},{3,7},{7,3}} | collective-permute-start | bytes 3145736 | tf_op jit(solution)/shard_map/ppermute | solution.py:503
  229.3 100.6 %collective-permute-start.2 = (f32[128,1024]{1,0:T(8,128)S(1)}, f32[128,1024]{1,0:T(8,128)}, u32[]{:S(2)}, u32[]{:S(2)}) collective-permute-start(f32[128,1024]{1,0:T(8,128)S(1)} %copy-done.4), channel_id=1, source_target_pairs={{0,4},{4,0},{1,5},{5,1},{2,6},{6,2},{3,7},{7,3}} | collective-permute-start | bytes 1572872 | tf_op jit(solution)/shard_map/ppermute | solution.py:503
  229.9 1.4 copy-start.2
  229.9 115.8 %collective-permute-start.16 = (bf16[128,4096]{1,0:T(8,128)(2,1)}, bf16[128,4096]{1,0:T(8,128)(2,1)}, u32[]{:S(2)}, u32[]{:S(2)}) collective-permute-start(bf16[128,4096]{1,0:T(8,128)(2,1)} %get-tuple-element.65), channel_id=1, source_target_pairs={{0,4},{4,0},{1,5},{5,1},{2,6},{6,2},{3,7},{7,3}} | collective-permute-start | bytes 3145736 | tf_op jit(solution)/shard_map/ppermute | solution.py:503
  248.8 98.5 %collective-permute-start.15 = (bf16[128,4096]{1,0:T(8,128)(2,1)}, bf16[128,4096]{1,0:T(8,128)(2,1)}, u32[]{:S(2)}, u32[]{:S(2)}) collective-permute-start(bf16[128,4096]{1,0:T(8,128)(2,1)} %get-tuple-element.64), channel_id=1, source_target_pairs={{0,4},{4,0},{1,5},{5,1},{2,6},{6,2},{3,7},{7,3}} | collective-permute-start | bytes 3145736 | tf_op jit(solution)/shard_map/ppermute | solution.py:503
  268.8 6.1 %copy-start = (bf16[256,1024]{1,0:T(8,128)(2,1)S(1)}, bf16[256,1024]{1,0:T(8,128)(2,1)}, u32[]{:S(2)}) copy-start(bf16[256,1024]{1,0:T(8,128)(2,1)} %get-tuple-element.35.rest_0_) | copy-start | bytes 1572868
  268.8 88.0 %collective-permute-start.14 = (bf16[128,4096]{1,0:T(8,128)(2,1)}, bf16[128,4096]{1,0:T(8,128)(2,1)S(1)}, u32[]{:S(2)}, u32[]{:S(2)}) collective-permute-start(bf16[128,4096]{1,0:T(8,128)(2,1)} %get-tuple-element.63), channel_id=1, source_target_pairs={{0,4},{4,0},{1,5},{5,1},{2,6},{6,2},{3,7},{7,3}} | collective-permute-start | bytes 3145736 | tf_op jit(solution)/shard_map/ppermute | solution.py:503
  273.7 55.7 %collective-permute-start.1 = (f32[128,512]{1,0:T(8,128)}, f32[128,512]{1,0:T(8,128)S(1)}, u32[]{:S(2)}, u32[]{:S(2)}) collective-permute-start(f32[128,512]{1,0:T(8,128)} %out_send.7), channel_id=1, source_target_pairs={{0,4},{4,0},{1,5},{5,1},{2,6},{6,2},{3,7},{7,3}} | collective-permute-start | bytes 786440 | tf_op jit(solution)/shard_map/ppermute | solution.py:503
  278.9 52.5 %copy-start.1 = (bf16[256,1024]{1,0:T(8,128)(2,1)S(1)}, bf16[256,1024]{1,0:T(8,128)(2,1)}, u32[]{:S(2)}) copy-start(bf16[256,1024]{1,0:T(8,128)(2,1)} %get-tuple-element.39.rest_4_) | copy-start | bytes 1572868
  329.4 7.6 %copy-start.5 = (f32[128,512]{1,0:T(8,128)}, f32[128,512]{1,0:T(8,128)S(1)}, u32[]{:S(2)}) copy-start(f32[128,512]{1,0:T(8,128)S(1)} %collective-permute-done.1.rest_1_) | copy-start | bytes 786436
  329.4 11.7 %collective-permute-start = (f32[128,512]{1,0:T(8,128)}, f32[128,512]{1,0:T(8,128)}, u32[]{:S(2)}, u32[]{:S(2)}) collective-permute-start(f32[128,512]{1,0:T(8,128)} %out_send.6), channel_id=1, source_target_pairs={{0,4},{4,0},{1,5},{5,1},{2,6},{6,2},{3,7},{7,3}} | collective-permute-start | bytes 786440 | tf_op jit(solution)/shard_map/ppermute | solution.py:503
  329.9 28.1 %collective-permute-start.13 = (bf16[128,2048]{1,0:T(8,128)(2,1)}, bf16[128,2048]{1,0:T(8,128)(2,1)S(1)}, u32[]{:S(2)}, u32[]{:S(2)}) collective-permute-start(bf16[128,2048]{1,0:T(8,128)(2,1)} %get-tuple-element.62), channel_id=1, source_target_pairs={{0,4},{4,0},{1,5},{5,1},{2,6},{6,2},{3,7},{7,3}} | collective-permute-start | bytes 1572872 | tf_op jit(solution)/shard_map/ppermute | solution.py:503
  336.9 4.1 %copy-start.6 = (bf16[128,1024]{1,0:T(8,128)(2,1)S(1)}, bf16[128,1024]{1,0:T(8,128)(2,1)}, u32[]{:S(2)}) copy-start(bf16[128,1024]{1,0:T(8,128)(2,1)} %get-tuple-element.61) | copy-start | bytes 786436
  341.1 17.7 %collective-permute-start.12 = (bf16[128,1024]{1,0:T(8,128)(2,1)S(1)}, bf16[128,1024]{1,0:T(8,128)(2,1)S(1)}, u32[]{:S(2)}, u32[]{:S(2)}) collective-permute-start(bf16[128,1024]{1,0:T(8,128)(2,1)S(1)} %copy-done.6), channel_id=1, source_target_pairs={{0,4},{4,0},{1,5},{5,1},{2,6},{6,2},{3,7},{7,3}} | collective-permute-start | bytes 786440 | tf_op jit(solution)/shard_map/ppermute | solution.py:503
  341.6 4.1 %copy-start.7 = (bf16[128,512]{1,0:T(8,128)(2,1)S(1)}, bf16[128,512]{1,0:T(8,128)(2,1)}, u32[]{:S(2)}) copy-start(bf16[128,512]{1,0:T(8,128)(2,1)} %get-tuple-element.60) | copy-start | bytes 393220
  345.7 13.8 %collective-permute-start.11 = (bf16[128,512]{1,0:T(8,128)(2,1)S(1)}, bf16[128,512]{1,0:T(8,128)(2,1)S(1)}, u32[]{:S(2)}, u32[]{:S(2)}) collective-permute-start(bf16[128,512]{1,0:T(8,128)(2,1)S(1)} %copy-done.7), channel_id=1, source_target_pairs={{0,4},{4,0},{1,5},{5,1},{2,6},{6,2},{3,7},{7,3}} | collective-permute-start | bytes 393224 | tf_op jit(solution)/shard_map/ppermute | solution.py:503
  347.3 12.9 %collective-permute-start.10 = (bf16[128,512]{1,0:T(8,128)(2,1)}, bf16[128,512]{1,0:T(8,128)(2,1)S(1)}, u32[]{:S(2)}, u32[]{:S(2)}) collective-permute-start(bf16[128,512]{1,0:T(8,128)(2,1)} %get-tuple-element.59), channel_id=1, source_target_pairs={{0,4},{4,0},{1,5},{5,1},{2,6},{6,2},{3,7},{7,3}} | collective-permute-start | bytes 393224 | tf_op jit(solution)/shard_map/ppermute | solution.py:503
  (1 other events, 1.2 us)

commit v4 on v3

--- a/solution.py
+++ b/solution.py
@@ -31,12 +31,14 @@
     q_cols = w_q.shape[1]
     bn = kv_cols
     nq = q_cols // bn
-    slots = 4
+    slots = 8
+    ahead = 4
+    deep = d_model // 2
     xr = 64
     rows = 2 * ROWS if with_kv else ROWS
     nx = rows // xr
     step = 32
-    lead = 2 if with_kv else 0
+    lead = 4 if with_kv else 0
 
     def kernel(x_hbm, gain_ref, pos_ref, freq_ref, wq_hbm, *rest):
         if with_kv:
@@ -56,15 +58,15 @@
         for copy in x_copies:
             copy.start()
 
-        def q_load(b):
-            slot = lax.rem(b + lead, slots)
-            return pltpu.make_async_copy(wq_hbm.at[:, pl.ds(pl.multiple_of(b * bn, bn), bn)], ring.at[slot], w_sem.at[slot])
-
-        kv_loads = [pltpu.make_async_copy(w_hbm, ring.at[n], w_sem.at[n]) for n, w_hbm in enumerate((wk_hbm, wv_hbm))] if with_kv else []
-        for load in kv_loads:
-            load.start()
-        for b in range(slots - lead):
-            q_load(b).start()
+        def q_load(b, part):
+            slot = lax.rem(2 * b + part + lead, slots)
+            return pltpu.make_async_copy(wq_hbm.at[pl.ds(part * deep, deep), pl.ds(pl.multiple_of(b * bn, bn), bn)], ring.at[slot], w_sem.at[slot])
+
+        def load(u):
+            if u >= lead:
+                return q_load((u - lead) // 2, u % 2)
+            w_hbm = (wk_hbm, wv_hbm)[u // 2]
+            return pltpu.make_async_copy(w_hbm.at[pl.ds((u % 2) * deep, deep)], ring.at[u], w_sem.at[u])
 
         half_dim = HEAD // 2
         freq2_ref[:, :half_dim] = freq_ref[...]
@@ -75,6 +77,9 @@
             angle = jnp.transpose(jnp.broadcast_to(pos_row, (LANES, LANES))) * freq2_ref[...]
             cos_ref[b * LANES:(b + 1) * LANES, :] = jnp.cos(angle)
             sin_ref[b * LANES:(b + 1) * LANES, :] = jnp.sin(angle) * sign
+
+        load(0).start()
+        load(1).start()
 
         def norm(r, carry):
             at = pl.ds(pl.multiple_of(r * step, step), step)
@@ -88,22 +93,28 @@
                 h_ref[at, cols] = (x_buf[at, cols].astype(F32) * inv * gain_ref[:, cols]).astype(BF16)
             return carry
 
-        def norm_part(i, carry):
-            pltpu.make_async_copy(x_hbm.at[pl.ds(group * ROWS + i * xr, xr)], x_buf.at[pl.ds(i * xr, xr)], x_sem.at[i]).wait()
-            return lax.fori_loop(i * (xr // step), (i + 1) * (xr // step), norm, carry)
-
-        lax.fori_loop(0, nx, norm_part, 0)
+        for i in range(nx):
+            x_copies[i].wait()
+        load(2).start()
+        load(3).start()
+        lax.fori_loop(0, rows // step, norm, 0)
+
+        def product(lhs_rows, slots_of, waits, after):
+            acc = None
+            for part in range(2):
+                waits(part)
+                after(part)
+                half_acc = jnp.dot(h_ref[:lhs_rows, part * deep:(part + 1) * deep], ring[slots_of(part)], preferred_element_type=F32)
+                acc = half_acc if acc is None else acc + half_acc
+            return acc
 
         if with_kv:
-            kv_loads[0].wait()
-            acc = jnp.dot(h_ref[...], ring[0], preferred_element_type=F32)
-            for g in range(bn // HEAD):
-                cols = slice(g * HEAD, (g + 1) * HEAD)
-                kv_ref[:, cols] = rope_head(acc[:, cols], cos_ref[...], sin_ref[...])
-            q_load(slots - 2).start()
-            kv_loads[1].wait()
-            kv_ref[:, kv_cols:] = jnp.dot(h_ref[...], ring[1], preferred_element_type=F32).astype(BF16)
-            q_load(slots - 1).start()
+            for n in range(2):
+                acc = product(rows, lambda part: 2 * n + part, lambda part: load(2 * n + part).wait(), lambda part: load(2 * n + part + ahead).start())
+                for g in range(bn // HEAD):
+                    cols = slice(g * HEAD, (g + 1) * HEAD)
+                    to = slice(n * kv_cols + g * HEAD, n * kv_cols + (g + 1) * HEAD)
+                    kv_ref[:, to] = rope_head(acc[:, cols], cos_ref[...], sin_ref[...]) if n == 0 else acc[:, cols].astype(BF16)
             pl.semaphore_wait(barrier, 2)
             sends = []
             for n, (dst, peer) in enumerate(((r2, across), (r1, core))):
@@ -116,14 +127,12 @@
             return pltpu.make_async_copy(q_buf.at[:, cols], q_hbm.at[:, cols], q_sem.at[b])
 
         def q_block(b, carry):
-            slot = lax.rem(b + lead, slots)
-            q_load(b).wait()
-            acc = jnp.dot(h_ref[:ROWS], ring[slot], preferred_element_type=F32)
-
-            @pl.when(b + slots < nq)
-            def _():
-                q_load(b + slots).start()
-
+            def after(part):
+                @pl.when(b + ahead // 2 < nq)
+                def _():
+                    q_load(b + ahead // 2, part).start()
+
+            acc = product(ROWS, lambda part: lax.rem(2 * b + part + lead, slots), lambda part: q_load(b, part).wait(), after)
             for g in range(bn // HEAD):
                 at = pl.ds(pl.multiple_of(b * bn + g * HEAD, HEAD), HEAD)
                 q_buf[:, at] = rope_head(acc[:, g * HEAD:(g + 1) * HEAD], cos_ref[:ROWS], sin_ref[:ROWS])
@@ -150,13 +159,13 @@
     return pl.pallas_call(
         kernel,
         grid=(1,),
-        in_specs=[any_spec(), whole(gain), whole(pos2), whole(inv_freq), any_spec()] + [any_spec()] * lead,
+        in_specs=[any_spec(), whole(gain), whole(pos2), whole(inv_freq), any_spec()] + [any_spec()] * (2 if with_kv else 0),
         out_specs=[any_spec()] + ([pl.BlockSpec(kv_shape.shape, lambda i: (0, 0)), any_spec(), any_spec(), any_spec()] if with_kv else []),
         out_shape=[jax.ShapeDtypeStruct((ROWS, q_cols), BF16)] + kv_out,
         scratch_shapes=[
             pltpu.VMEM((rows, d_model), BF16),
             pltpu.VMEM((rows, d_model), BF16),
-            pltpu.VMEM((slots, d_model, bn), BF16),
+            pltpu.VMEM((slots, deep, bn), BF16),
             pltpu.VMEM((ROWS, q_cols), BF16),
             pltpu.VMEM((rows, HEAD), F32),
             pltpu.VMEM((rows, HEAD), F32),
@@ -207,10 +216,10 @@
             at = pl.ds(pl.multiple_of((1 - tp) * half_cols + j * bn, bn), bn)
             return pltpu.make_async_copy(w_hbm.at[:, at], w_buf.at[j], w_sem.at[j])
 
+        for copy in copies:
+            copy.wait()
         for j in range(cols // bn):
             w_copy(j).start()
-        for copy in copies:
-            copy.wait()
         piece = dev if half == 0 else 2 * cp_size - 1 - dev
         lane = lax.broadcasted_iota(jnp.int32, (qb, LANES), 1)
         t0 = piece * rows + (row_group % 2) * qb
@@ -410,8 +419,8 @@
                 extra.append(pltpu.make_async_copy(recv, r_buf.at[:, starts[n]:starts[n] + recv.shape[1]], r_sem.at[n]))
             for copy in extra:
                 copy.start()
-        for j in range(1, nb):
-            w_copy(j).start()
+        if nb > 1:
+            w_copy(1).start()
         o_copy.wait()
         for copy in extra:
             copy.wait()
@@ -419,6 +428,11 @@
         def block(j, carry):
             at = pl.ds(pl.multiple_of(j * bn, bn), bn)
             w_copy(j).wait()
+
+            @pl.when(j + 2 < nb)
+            def _():
+                w_copy(j + 2).start()
+
             acc = jnp.dot(o_buf[...], w_buf[j], preferred_element_type=F32)
             if own:
                 c_buf[:, at] = (x_buf[:, at].astype(F32) + (acc + r_buf[:, at])).astype(BF16)

time: 362 us -> 348 us (0.961)
  Pallas kernels: 295 us -> 269 us
  waiting for transfers between devices: 41.3 us -> 51.4 us
    pallas_call x13, Pallas kernels: 126 us -> 111 us  [out_cols(): pl.pallas_call(kernel, grid=(1,), in_specs=[any_spec()] * len(ins), out_s...]
    ppermute x17, waiting for transfers between devices: 41.3 us -> 51.4 us  [swap(): return lax.ppermute(value, 'tp', swap_tp)]
    pallas_call x4, Pallas kernels: 45.9 us -> 39.4 us  [attend_send(): pl.pallas_call(kernel, grid_spec=pltpu.PrefetchScalarGridSpec(num_scalar_...]
  transfers between devices with their start and end apart: 17 -> 17, of which waited for: 1 -> 1; matrix products, arithmetic and copies ran while one was open for 1% -> 1% of each run, Pallas kernels for 66% -> 63%
where the time goes in v4:
time: 348 us; the launch traced here: 347 us
  Pallas kernels  269 us (77%)
  waiting for transfers between devices  51.4 us (15%)
  starting transfers between devices  19.2 us (6%)
  local copies, waits for them, and re-layouts  6.26 us (2%)
    pallas_call x4, Pallas kernels, front(): pl.pallas_call(kernel, grid=(1,), in_specs=[any_spec(), whole(gain), whol...  111 us
    pallas_call x13, Pallas kernels, out_cols(): pl.pallas_call(kernel, grid=(1,), in_specs=[any_spec()] * len(ins), out_s...  111 us
    ppermute x17, waiting for transfers between devices, swap(): return lax.ppermute(value, 'tp', swap_tp)  51.4 us
    pallas_call x4, Pallas kernels, attend_send(): pl.pallas_call(kernel, grid_spec=pltpu.PrefetchScalarGridSpec(num_scalar_...  39.4 us
    ppermute x17, starting transfers between devices, swap(): return lax.ppermute(value, 'tp', swap_tp)  19.2 us
    pallas_call x7, Pallas kernels, place(): pl.pallas_call(kernel, grid_spec=pltpu.PrefetchScalarGridSpec(num_scalar_...  8.06 us
  transfers between devices with their start and end apart: 17, of which 1 were waited for; matrix products, arithmetic and copies ran while one was open for 1% of the time, Pallas kernels for 63%

profile of v4, /device:TPU:0, one launch (start us, length us, event | category | flops | bytes accessed | tf_op | source)
XLA Modules:
  0.0 347.2 jit_solution(1866583831972127692)
XLA Ops:
  0.6 31.2 %front.5 = (bf16[128,4096]{1,0:T(8,128)(2,1)}, bf16[256,1024]{1,0:T(8,128)(2,1)}, bf16[256,1024]{1,0:T(8,128)(2,1)}, bf16[256,1024]{1,0:T(8,128)(2,1)}, bf16[256,1024]{1,0:T(8,128)(2,1)}) custom-call(bf16[512,8192]{1,0:T(8,128)(2,1)} %rest_0_.17, f32[1,8192]{1,0:T(1,128)} %bitcast.4, s32[4,128]{1,0:T(4,128)} %bitcast.8, f32[1,64]{1,0:T(1,128)} %bitcast.16, ...), custom_call_target="tpu_custom_call" | custom-call | flops 21474836480 | bytes 71303168 | tf_op jit(solution)/shard_map/front/pallas_call | solution.py:159
  31.8 8.4 %attend_send.7 = (bf16[128,4096]{1,0:T(8,128)(2,1)}, f32[128,1024]{1,0:T(8,128)}) custom-call(s32[512]{0:T(512)} %pos_ref.7, s32[4,128]{1,0:T(4,128)} %bitcast.9, bf16[128,4096]{1,0:T(8,128)(2,1)} %get-tuple-element.50.q_hbm, bf16[4096,8192]{1,0:T(8,128)(2,1)} %w_hbm.33, bf16[256,1024]{1,0:T(8,128)(2,1)} %get-tuple-element.35.rest_0_, ...), custom_call_target="tpu_custom_call" | custom-call | flops 2147483648 | bytes 8388608 | tf_op jit(solution)/shard_map/attend_send/pallas_call | solution.py:350
  40.2 10.7 %out_send.11 = f32[128,3072]{1,0:T(8,128)} custom-call(bf16[128,4096]{1,0:T(8,128)(2,1)} %get-tuple-element.51.o_hbm, bf16[4096,8192]{1,0:T(8,128)(2,1)} %w_hbm.33), custom_call_target="tpu_custom_call" | custom-call | flops 3221225472 | bytes 26214400 | tf_op jit(solution)/shard_map/out_send/pallas_call | solution.py:461
  50.9 3.4 collective-permute-start.9
  54.3 24.5 %front.7.q_hbm = bf16[128,4096]{1,0:T(8,128)(2,1)} custom-call(bf16[512,8192]{1,0:T(8,128)(2,1)} %rest_0_.17, f32[1,8192]{1,0:T(1,128)} %bitcast.5, s32[4,128]{1,0:T(4,128)} %bitcast.10, f32[1,64]{1,0:T(1,128)} %bitcast.17, bf16[8192,4096]{1,0:T(8,128)(2,1)} %wq_hbm.7), custom_call_target="tpu_custom_call" | custom-call | flops 10737418240 | bytes 69206016 | tf_op jit(solution)/shard_map/front/pallas_call | solution.py:159
  78.8 9.2 %attend_send.6 = (bf16[128,4096]{1,0:T(8,128)(2,1)}, f32[128,1024]{1,0:T(8,128)}) custom-call(s32[512]{0:T(512)} %pos_ref.7, s32[4,128]{1,0:T(4,128)} %bitcast.11, bf16[128,4096]{1,0:T(8,128)(2,1)} %front.7.q_hbm, bf16[4096,8192]{1,0:T(8,128)(2,1)} %w_hbm.33, bf16[256,1024]{1,0:T(8,128)(2,1)} %get-tuple-element.35.rest_0_, ...), custom_call_target="tpu_custom_call" | custom-call | flops 2147483648 | bytes 8388608 | tf_op jit(solution)/shard_map/attend_send/pallas_call | solution.py:350
  88.0 10.7 %out_send.10 = f32[128,3072]{1,0:T(8,128)} custom-call(bf16[128,4096]{1,0:T(8,128)(2,1)} %get-tuple-element.48.o_hbm, bf16[4096,8192]{1,0:T(8,128)(2,1)} %w_hbm.33), custom_call_target="tpu_custom_call" | custom-call | flops 3221225472 | bytes 26214400 | tf_op jit(solution)/shard_map/out_send/pallas_call | solution.py:461
  100.8 31.2 %front.6 = (bf16[128,4096]{1,0:T(8,128)(2,1)}, bf16[256,1024]{1,0:T(8,128)(2,1)}, bf16[256,1024]{1,0:T(8,128)(2,1)}, bf16[256,1024]{1,0:T(8,128)(2,1)}, bf16[256,1024]{1,0:T(8,128)(2,1)}) custom-call(bf16[512,8192]{1,0:T(8,128)(2,1)} %rest_0_.17, f32[1,8192]{1,0:T(1,128)} %bitcast.6, s32[4,128]{1,0:T(4,128)} %bitcast.12, f32[1,64]{1,0:T(1,128)} %bitcast.18, ...), custom_call_target="tpu_custom_call" | custom-call | flops 21474836480 | bytes 71303168 | tf_op jit(solution)/shard_map/front/pallas_call | solution.py:159
  132.0 9.9 %attend_send.5 = (bf16[128,4096]{1,0:T(8,128)(2,1)}, f32[128,1024]{1,0:T(8,128)}) custom-call(s32[512]{0:T(512)} %pos_ref.7, s32[4,128]{1,0:T(4,128)} %bitcast.13, bf16[128,4096]{1,0:T(8,128)(2,1)} %get-tuple-element.45.q_hbm, bf16[4096,8192]{1,0:T(8,128)(2,1)} %w_hbm.33, bf16[256,1024]{1,0:T(8,128)(2,1)} %get-tuple-element.35.rest_0_, ...), custom_call_target="tpu_custom_call" | custom-call | flops 2147483648 | bytes 8388608 | tf_op jit(solution)/shard_map/attend_send/pallas_call | solution.py:350
  141.9 10.7 %out_send.9 = f32[128,3072]{1,0:T(8,128)} custom-call(bf16[128,4096]{1,0:T(8,128)(2,1)} %get-tuple-element.46.o_hbm, bf16[4096,8192]{1,0:T(8,128)(2,1)} %w_hbm.33), custom_call_target="tpu_custom_call" | custom-call | flops 3221225472 | bytes 26214400 | tf_op jit(solution)/shard_map/out_send/pallas_call | solution.py:461
  154.7 24.5 %front.4.q_hbm = bf16[128,4096]{1,0:T(8,128)(2,1)} custom-call(bf16[512,8192]{1,0:T(8,128)(2,1)} %rest_0_.17, f32[1,8192]{1,0:T(1,128)} %bitcast.7, s32[4,128]{1,0:T(4,128)} %bitcast.14, f32[1,64]{1,0:T(1,128)} %bitcast.19, bf16[8192,4096]{1,0:T(8,128)(2,1)} %wq_hbm.7), custom_call_target="tpu_custom_call" | custom-call | flops 10737418240 | bytes 69206016 | tf_op jit(solution)/shard_map/front/pallas_call | solution.py:159
  179.2 11.9 %attend_send.4 = (bf16[128,4096]{1,0:T(8,128)(2,1)}, f32[128,2048]{1,0:T(8,128)}) custom-call(s32[512]{0:T(512)} %pos_ref.7, s32[4,128]{1,0:T(4,128)} %bitcast.15, bf16[128,4096]{1,0:T(8,128)(2,1)} %front.4.q_hbm, bf16[4096,8192]{1,0:T(8,128)(2,1)} %w_hbm.33, bf16[256,1024]{1,0:T(8,128)(2,1)} %get-tuple-element.35.rest_0_, ...), custom_call_target="tpu_custom_call" | custom-call | flops 3221225472 | bytes 16777216 | tf_op jit(solution)/shard_map/attend_send/pallas_call | solution.py:350
  191.0 5.3 %out_send.8 = f32[128,1024]{1,0:T(8,128)} custom-call(bf16[128,4096]{1,0:T(8,128)(2,1)} %get-tuple-element.43.o_hbm, bf16[4096,8192]{1,0:T(8,128)(2,1)} %w_hbm.33), custom_call_target="tpu_custom_call" | custom-call | flops 1073741824 | bytes 9437184 | tf_op jit(solution)/shard_map/out_send/pallas_call | solution.py:461
  198.4 14.4 %out_own.7 = (bf16[512,8192]{1,0:T(8,128)(2,1)}, bf16[128,4096]{1,0:T(8,128)(2,1)}) custom-call(bf16[128,4096]{1,0:T(8,128)(2,1)} %get-tuple-element.51.o_hbm, bf16[4096,8192]{1,0:T(8,128)(2,1)} %w_hbm.33, bf16[512,8192]{1,0:T(8,128)(2,1)} %rest_0_.17, f32[128,1024]{1,0:T(8,128)} %collective-permute-done.8.rest_1_, f32[128,3072]{1,0:T(8,128)} %collective-permute-done.9.rest_2_), custom_call_target="tpu_custom_call" | custom-call | flops 4294967296 | bytes 34603008 | tf_op jit(solution)/shard_map/out_own/pallas_call | solution.py:461
  214.8 14.4 %out_own.8 = (bf16[512,8192]{1,0:T(8,128)(2,1)}, bf16[128,4096]{1,0:T(8,128)(2,1)}) custom-call(bf16[128,4096]{1,0:T(8,128)(2,1)} %get-tuple-element.48.o_hbm, bf16[4096,8192]{1,0:T(8,128)(2,1)} %w_hbm.33, bf16[512,8192]{1,0:T(8,128)(2,1)} %rest_0_.17, f32[128,1024]{1,0:T(8,128)} %collective-permute-done.6.rest_1_, ...), custom_call_target="tpu_custom_call", output_to_operand_aliasing={{0}: (5, {})} | custom-call | flops 4294967296 | bytes 34603008 | tf_op jit(solution)/shard_map/out_own/pallas_call | solution.py:461
  231.6 14.4 %out_own.9 = (bf16[512,8192]{1,0:T(8,128)(2,1)}, bf16[128,4096]{1,0:T(8,128)(2,1)}) custom-call(bf16[128,4096]{1,0:T(8,128)(2,1)} %get-tuple-element.46.o_hbm, bf16[4096,8192]{1,0:T(8,128)(2,1)} %w_hbm.33, bf16[512,8192]{1,0:T(8,128)(2,1)} %rest_0_.17, f32[128,1024]{1,0:T(8,128)} %collective-permute-done.4.rest_1_, ...), custom_call_target="tpu_custom_call", output_to_operand_aliasing={{0}: (5, {})} | custom-call | flops 4294967296 | bytes 34603008 | tf_op jit(solution)/shard_map/out_own/pallas_call | solution.py:461
  246.8 4.0 %out_send.7 = f32[128,512]{1,0:T(8,128)} custom-call(bf16[128,4096]{1,0:T(8,128)(2,1)} %get-tuple-element.43.o_hbm, bf16[4096,8192]{1,0:T(8,128)(2,1)} %w_hbm.33), custom_call_target="tpu_custom_call" | custom-call | flops 536870912 | bytes 5242880 | tf_op jit(solution)/shard_map/out_send/pallas_call | solution.py:461
  252.0 4.0 %out_send.6 = f32[128,512]{1,0:T(8,128)} custom-call(bf16[128,4096]{1,0:T(8,128)(2,1)} %get-tuple-element.43.o_hbm, bf16[4096,8192]{1,0:T(8,128)(2,1)} %w_hbm.33), custom_call_target="tpu_custom_call" | custom-call | flops 536870912 | bytes 5242880 | tf_op jit(solution)/shard_map/out_send/pallas_call | solution.py:461
  256.0 8.6 %out_own.10 = (bf16[512,8192]{1,0:T(8,128)(2,1)}, bf16[128,2048]{1,0:T(8,128)(2,1)}) custom-call(bf16[128,4096]{1,0:T(8,128)(2,1)} %get-tuple-element.43.o_hbm, bf16[4096,8192]{1,0:T(8,128)(2,1)} %w_hbm.33, bf16[512,8192]{1,0:T(8,128)(2,1)} %rest_0_.17, f32[128,2048]{1,0:T(8,128)} %collective-permute-done.3.rest_1_, ...), custom_call_target="tpu_custom_call", output_to_operand_aliasing={{0}: (4, {})} | custom-call | flops 2147483648 | bytes 17825792 | tf_op jit(solution)/shard_map/out_own/pallas_call | solution.py:461
  264.6 51.3 %collective-permute-done.1.rest_1_ = f32[128,512]{1,0:T(8,128)S(1)} collective-permute-done((f32[128,512]{1,0:T(8,128)}, f32[128,512]{1,0:T(8,128)S(1)}, u32[]{:S(2)}, u32[]{:S(2)}) %collective-permute-start.1) | collective-permute-done | bytes 262176 | tf_op jit(solution)/shard_map/ppermute | solution.py:517
  318.0 5.5 %out_own.11 = (bf16[512,8192]{1,0:T(8,128)(2,1)}, bf16[128,1024]{1,0:T(8,128)(2,1)}) custom-call(bf16[128,4096]{1,0:T(8,128)(2,1)} %get-tuple-element.43.o_hbm, bf16[4096,8192]{1,0:T(8,128)(2,1)} %w_hbm.33, bf16[512,8192]{1,0:T(8,128)(2,1)} %rest_0_.17, f32[128,1024]{1,0:T(8,128)} %collective-permute-done.2.rest_1_, ...), custom_call_target="tpu_custom_call", output_to_operand_aliasing={{0}: (4, {})} | custom-call | flops 1073741824 | bytes 9437184 | tf_op jit(solution)/shard_map/out_own/pallas_call | solution.py:461
  323.6 4.1 %out_own.12 = (bf16[512,8192]{1,0:T(8,128)(2,1)}, bf16[128,512]{1,0:T(8,128)(2,1)}) custom-call(bf16[128,4096]{1,0:T(8,128)(2,1)} %get-tuple-element.43.o_hbm, bf16[4096,8192]{1,0:T(8,128)(2,1)} %w_hbm.33, bf16[512,8192]{1,0:T(8,128)(2,1)} %rest_0_.17, f32[128,512]{1,0:T(8,128)} %copy-done.5, ...), custom_call_target="tpu_custom_call", output_to_operand_aliasing={{0}: (4, {})} | custom-call | flops 536870912 | bytes 5242880 | tf_op jit(solution)/shard_map/out_own/pallas_call | solution.py:461
  328.0 4.1 %out_own.13 = (bf16[512,8192]{1,0:T(8,128)(2,1)}, bf16[128,512]{1,0:T(8,128)(2,1)}) custom-call(bf16[128,4096]{1,0:T(8,128)(2,1)} %get-tuple-element.43.o_hbm, bf16[4096,8192]{1,0:T(8,128)(2,1)} %w_hbm.33, bf16[512,8192]{1,0:T(8,128)(2,1)} %rest_0_.17, f32[128,512]{1,0:T(8,128)} %collective-permute-done.rest_1_, ...), custom_call_target="tpu_custom_call", output_to_operand_aliasing={{0}: (4, {})} | custom-call | flops 536870912 | bytes 5242880 | tf_op jit(solution)/shard_map/out_own/pallas_call | solution.py:461
  339.1 2.0 place.7.y_in
  (59 shorter events, 28.2 us)
Async XLA Ops:
  50.9 145.4 %collective-permute-start.9 = (f32[128,3072]{1,0:T(8,128)}, f32[128,3072]{1,0:T(8,128)}, u32[]{:S(2)}, u32[]{:S(2)}) collective-permute-start(f32[128,3072]{1,0:T(8,128)} %out_send.11), channel_id=1, source_target_pairs={{0,4},{4,0},{1,5},{5,1},{2,6},{6,2},{3,7},{7,3}} | collective-permute-start | bytes 4718600 | tf_op jit(solution)/shard_map/ppermute | solution.py:517
  54.3 142.0 %collective-permute-start.8 = (f32[128,1024]{1,0:T(8,128)}, f32[128,1024]{1,0:T(8,128)}, u32[]{:S(2)}, u32[]{:S(2)}) collective-permute-start(f32[128,1024]{1,0:T(8,128)} %get-tuple-element.52), channel_id=1, source_target_pairs={{0,4},{4,0},{1,5},{5,1},{2,6},{6,2},{3,7},{7,3}} | collective-permute-start | bytes 1572872 | tf_op jit(solution)/shard_map/ppermute | solution.py:517
  98.8 114.1 %collective-permute-start.7 = (f32[128,3072]{1,0:T(8,128)}, f32[128,3072]{1,0:T(8,128)S(1)}, u32[]{:S(2)}, u32[]{:S(2)}) collective-permute-start(f32[128,3072]{1,0:T(8,128)} %out_send.10), channel_id=1, source_target_pairs={{0,4},{4,0},{1,5},{5,1},{2,6},{6,2},{3,7},{7,3}} | collective-permute-start | bytes 4718600 | tf_op jit(solution)/shard_map/ppermute | solution.py:517
  100.8 111.9 %collective-permute-start.6 = (f32[128,1024]{1,0:T(8,128)}, f32[128,1024]{1,0:T(8,128)}, u32[]{:S(2)}, u32[]{:S(2)}) collective-permute-start(f32[128,1024]{1,0:T(8,128)} %get-tuple-element.49), channel_id=1, source_target_pairs={{0,4},{4,0},{1,5},{5,1},{2,6},{6,2},{3,7},{7,3}} | collective-permute-start | bytes 1572872 | tf_op jit(solution)/shard_map/ppermute | solution.py:517
  152.7 77.7 %collective-permute-start.5 = (f32[128,3072]{1,0:T(8,128)}, f32[128,3072]{1,0:T(8,128)S(1)}, u32[]{:S(2)}, u32[]{:S(2)}) collective-permute-start(f32[128,3072]{1,0:T(8,128)} %out_send.9), channel_id=1, source_target_pairs={{0,4},{4,0},{1,5},{5,1},{2,6},{6,2},{3,7},{7,3}} | collective-permute-start | bytes 4718600 | tf_op jit(solution)/shard_map/ppermute | solution.py:517
  196.3 32.9 %collective-permute-start.4 = (f32[128,1024]{1,0:T(8,128)}, f32[128,1024]{1,0:T(8,128)}, u32[]{:S(2)}, u32[]{:S(2)}) collective-permute-start(f32[128,1024]{1,0:T(8,128)} %get-tuple-element.47), channel_id=1, source_target_pairs={{0,4},{4,0},{1,5},{5,1},{2,6},{6,2},{3,7},{7,3}} | collective-permute-start | bytes 1572872 | tf_op jit(solution)/shard_map/ppermute | solution.py:517
  196.4 16.4 %copy-start.4 = (f32[128,1024]{1,0:T(8,128)S(1)}, f32[128,1024]{1,0:T(8,128)}, u32[]{:S(2)}) copy-start(f32[128,1024]{1,0:T(8,128)} %out_send.8) | copy-start | bytes 1572868
  196.4 54.4 %collective-permute-start.3 = (f32[128,2048]{1,0:T(8,128)}, f32[128,2048]{1,0:T(8,128)}, u32[]{:S(2)}, u32[]{:S(2)}) collective-permute-start(f32[128,2048]{1,0:T(8,128)} %get-tuple-element.44), channel_id=1, source_target_pairs={{0,4},{4,0},{1,5},{5,1},{2,6},{6,2},{3,7},{7,3}} | collective-permute-start | bytes 3145736 | tf_op jit(solution)/shard_map/ppermute | solution.py:517
  212.7 103.5 %collective-permute-start.2 = (f32[128,1024]{1,0:T(8,128)S(1)}, f32[128,1024]{1,0:T(8,128)}, u32[]{:S(2)}, u32[]{:S(2)}) collective-permute-start(f32[128,1024]{1,0:T(8,128)S(1)} %copy-done.4), channel_id=1, source_target_pairs={{0,4},{4,0},{1,5},{5,1},{2,6},{6,2},{3,7},{7,3}} | collective-permute-start | bytes 1572872 | tf_op jit(solution)/shard_map/ppermute | solution.py:517
  212.9 1.9 copy-start.2
  212.9 119.2 %collective-permute-start.16 = (bf16[128,4096]{1,0:T(8,128)(2,1)}, bf16[128,4096]{1,0:T(8,128)(2,1)}, u32[]{:S(2)}, u32[]{:S(2)}) collective-permute-start(bf16[128,4096]{1,0:T(8,128)(2,1)} %get-tuple-element.65), channel_id=1, source_target_pairs={{0,4},{4,0},{1,5},{5,1},{2,6},{6,2},{3,7},{7,3}} | collective-permute-start | bytes 3145736 | tf_op jit(solution)/shard_map/ppermute | solution.py:517
  229.2 104.7 %collective-permute-start.15 = (bf16[128,4096]{1,0:T(8,128)(2,1)}, bf16[128,4096]{1,0:T(8,128)(2,1)}, u32[]{:S(2)}, u32[]{:S(2)}) collective-permute-start(bf16[128,4096]{1,0:T(8,128)(2,1)} %get-tuple-element.64), channel_id=1, source_target_pairs={{0,4},{4,0},{1,5},{5,1},{2,6},{6,2},{3,7},{7,3}} | collective-permute-start | bytes 3145736 | tf_op jit(solution)/shard_map/ppermute | solution.py:517
  246.0 6.1 %copy-start = (bf16[256,1024]{1,0:T(8,128)(2,1)S(1)}, bf16[256,1024]{1,0:T(8,128)(2,1)}, u32[]{:S(2)}) copy-start(bf16[256,1024]{1,0:T(8,128)(2,1)} %get-tuple-element.35.rest_0_) | copy-start | bytes 1572868
  246.0 97.3 %collective-permute-start.14 = (bf16[128,4096]{1,0:T(8,128)(2,1)}, bf16[128,4096]{1,0:T(8,128)(2,1)S(1)}, u32[]{:S(2)}, u32[]{:S(2)}) collective-permute-start(bf16[128,4096]{1,0:T(8,128)(2,1)} %get-tuple-element.63), channel_id=1, source_target_pairs={{0,4},{4,0},{1,5},{5,1},{2,6},{6,2},{3,7},{7,3}} | collective-permute-start | bytes 3145736 | tf_op jit(solution)/shard_map/ppermute | solution.py:517
  250.8 65.2 %collective-permute-start.1 = (f32[128,512]{1,0:T(8,128)}, f32[128,512]{1,0:T(8,128)S(1)}, u32[]{:S(2)}, u32[]{:S(2)}) collective-permute-start(f32[128,512]{1,0:T(8,128)} %out_send.7), channel_id=1, source_target_pairs={{0,4},{4,0},{1,5},{5,1},{2,6},{6,2},{3,7},{7,3}} | collective-permute-start | bytes 786440 | tf_op jit(solution)/shard_map/ppermute | solution.py:517
  256.0 62.0 %copy-start.1 = (bf16[256,1024]{1,0:T(8,128)(2,1)S(1)}, bf16[256,1024]{1,0:T(8,128)(2,1)}, u32[]{:S(2)}) copy-start(bf16[256,1024]{1,0:T(8,128)(2,1)} %get-tuple-element.39.rest_4_) | copy-start | bytes 1572868
  316.0 7.6 %copy-start.5 = (f32[128,512]{1,0:T(8,128)}, f32[128,512]{1,0:T(8,128)S(1)}, u32[]{:S(2)}) copy-start(f32[128,512]{1,0:T(8,128)S(1)} %collective-permute-done.1.rest_1_) | copy-start | bytes 786436
  316.0 11.7 %collective-permute-start = (f32[128,512]{1,0:T(8,128)}, f32[128,512]{1,0:T(8,128)}, u32[]{:S(2)}, u32[]{:S(2)}) collective-permute-start(f32[128,512]{1,0:T(8,128)} %out_send.6), channel_id=1, source_target_pairs={{0,4},{4,0},{1,5},{5,1},{2,6},{6,2},{3,7},{7,3}} | collective-permute-start | bytes 786440 | tf_op jit(solution)/shard_map/ppermute | solution.py:517
  316.3 28.1 %collective-permute-start.13 = (bf16[128,2048]{1,0:T(8,128)(2,1)}, bf16[128,2048]{1,0:T(8,128)(2,1)S(1)}, u32[]{:S(2)}, u32[]{:S(2)}) collective-permute-start(bf16[128,2048]{1,0:T(8,128)(2,1)} %get-tuple-element.62), channel_id=1, source_target_pairs={{0,4},{4,0},{1,5},{5,1},{2,6},{6,2},{3,7},{7,3}} | collective-permute-start | bytes 1572872 | tf_op jit(solution)/shard_map/ppermute | solution.py:517
  323.6 4.1 %copy-start.6 = (bf16[128,1024]{1,0:T(8,128)(2,1)S(1)}, bf16[128,1024]{1,0:T(8,128)(2,1)}, u32[]{:S(2)}) copy-start(bf16[128,1024]{1,0:T(8,128)(2,1)} %get-tuple-element.61) | copy-start | bytes 786436
  327.7 17.5 %collective-permute-start.12 = (bf16[128,1024]{1,0:T(8,128)(2,1)S(1)}, bf16[128,1024]{1,0:T(8,128)(2,1)S(1)}, u32[]{:S(2)}, u32[]{:S(2)}) collective-permute-start(bf16[128,1024]{1,0:T(8,128)(2,1)S(1)} %copy-done.6), channel_id=1, source_target_pairs={{0,4},{4,0},{1,5},{5,1},{2,6},{6,2},{3,7},{7,3}} | collective-permute-start | bytes 786440 | tf_op jit(solution)/shard_map/ppermute | solution.py:517
  328.0 4.1 %copy-start.7 = (bf16[128,512]{1,0:T(8,128)(2,1)S(1)}, bf16[128,512]{1,0:T(8,128)(2,1)}, u32[]{:S(2)}) copy-start(bf16[128,512]{1,0:T(8,128)(2,1)} %get-tuple-element.60) | copy-start | bytes 393220
  332.1 13.8 %collective-permute-start.11 = (bf16[128,512]{1,0:T(8,128)(2,1)S(1)}, bf16[128,512]{1,0:T(8,128)(2,1)S(1)}, u32[]{:S(2)}, u32[]{:S(2)}) collective-permute-start(bf16[128,512]{1,0:T(8,128)(2,1)S(1)} %copy-done.7), channel_id=1, source_target_pairs={{0,4},{4,0},{1,5},{5,1},{2,6},{6,2},{3,7},{7,3}} | collective-permute-start | bytes 393224 | tf_op jit(solution)/shard_map/ppermute | solution.py:517
  333.9 12.7 %collective-permute-start.10 = (bf16[128,512]{1,0:T(8,128)(2,1)}, bf16[128,512]{1,0:T(8,128)(2,1)S(1)}, u32[]{:S(2)}, u32[]{:S(2)}) collective-permute-start(bf16[128,512]{1,0:T(8,128)(2,1)} %get-tuple-element.59), channel_id=1, source_target_pairs={{0,4},{4,0},{1,5},{5,1},{2,6},{6,2},{3,7},{7,3}} | collective-permute-start | bytes 393224 | tf_op jit(solution)/shard_map/ppermute | solution.py:517
  (1 other events, 1.2 us)

commit v5 on v4

--- a/solution.py
+++ b/solution.py
@@ -10,7 +10,7 @@
 BF16 = jnp.bfloat16
 HEAD = 128
 LANES = 128
-VMEM_BYTES = 60 * 1024 * 1024
+VMEM_BYTES = 67043328
 ROWS = 128
 CHUNKS = ((1024, 3072), (1024, 3072), (1024, 3072), (2048, 1024, 512, 512))
 PLAN = (("make", 0, 0, 2), ("make", 1, 0, 2), ("own", 0, 0, 2), ("make", 2, 0, 2), ("own", 1, 0, 2), ("make", 3, 0, 4), ("own", 2, 0, 2), ("own", 3, 0, 1), ("own", 3, 1, 2), ("own", 3, 2, 3), ("own", 3, 3, 4))
@@ -68,6 +68,9 @@
             w_hbm = (wk_hbm, wv_hbm)[u // 2]
             return pltpu.make_async_copy(w_hbm.at[pl.ds((u % 2) * deep, deep)], ring.at[u], w_sem.at[u])
 
+        load(0).start()
+        load(1).start()
+
         half_dim = HEAD // 2
         freq2_ref[:, :half_dim] = freq_ref[...]
         freq2_ref[:, half_dim:] = freq_ref[...]
@@ -77,9 +80,6 @@
             angle = jnp.transpose(jnp.broadcast_to(pos_row, (LANES, LANES))) * freq2_ref[...]
             cos_ref[b * LANES:(b + 1) * LANES, :] = jnp.cos(angle)
             sin_ref[b * LANES:(b + 1) * LANES, :] = jnp.sin(angle) * sign
-
-        load(0).start()
-        load(1).start()
 
         def norm(r, carry):
             at = pl.ds(pl.multiple_of(r * step, step), step)
@@ -192,7 +192,7 @@
     k_dim = q.shape[1]
     half_cols = w_o.shape[1] // 2
     bn = 512
-    unroll = 2 if row_group == 0 else 1
+    unroll = 2 if row_group < 3 else 1
 
     def kernel(pos_ref, pos2_ref, q_hbm, w_hbm, *rest):
         kv_hbm = rest[:parts]
@@ -209,7 +209,7 @@
             at = pl.ds(pl.multiple_of(n * group * HEAD, group * HEAD), group * HEAD)
             return pltpu.make_async_copy(q_hbm.at[:, at], q_buf.at[:, at], q_sem.at[n])
 
-        for n in range(kv_heads):
+        for n in range(unroll):
             q_copy(n).start()
 
         def w_copy(j):
@@ -218,6 +218,8 @@
 
         for copy in copies:
             copy.wait()
+        for n in range(unroll, kv_heads):
+            q_copy(n).start()
         for j in range(cols // bn):
             w_copy(j).start()
         piece = dev if half == 0 else 2 * cp_size - 1 - dev

time: 348 us -> 351 us (level)
  transfers between devices with their start and end apart: 17 -> 17, of which waited for: 1 -> 1; matrix products, arithmetic and copies ran while one was open for 1% -> 2% of each run, Pallas kernels for 63% -> 63%
where the time goes in v5:
time: 351 us; the launch traced here: 350 us
  Pallas kernels  272 us (77%)
  waiting for transfers between devices  52.1 us (15%)
  starting transfers between devices  18.1 us (5%)
  local copies, waits for them, and re-layouts  6.87 us (2%)
    pallas_call x4, Pallas kernels, front(): pl.pallas_call(kernel, grid=(1,), in_specs=[any_spec(), whole(gain), whol...  111 us
    pallas_call x13, Pallas kernels, out_cols(): pl.pallas_call(kernel, grid=(1,), in_specs=[any_spec()] * len(ins), out_s...  111 us
    ppermute x17, waiting for transfers between devices, swap(): return lax.ppermute(value, 'tp', swap_tp)  52.1 us
    pallas_call x4, Pallas kernels, attend_send(): pl.pallas_call(kernel, grid_spec=pltpu.PrefetchScalarGridSpec(num_scalar_...  39.6 us
    ppermute x17, starting transfers between devices, swap(): return lax.ppermute(value, 'tp', swap_tp)  18.1 us
    pallas_call x7, Pallas kernels, place(): pl.pallas_call(kernel, grid_spec=pltpu.PrefetchScalarGridSpec(num_scalar_...  11 us
  transfers between devices with their start and end apart: 17, of which 1 were waited for; matrix products, arithmetic and copies ran while one was open for 2% of the time, Pallas kernels for 63%

profile of v5, /device:TPU:0, one launch (start us, length us, event | category | flops | bytes accessed | tf_op | source)
XLA Modules:
  0.0 350.3 jit_solution(4114996328176713172)
XLA Ops:
  0.6 31.2 %front.5 = (bf16[128,4096]{1,0:T(8,128)(2,1)}, bf16[256,1024]{1,0:T(8,128)(2,1)}, bf16[256,1024]{1,0:T(8,128)(2,1)}, bf16[256,1024]{1,0:T(8,128)(2,1)}, bf16[256,1024]{1,0:T(8,128)(2,1)}) custom-call(bf16[512,8192]{1,0:T(8,128)(2,1)} %rest_0_.17, f32[1,8192]{1,0:T(1,128)} %bitcast.4, s32[4,128]{1,0:T(4,128)} %bitcast.8, f32[1,64]{1,0:T(1,128)} %bitcast.16, ...), custom_call_target="tpu_custom_call" | custom-call | flops 21474836480 | bytes 71303168 | tf_op jit(solution)/shard_map/front/pallas_call | solution.py:159
  31.8 8.6 %attend_send.7 = (bf16[128,4096]{1,0:T(8,128)(2,1)}, f32[128,1024]{1,0:T(8,128)}) custom-call(s32[512]{0:T(512)} %pos_ref.7, s32[4,128]{1,0:T(4,128)} %bitcast.9, bf16[128,4096]{1,0:T(8,128)(2,1)} %get-tuple-element.50.q_hbm, bf16[4096,8192]{1,0:T(8,128)(2,1)} %w_hbm.33, bf16[256,1024]{1,0:T(8,128)(2,1)} %get-tuple-element.35.rest_0_, ...), custom_call_target="tpu_custom_call" | custom-call | flops 2147483648 | bytes 8388608 | tf_op jit(solution)/shard_map/attend_send/pallas_call | solution.py:352
  40.4 10.7 %out_send.11 = f32[128,3072]{1,0:T(8,128)} custom-call(bf16[128,4096]{1,0:T(8,128)(2,1)} %get-tuple-element.51.o_hbm, bf16[4096,8192]{1,0:T(8,128)(2,1)} %w_hbm.33), custom_call_target="tpu_custom_call" | custom-call | flops 3221225472 | bytes 26214400 | tf_op jit(solution)/shard_map/out_send/pallas_call | solution.py:463
  51.1 3.4 collective-permute-start.9
  54.5 24.5 %front.7.q_hbm = bf16[128,4096]{1,0:T(8,128)(2,1)} custom-call(bf16[512,8192]{1,0:T(8,128)(2,1)} %rest_0_.17, f32[1,8192]{1,0:T(1,128)} %bitcast.5, s32[4,128]{1,0:T(4,128)} %bitcast.10, f32[1,64]{1,0:T(1,128)} %bitcast.17, bf16[8192,4096]{1,0:T(8,128)(2,1)} %wq_hbm.7), custom_call_target="tpu_custom_call" | custom-call | flops 10737418240 | bytes 69206016 | tf_op jit(solution)/shard_map/front/pallas_call | solution.py:159
  79.0 8.6 %attend_send.6 = (bf16[128,4096]{1,0:T(8,128)(2,1)}, f32[128,1024]{1,0:T(8,128)}) custom-call(s32[512]{0:T(512)} %pos_ref.7, s32[4,128]{1,0:T(4,128)} %bitcast.11, bf16[128,4096]{1,0:T(8,128)(2,1)} %front.7.q_hbm, bf16[4096,8192]{1,0:T(8,128)(2,1)} %w_hbm.33, bf16[256,1024]{1,0:T(8,128)(2,1)} %get-tuple-element.35.rest_0_, ...), custom_call_target="tpu_custom_call" | custom-call | flops 2147483648 | bytes 8388608 | tf_op jit(solution)/shard_map/attend_send/pallas_call | solution.py:352
  87.5 10.8 %out_send.10 = f32[128,3072]{1,0:T(8,128)} custom-call(bf16[128,4096]{1,0:T(8,128)(2,1)} %get-tuple-element.48.o_hbm, bf16[4096,8192]{1,0:T(8,128)(2,1)} %w_hbm.33), custom_call_target="tpu_custom_call" | custom-call | flops 3221225472 | bytes 26214400 | tf_op jit(solution)/shard_map/out_send/pallas_call | solution.py:463
  100.3 31.2 %front.6 = (bf16[128,4096]{1,0:T(8,128)(2,1)}, bf16[256,1024]{1,0:T(8,128)(2,1)}, bf16[256,1024]{1,0:T(8,128)(2,1)}, bf16[256,1024]{1,0:T(8,128)(2,1)}, bf16[256,1024]{1,0:T(8,128)(2,1)}) custom-call(bf16[512,8192]{1,0:T(8,128)(2,1)} %rest_0_.17, f32[1,8192]{1,0:T(1,128)} %bitcast.6, s32[4,128]{1,0:T(4,128)} %bitcast.12, f32[1,64]{1,0:T(1,128)} %bitcast.18, ...), custom_call_target="tpu_custom_call" | custom-call | flops 21474836480 | bytes 71303168 | tf_op jit(solution)/shard_map/front/pallas_call | solution.py:159
  131.5 9.4 %attend_send.5 = (bf16[128,4096]{1,0:T(8,128)(2,1)}, f32[128,1024]{1,0:T(8,128)}) custom-call(s32[512]{0:T(512)} %pos_ref.7, s32[4,128]{1,0:T(4,128)} %bitcast.13, bf16[128,4096]{1,0:T(8,128)(2,1)} %get-tuple-element.45.q_hbm, bf16[4096,8192]{1,0:T(8,128)(2,1)} %w_hbm.33, bf16[256,1024]{1,0:T(8,128)(2,1)} %get-tuple-element.35.rest_0_, ...), custom_call_target="tpu_custom_call" | custom-call | flops 2147483648 | bytes 8388608 | tf_op jit(solution)/shard_map/attend_send/pallas_call | solution.py:352
  141.0 10.7 %out_send.9 = f32[128,3072]{1,0:T(8,128)} custom-call(bf16[128,4096]{1,0:T(8,128)(2,1)} %get-tuple-element.46.o_hbm, bf16[4096,8192]{1,0:T(8,128)(2,1)} %w_hbm.33), custom_call_target="tpu_custom_call" | custom-call | flops 3221225472 | bytes 26214400 | tf_op jit(solution)/shard_map/out_send/pallas_call | solution.py:463
  153.7 24.5 %front.4.q_hbm = bf16[128,4096]{1,0:T(8,128)(2,1)} custom-call(bf16[512,8192]{1,0:T(8,128)(2,1)} %rest_0_.17, f32[1,8192]{1,0:T(1,128)} %bitcast.7, s32[4,128]{1,0:T(4,128)} %bitcast.14, f32[1,64]{1,0:T(1,128)} %bitcast.19, bf16[8192,4096]{1,0:T(8,128)(2,1)} %wq_hbm.7), custom_call_target="tpu_custom_call" | custom-call | flops 10737418240 | bytes 69206016 | tf_op jit(solution)/shard_map/front/pallas_call | solution.py:159
  178.2 13.1 %attend_send.4 = (bf16[128,4096]{1,0:T(8,128)(2,1)}, f32[128,2048]{1,0:T(8,128)}) custom-call(s32[512]{0:T(512)} %pos_ref.7, s32[4,128]{1,0:T(4,128)} %bitcast.15, bf16[128,4096]{1,0:T(8,128)(2,1)} %front.4.q_hbm, bf16[4096,8192]{1,0:T(8,128)(2,1)} %w_hbm.33, bf16[256,1024]{1,0:T(8,128)(2,1)} %get-tuple-element.35.rest_0_, ...), custom_call_target="tpu_custom_call" | custom-call | flops 3221225472 | bytes 16777216 | tf_op jit(solution)/shard_map/attend_send/pallas_call | solution.py:352
  191.3 5.2 %out_send.8 = f32[128,1024]{1,0:T(8,128)} custom-call(bf16[128,4096]{1,0:T(8,128)(2,1)} %get-tuple-element.43.o_hbm, bf16[4096,8192]{1,0:T(8,128)(2,1)} %w_hbm.33), custom_call_target="tpu_custom_call" | custom-call | flops 1073741824 | bytes 9437184 | tf_op jit(solution)/shard_map/out_send/pallas_call | solution.py:463
  198.6 14.4 %out_own.7 = (bf16[512,8192]{1,0:T(8,128)(2,1)}, bf16[128,4096]{1,0:T(8,128)(2,1)}) custom-call(bf16[128,4096]{1,0:T(8,128)(2,1)} %get-tuple-element.51.o_hbm, bf16[4096,8192]{1,0:T(8,128)(2,1)} %w_hbm.33, bf16[512,8192]{1,0:T(8,128)(2,1)} %rest_0_.17, f32[128,1024]{1,0:T(8,128)} %collective-permute-done.8.rest_1_, f32[128,3072]{1,0:T(8,128)} %collective-permute-done.9.rest_2_), custom_call_target="tpu_custom_call" | custom-call | flops 4294967296 | bytes 34603008 | tf_op jit(solution)/shard_map/out_own/pallas_call | solution.py:463
  215.0 14.4 %out_own.8 = (bf16[512,8192]{1,0:T(8,128)(2,1)}, bf16[128,4096]{1,0:T(8,128)(2,1)}) custom-call(bf16[128,4096]{1,0:T(8,128)(2,1)} %get-tuple-element.48.o_hbm, bf16[4096,8192]{1,0:T(8,128)(2,1)} %w_hbm.33, bf16[512,8192]{1,0:T(8,128)(2,1)} %rest_0_.17, f32[128,1024]{1,0:T(8,128)} %collective-permute-done.6.rest_1_, ...), custom_call_target="tpu_custom_call", output_to_operand_aliasing={{0}: (5, {})} | custom-call | flops 4294967296 | bytes 34603008 | tf_op jit(solution)/shard_map/out_own/pallas_call | solution.py:463
  229.4 14.4 %out_own.9 = (bf16[512,8192]{1,0:T(8,128)(2,1)}, bf16[128,4096]{1,0:T(8,128)(2,1)}) custom-call(bf16[128,4096]{1,0:T(8,128)(2,1)} %get-tuple-element.46.o_hbm, bf16[4096,8192]{1,0:T(8,128)(2,1)} %w_hbm.33, bf16[512,8192]{1,0:T(8,128)(2,1)} %rest_0_.17, f32[128,1024]{1,0:T(8,128)} %collective-permute-done.4.rest_1_, ...), custom_call_target="tpu_custom_call", output_to_operand_aliasing={{0}: (5, {})} | custom-call | flops 4294967296 | bytes 34603008 | tf_op jit(solution)/shard_map/out_own/pallas_call | solution.py:463
  245.8 4.0 %out_send.7 = f32[128,512]{1,0:T(8,128)} custom-call(bf16[128,4096]{1,0:T(8,128)(2,1)} %get-tuple-element.43.o_hbm, bf16[4096,8192]{1,0:T(8,128)(2,1)} %w_hbm.33), custom_call_target="tpu_custom_call" | custom-call | flops 536870912 | bytes 5242880 | tf_op jit(solution)/shard_map/out_send/pallas_call | solution.py:463
  251.8 4.0 %out_send.6 = f32[128,512]{1,0:T(8,128)} custom-call(bf16[128,4096]{1,0:T(8,128)(2,1)} %get-tuple-element.43.o_hbm, bf16[4096,8192]{1,0:T(8,128)(2,1)} %w_hbm.33), custom_call_target="tpu_custom_call" | custom-call | flops 536870912 | bytes 5242880 | tf_op jit(solution)/shard_map/out_send/pallas_call | solution.py:463
  255.7 8.5 %out_own.10 = (bf16[512,8192]{1,0:T(8,128)(2,1)}, bf16[128,2048]{1,0:T(8,128)(2,1)}) custom-call(bf16[128,4096]{1,0:T(8,128)(2,1)} %get-tuple-element.43.o_hbm, bf16[4096,8192]{1,0:T(8,128)(2,1)} %w_hbm.33, bf16[512,8192]{1,0:T(8,128)(2,1)} %rest_0_.17, f32[128,2048]{1,0:T(8,128)} %collective-permute-done.3.rest_1_, ...), custom_call_target="tpu_custom_call", output_to_operand_aliasing={{0}: (4, {})} | custom-call | flops 2147483648 | bytes 17825792 | tf_op jit(solution)/shard_map/out_own/pallas_call | solution.py:463
  264.3 52.0 %collective-permute-done.1.rest_1_ = f32[128,512]{1,0:T(8,128)} collective-permute-done((f32[128,512]{1,0:T(8,128)}, f32[128,512]{1,0:T(8,128)}, u32[]{:S(2)}, u32[]{:S(2)}) %collective-permute-start.1) | collective-permute-done | bytes 262176 | tf_op jit(solution)/shard_map/ppermute | solution.py:519
  320.2 5.5 %out_own.11 = (bf16[512,8192]{1,0:T(8,128)(2,1)}, bf16[128,1024]{1,0:T(8,128)(2,1)}) custom-call(bf16[128,4096]{1,0:T(8,128)(2,1)} %get-tuple-element.43.o_hbm, bf16[4096,8192]{1,0:T(8,128)(2,1)} %w_hbm.33, bf16[512,8192]{1,0:T(8,128)(2,1)} %rest_0_.17, f32[128,1024]{1,0:T(8,128)} %collective-permute-done.2.rest_1_, ...), custom_call_target="tpu_custom_call", output_to_operand_aliasing={{0}: (4, {})} | custom-call | flops 1073741824 | bytes 9437184 | tf_op jit(solution)/shard_map/out_own/pallas_call | solution.py:463
  325.7 4.1 %out_own.12 = (bf16[512,8192]{1,0:T(8,128)(2,1)}, bf16[128,512]{1,0:T(8,128)(2,1)}) custom-call(bf16[128,4096]{1,0:T(8,128)(2,1)} %get-tuple-element.43.o_hbm, bf16[4096,8192]{1,0:T(8,128)(2,1)} %w_hbm.33, bf16[512,8192]{1,0:T(8,128)(2,1)} %rest_0_.17, f32[128,512]{1,0:T(8,128)} %collective-permute-done.1.rest_1_, ...), custom_call_target="tpu_custom_call", output_to_operand_aliasing={{0}: (4, {})} | custom-call | flops 536870912 | bytes 5242880 | tf_op jit(solution)/shard_map/out_own/pallas_call | solution.py:463
  330.1 4.1 %out_own.13 = (bf16[512,8192]{1,0:T(8,128)(2,1)}, bf16[128,512]{1,0:T(8,128)(2,1)}) custom-call(bf16[128,4096]{1,0:T(8,128)(2,1)} %get-tuple-element.43.o_hbm, bf16[4096,8192]{1,0:T(8,128)(2,1)} %w_hbm.33, bf16[512,8192]{1,0:T(8,128)(2,1)} %rest_0_.17, f32[128,512]{1,0:T(8,128)} %collective-permute-done.rest_1_, ...), custom_call_target="tpu_custom_call", output_to_operand_aliasing={{0}: (4, {})} | custom-call | flops 536870912 | bytes 5242880 | tf_op jit(solution)/shard_map/out_own/pallas_call | solution.py:463
  343.4 2.0 place.9.y_in
  (43 shorter events, 30.6 us)
Async XLA Ops:
  51.1 145.5 %collective-permute-start.9 = (f32[128,3072]{1,0:T(8,128)}, f32[128,3072]{1,0:T(8,128)}, u32[]{:S(2)}, u32[]{:S(2)}) collective-permute-start(f32[128,3072]{1,0:T(8,128)} %out_send.11), channel_id=1, source_target_pairs={{0,4},{4,0},{1,5},{5,1},{2,6},{6,2},{3,7},{7,3}} | collective-permute-start | bytes 4718600 | tf_op jit(solution)/shard_map/ppermute | solution.py:519
  54.5 142.1 %collective-permute-start.8 = (f32[128,1024]{1,0:T(8,128)}, f32[128,1024]{1,0:T(8,128)}, u32[]{:S(2)}, u32[]{:S(2)}) collective-permute-start(f32[128,1024]{1,0:T(8,128)} %get-tuple-element.52), channel_id=1, source_target_pairs={{0,4},{4,0},{1,5},{5,1},{2,6},{6,2},{3,7},{7,3}} | collective-permute-start | bytes 1572872 | tf_op jit(solution)/shard_map/ppermute | solution.py:519
  98.3 114.7 %collective-permute-start.7 = (f32[128,3072]{1,0:T(8,128)}, f32[128,3072]{1,0:T(8,128)}, u32[]{:S(2)}, u32[]{:S(2)}) collective-permute-start(f32[128,3072]{1,0:T(8,128)} %out_send.10), channel_id=1, source_target_pairs={{0,4},{4,0},{1,5},{5,1},{2,6},{6,2},{3,7},{7,3}} | collective-permute-start | bytes 4718600 | tf_op jit(solution)/shard_map/ppermute | solution.py:519
  100.3 112.7 %collective-permute-start.6 = (f32[128,1024]{1,0:T(8,128)}, f32[128,1024]{1,0:T(8,128)}, u32[]{:S(2)}, u32[]{:S(2)}) collective-permute-start(f32[128,1024]{1,0:T(8,128)} %get-tuple-element.49), channel_id=1, source_target_pairs={{0,4},{4,0},{1,5},{5,1},{2,6},{6,2},{3,7},{7,3}} | collective-permute-start | bytes 1572872 | tf_op jit(solution)/shard_map/ppermute | solution.py:519
  151.7 77.7 %collective-permute-start.5 = (f32[128,3072]{1,0:T(8,128)}, f32[128,3072]{1,0:T(8,128)}, u32[]{:S(2)}, u32[]{:S(2)}) collective-permute-start(f32[128,3072]{1,0:T(8,128)} %out_send.9), channel_id=1, source_target_pairs={{0,4},{4,0},{1,5},{5,1},{2,6},{6,2},{3,7},{7,3}} | collective-permute-start | bytes 4718600 | tf_op jit(solution)/shard_map/ppermute | solution.py:519
  196.5 32.8 %collective-permute-start.4 = (f32[128,1024]{1,0:T(8,128)}, f32[128,1024]{1,0:T(8,128)}, u32[]{:S(2)}, u32[]{:S(2)}) collective-permute-start(f32[128,1024]{1,0:T(8,128)} %get-tuple-element.47), channel_id=1, source_target_pairs={{0,4},{4,0},{1,5},{5,1},{2,6},{6,2},{3,7},{7,3}} | collective-permute-start | bytes 1572872 | tf_op jit(solution)/shard_map/ppermute | solution.py:519
  196.6 53.2 %collective-permute-start.3 = (f32[128,2048]{1,0:T(8,128)}, f32[128,2048]{1,0:T(8,128)}, u32[]{:S(2)}, u32[]{:S(2)}) collective-permute-start(f32[128,2048]{1,0:T(8,128)} %get-tuple-element.44), channel_id=1, source_target_pairs={{0,4},{4,0},{1,5},{5,1},{2,6},{6,2},{3,7},{7,3}} | collective-permute-start | bytes 3145736 | tf_op jit(solution)/shard_map/ppermute | solution.py:519
  213.0 103.6 %collective-permute-start.2 = (f32[128,1024]{1,0:T(8,128)}, f32[128,1024]{1,0:T(8,128)}, u32[]{:S(2)}, u32[]{:S(2)}) collective-permute-start(f32[128,1024]{1,0:T(8,128)} %out_send.8), channel_id=1, source_target_pairs={{0,4},{4,0},{1,5},{5,1},{2,6},{6,2},{3,7},{7,3}} | collective-permute-start | bytes 1572872 | tf_op jit(solution)/shard_map/ppermute | solution.py:519
  213.0 121.1 %collective-permute-start.16 = (bf16[128,4096]{1,0:T(8,128)(2,1)}, bf16[128,4096]{1,0:T(8,128)(2,1)}, u32[]{:S(2)}, u32[]{:S(2)}) collective-permute-start(bf16[128,4096]{1,0:T(8,128)(2,1)} %get-tuple-element.65), channel_id=1, source_target_pairs={{0,4},{4,0},{1,5},{5,1},{2,6},{6,2},{3,7},{7,3}} | collective-permute-start | bytes 3145736 | tf_op jit(solution)/shard_map/ppermute | solution.py:519
  229.4 106.5 %collective-permute-start.15 = (bf16[128,4096]{1,0:T(8,128)(2,1)}, bf16[128,4096]{1,0:T(8,128)(2,1)}, u32[]{:S(2)}, u32[]{:S(2)}) collective-permute-start(bf16[128,4096]{1,0:T(8,128)(2,1)} %get-tuple-element.64), channel_id=1, source_target_pairs={{0,4},{4,0},{1,5},{5,1},{2,6},{6,2},{3,7},{7,3}} | collective-permute-start | bytes 3145736 | tf_op jit(solution)/shard_map/ppermute | solution.py:519
  243.8 99.6 %collective-permute-start.14 = (bf16[128,4096]{1,0:T(8,128)(2,1)}, bf16[128,4096]{1,0:T(8,128)(2,1)}, u32[]{:S(2)}, u32[]{:S(2)}) collective-permute-start(bf16[128,4096]{1,0:T(8,128)(2,1)} %get-tuple-element.63), channel_id=1, source_target_pairs={{0,4},{4,0},{1,5},{5,1},{2,6},{6,2},{3,7},{7,3}} | collective-permute-start | bytes 3145736 | tf_op jit(solution)/shard_map/ppermute | solution.py:519
  249.8 66.5 %collective-permute-start.1 = (f32[128,512]{1,0:T(8,128)}, f32[128,512]{1,0:T(8,128)}, u32[]{:S(2)}, u32[]{:S(2)}) collective-permute-start(f32[128,512]{1,0:T(8,128)} %out_send.7), channel_id=1, source_target_pairs={{0,4},{4,0},{1,5},{5,1},{2,6},{6,2},{3,7},{7,3}} | collective-permute-start | bytes 786440 | tf_op jit(solution)/shard_map/ppermute | solution.py:519
  316.3 13.5 %collective-permute-start = (f32[128,512]{1,0:T(8,128)}, f32[128,512]{1,0:T(8,128)}, u32[]{:S(2)}, u32[]{:S(2)}) collective-permute-start(f32[128,512]{1,0:T(8,128)} %out_send.6), channel_id=1, source_target_pairs={{0,4},{4,0},{1,5},{5,1},{2,6},{6,2},{3,7},{7,3}} | collective-permute-start | bytes 786440 | tf_op jit(solution)/shard_map/ppermute | solution.py:519
  316.6 28.9 %collective-permute-start.13 = (bf16[128,2048]{1,0:T(8,128)(2,1)}, bf16[128,2048]{1,0:T(8,128)(2,1)}, u32[]{:S(2)}, u32[]{:S(2)}) collective-permute-start(bf16[128,2048]{1,0:T(8,128)(2,1)} %get-tuple-element.62), channel_id=1, source_target_pairs={{0,4},{4,0},{1,5},{5,1},{2,6},{6,2},{3,7},{7,3}} | collective-permute-start | bytes 1572872 | tf_op jit(solution)/shard_map/ppermute | solution.py:519
  329.8 17.6 %collective-permute-start.12 = (bf16[128,1024]{1,0:T(8,128)(2,1)}, bf16[128,1024]{1,0:T(8,128)(2,1)}, u32[]{:S(2)}, u32[]{:S(2)}) collective-permute-start(bf16[128,1024]{1,0:T(8,128)(2,1)} %get-tuple-element.61), channel_id=1, source_target_pairs={{0,4},{4,0},{1,5},{5,1},{2,6},{6,2},{3,7},{7,3}} | collective-permute-start | bytes 786440 | tf_op jit(solution)/shard_map/ppermute | solution.py:519
  334.2 14.8 %collective-permute-start.11 = (bf16[128,512]{1,0:T(8,128)(2,1)}, bf16[128,512]{1,0:T(8,128)(2,1)S(1)}, u32[]{:S(2)}, u32[]{:S(2)}) collective-permute-start(bf16[128,512]{1,0:T(8,128)(2,1)} %get-tuple-element.60), channel_id=1, source_target_pairs={{0,4},{4,0},{1,5},{5,1},{2,6},{6,2},{3,7},{7,3}} | collective-permute-start | bytes 393224 | tf_op jit(solution)/shard_map/ppermute | solution.py:519
  335.9 13.8 %collective-permute-start.10 = (bf16[128,512]{1,0:T(8,128)(2,1)}, bf16[128,512]{1,0:T(8,128)(2,1)S(1)}, u32[]{:S(2)}, u32[]{:S(2)}) collective-permute-start(bf16[128,512]{1,0:T(8,128)(2,1)} %get-tuple-element.59), channel_id=1, source_target_pairs={{0,4},{4,0},{1,5},{5,1},{2,6},{6,2},{3,7},{7,3}} | collective-permute-start | bytes 393224 | tf_op jit(solution)/shard_map/ppermute | solution.py:519
